TPU v7x, 8 devices: a whole 2x2x1 slice. The times are simulated.
8 devices in a mesh: rep: 2 (over y, z), dp: 4 (over x, core).
Axes of the slice: x: 2, y: 2, z: 1, core: 2. Of those that a mesh axis runs over, the one named last changes fastest.
Arguments:
- x: bfloat16 [8, 2048, 1280], P(('rep', 'dp')), parts along dimension 0
- dy: bfloat16 [8, 2048, 1280], P(('rep', 'dp')), parts along dimension 0
- w_gate: bfloat16 [2, 1280, 4480], replicated
- w_up: bfloat16 [2, 1280, 4480], replicated
- w_down: bfloat16 [2, 4480, 1280], replicated
- m_w_gate: float32 [2, 1280, 4480], P(None, 'dp')
- m_w_up: float32 [2, 1280, 4480], P(None, 'dp')
- m_w_down: float32 [2, 4480, 1280], P(None, 'dp')
- v_w_gate: float32 [2, 1280, 4480], P(None, 'dp')
- v_w_up: float32 [2, 1280, 4480], P(None, 'dp')
- v_w_down: float32 [2, 4480, 1280], P(None, 'dp')
Outputs:
- output 1: bfloat16 [4, 1280, 4480], P('rep'), parts along dimension 0
- output 2: bfloat16 [4, 1280, 4480], P('rep'), parts along dimension 0
- output 3: bfloat16 [4, 4480, 1280], P('rep'), parts along dimension 0
- output 4: float32 [4, 1280, 4480], P('rep', 'dp'), parts along dimension 0
- output 5: float32 [4, 1280, 4480], P('rep', 'dp'), parts along dimension 0
- output 6: float32 [4, 4480, 1280], P('rep', 'dp'), parts along dimension 0
- output 7: float32 [4, 1280, 4480], P('rep', 'dp'), parts along dimension 0
- output 8: float32 [4, 1280, 4480], P('rep', 'dp'), parts along dimension 0
- output 9: float32 [4, 4480, 1280], P('rep', 'dp'), parts along dimension 0
There are 2 independent parts. A program takes and returns all parts, laid end to end along the dimension named above; an argument that names none is the same for every part.
All inputs are finite; a program needn't handle non-finite values.
Results may differ from a plain program's by a relative error of at most 0.022.
Values are sent between devices in bfloat16 or wider.
A program may use at most 2 GiB of HBM per device.

v0:
```python
import jax
import jax.numpy as jnp
from jax import lax

NAMES = ("w_gate", "w_up", "w_down")


def matmul(a, w):
    return jnp.dot(a, w, preferred_element_type=jnp.float32).astype(jnp.bfloat16)


def normed(h):
    wide = h.astype(jnp.float32)
    scale = lax.rsqrt(jnp.mean(wide**2, -1, keepdims=True) + 1e-6)
    return (wide * scale).astype(jnp.bfloat16)


def layer(h, w):
    a = normed(h)
    gate = jnp.dot(a, w["w_gate"], preferred_element_type=jnp.float32)
    up = jnp.dot(a, w["w_up"], preferred_element_type=jnp.float32)
    return h + matmul((jax.nn.silu(gate) * up).astype(jnp.bfloat16), w["w_down"])


def adamw(w, m, v, g):
    m = 0.9 * m + 0.1 * g
    v = 0.95 * v + 0.05 * g * g
    step = m * lax.rsqrt(v + 1e-8) + 0.1 * w
    return (w - 0.02 * step).astype(jnp.bfloat16), m, v


def clipped(gradients, sum_of_squares, count):
    factor = jnp.minimum(1.0, 0.5 * lax.rsqrt(sum_of_squares / count + 1e-30))
    return [g * factor for g in gradients]


def stack(weights, h):
    for number in range(weights["w_gate"].shape[0]):
        h = layer(h, {name: w[number] for name, w in weights.items()})
    return h


def solution(mesh):
    groups = mesh.shape["rep"]

    def step(x, dy, *arrays):
        weights, m, v = (arrays[i : i + 3] for i in (0, 3, 6))
        x, dy = (t.reshape(groups, -1, *t.shape[1:]) for t in (x, dy))

        def of_a_group(x, dy):
            _, back = jax.vjp(lambda w: stack(w, x), dict(zip(NAMES, weights, strict=True)))
            by_weights = back(dy)[0]
            gradients = [by_weights[name].astype(jnp.float32) for name in NAMES]
            gradients = clipped(gradients, sum(jnp.sum(g * g) for g in gradients), sum(g.size for g in gradients))
            new = [adamw(w.astype(jnp.float32), m, v, g) for w, m, v, g in zip(weights, m, v, gradients, strict=True)]
            return tuple(one[which] for which in range(3) for one in new)

        return tuple(t.reshape(-1, *t.shape[2:]) for t in jax.vmap(of_a_group)(x, dy))

    return step
```

profile of v0, /device:TPU:0, one launch (start us, length us, event | category | flops | bytes accessed | tf_op | source)
XLA Modules:
  0.0 1881.8 jit_solution(10403524154998212299)
XLA Ops:
  18.8 32.1 %fusion.83 = f32[2048,4480]{1,0:T(8,128)} fusion(bf16[2,1280,4480]{2,1,0:T(8,128)(2,1)} %param, bf16[1,2048,1280]{2,1,0:T(8,128)(2,1)} %param.2, f32[2048]{0:T(1024)S(1)} %add_rsqrt_fusion), kind=kOutput, calls=%fused_computation.112 | convolution fusion | flops 23495966720 | bytes 53420032 | tf_op jit(solution)/vmap(jvp())/dot_general | solution.py:20
  50.9 30.0 %fusion.81 = f32[2048,4480]{1,0:T(8,128)} fusion(bf16[2,1280,4480]{2,1,0:T(8,128)(2,1)} %param.3, bf16[1,2048,1280]{2,1,0:T(8,128)(2,1)S(1)} %bitcast.356, f32[2048]{0:T(1024)S(1)} %add_rsqrt_fusion), kind=kOutput, calls=%fused_computation.110 | convolution fusion | flops 23495966720 | bytes 53420032 | tf_op jit(solution)/vmap(jvp())/dot_general | solution.py:21
  80.9 30.6 %fusion.35 = bf16[2048,4480]{1,0:T(8,128)(2,1)} fusion(f32[2048,4480]{1,0:T(8,128)} %fusion.81, f32[2048,4480]{1,0:T(8,128)} %fusion.83), kind=kLoop, calls=%fused_computation.43 | loop fusion | flops 55050240 | bytes 91750400
  111.5 33.4 %fusion.92 = (f32[2048]{0:T(1024)S(1)}, bf16[1,1,2048,1280]{2,3,1,0:T(8,128)(2,1)}) fusion(bf16[2048,4480]{1,0:T(8,128)(2,1)} %fusion.35, bf16[2,4480,1280]{2,1,0:T(8,128)(2,1)} %param.4, bf16[1,2048,1280]{1,2,0:T(8,128)(2,1)} %copy), kind=kOutput, calls=%fused_computation.121 | convolution fusion | flops 23501207552 | bytes 40312832 | tf_op jit(solution)/vmap(jvp())/dot_general | solution.py:9
  145.5 32.1 %fusion.70 = f32[2048,4480]{1,0:T(8,128)} fusion(bf16[2,1280,4480]{2,1,0:T(8,128)(2,1)} %param, bf16[1,1,2048,1280]{2,3,1,0:T(8,128)(2,1)} %get-tuple-element.10, f32[2048]{0:T(1024)S(1)} %bitcast.362), kind=kOutput, calls=%fused_computation.99 | convolution fusion | flops 23495966720 | bytes 53420032 | tf_op jit(solution)/vmap(jvp())/dot_general | solution.py:20
  177.6 30.7 %fusion.74 = f32[2048,4480]{1,0:T(8,128)} fusion(bf16[2,1280,4480]{2,1,0:T(8,128)(2,1)} %param.3, bf16[1,1,2048,1280]{2,3,1,0:T(8,128)(2,1)S(1)} %copy-done.5, f32[2048]{0:T(1024)S(1)} %bitcast.363), kind=kOutput, calls=%fused_computation.103 | convolution fusion | flops 23495966720 | bytes 53420032 | tf_op jit(solution)/vmap(jvp())/dot_general | solution.py:21
  208.3 30.5 %convolution_convert_fusion.1 = bf16[2048,4480]{1,0:T(8,128)(2,1)} fusion(bf16[2,4480,1280]{2,1,0:T(8,128)(2,1)} %param.4, bf16[1,2048,1280]{2,1,0:T(8,128)(2,1)S(1)} %bitcast.358), kind=kOutput, calls=%fused_computation.42 | convolution fusion | flops 23497277440 | bytes 35061760 | tf_op jit(solution)/vmap(transpose(jvp()))/dot_general | solution.py:9
  246.7 35.9 %fusion.6 = bf16[2048,4480]{1,0:T(8,128)(2,1)} fusion(f32[2048,4480]{1,0:T(8,128)} %fusion.70, f32[2048,4480]{1,0:T(8,128)} %fusion.74, bf16[2048,4480]{1,0:T(8,128)(2,1)} %convolution_convert_fusion.1), kind=kLoop, calls=%fused_computation.11 | loop fusion | flops 110100480 | bytes 110100480
  282.6 32.0 %fusion.106 = bf16[2048,1280]{0,1:T(8,128)(2,1)} fusion(bf16[2048,4480]{1,0:T(8,128)(2,1)} %fusion.6, bf16[2,1280,4480]{2,1,0:T(8,128)(2,1)} %param), kind=kOutput, calls=%fused_computation.132 | convolution fusion | flops 23488102400 | bytes 35061760 | tf_op jit(solution)/vmap(transpose(jvp()))/dot_general | solution.py:20
  314.6 37.1 %fusion.94 = (f32[2048]{0:T(1024)S(1)}, bf16[1,1,2048,1280]{2,3,1,0:T(8,128)(2,1)}) fusion(bf16[1,1,2048,1280]{2,3,1,0:T(8,128)(2,1)} %get-tuple-element.10, bf16[2048,1280]{0,1:T(8,128)(2,1)} %fusion.106, bf16[2,1280,4480]{2,1,0:T(8,128)(2,1)} %param.3, bf16[2048,4480]{1,0:T(8,128)(2,1)} %convolution_convert_fusion.1, f32[2048,4480]{1,0:T(8,128)} %fusion.70), kind=kOutput, calls=%fused_computation.123 | convolution fusion | flops 23558879232 | bytes 82255872 | tf_op jit(solution)/vmap(transpose(jvp()))/dot_general | solution.py:21
  351.8 12.4 fusion.137
  364.2 30.5 %convolution_bitcast_fusion = f32[1,4480,1280]{2,1,0:T(8,128)} fusion(bf16[2048,4480]{1,0:T(8,128)(2,1)} %fusion.35, bf16[2048,1280]{0,1:T(8,128)(2,1)} %fusion.137), kind=kOutput, calls=%fused_computation.36 | convolution fusion | flops 23488102400 | bytes 46530560 | tf_op jit(solution)/vmap(transpose(jvp()))/dot_general | solution.py:9
  394.8 49.4 %convolution_bitcast_fusion.1 = f32[1,4480,1280]{2,1,0:T(8,128)} fusion(f32[2048,4480]{1,0:T(8,128)} %fusion.74, f32[2048,4480]{1,0:T(8,128)} %fusion.70, bf16[1,2048,1280]{2,1,0:T(8,128)(2,1)} %param.5), kind=kOutput, calls=%fused_computation.37 | convolution fusion | flops 23543152640 | bytes 101580800 | tf_op jit(solution)/vmap(transpose(jvp()))/dot_general | solution.py:9
  444.3 31.7 %convolution_convert_fusion = bf16[2048,4480]{1,0:T(8,128)(2,1)} fusion(bf16[2048,1280]{0,1:T(8,128)(2,1)} %fusion.137, bf16[2,4480,1280]{2,1,0:T(8,128)(2,1)} %param.4), kind=kOutput, calls=%fused_computation.41 | convolution fusion | flops 23497277440 | bytes 35061760 | tf_op jit(solution)/vmap(transpose(jvp()))/dot_general | solution.py:9
  476.0 38.9 %fusion.32 = f32[1,1280,4480]{2,1,0:T(8,128)} fusion(bf16[2048,4480]{1,0:T(8,128)(2,1)} %convolution_convert_fusion, f32[2048,4480]{1,0:T(8,128)} %fusion.83, bf16[1,2048,1280]{1,2,0:T(8,128)(2,1)} %copy, f32[2048]{0:T(1024)S(1)} %copy-done.12), kind=kOutput, calls=%fused_computation.40 | convolution fusion | flops 23551016960 | bytes 83238912 | tf_op jit(solution)/vmap(transpose(jvp()))/dot_general | solution.py:21
  515.5 38.8 %fusion.29 = f32[1,1280,4480]{2,1,0:T(8,128)} fusion(bf16[2048,4480]{1,0:T(8,128)(2,1)} %convolution_convert_fusion.1, f32[2048,4480]{1,0:T(8,128)} %fusion.70, bf16[1,1,2048,1280]{2,3,1,0:T(8,128)(2,1)} %get-tuple-element.10, f32[2048]{0:T(1024)S(1)} %bitcast.365), kind=kOutput, calls=%fused_computation.39 | convolution fusion | flops 23551016960 | bytes 83238912 | tf_op jit(solution)/vmap(transpose(jvp()))/dot_general | solution.py:21
  554.4 54.9 %fusion.26 = f32[1,1280,4480]{2,1,0:T(8,128)} fusion(f32[2048,4480]{1,0:T(8,128)} %fusion.83, f32[2048,4480]{1,0:T(8,128)} %fusion.81, bf16[2048,4480]{1,0:T(8,128)(2,1)} %convolution_convert_fusion, bf16[1,2048,1280]{1,2,0:T(8,128)(2,1)} %copy, f32[2048]{0:T(1024)S(1)} %copy-done.12), kind=kOutput, calls=%fused_computation.35 | convolution fusion | flops 23596892160 | bytes 119939072 | tf_op jit(solution)/vmap(transpose(jvp()))/dot_general | solution.py:20
  609.4 31.1 %convolution_bitcast_fusion.2 = f32[1,1280,4480]{2,1,0:T(8,128)} fusion(bf16[2048,4480]{1,0:T(8,128)(2,1)} %fusion.6, bf16[1,1,2048,1280]{2,3,1,0:T(8,128)(2,1)} %get-tuple-element.10, f32[2048]{0:T(1024)S(1)} %bitcast.366), kind=kOutput, calls=%fused_computation.38 | convolution fusion | flops 23495966720 | bytes 46538752 | tf_op jit(solution)/vmap(transpose(jvp()))/dot_general | solution.py:20
  645.5 73.3 %reduce-scatter.27.cloned.1.call-done = f32[1,1120,1280]{2,1,0:T(8,128)} async-done(((f32[1,4480,1280]{2,1,0:T(8,128)}), f32[1,1120,1280]{2,1,0:T(8,128)}) %reduce-scatter.27.cloned.1.call-update) | async-done | bytes 5734416
  726.9 154.4 %reduce-scatter.25.cloned.1.call-done = f32[1,320,4480]{2,1,0:T(8,128)} async-done(((f32[1,1280,4480]{2,1,0:T(8,128)}), f32[1,320,4480]{2,1,0:T(8,128)}) %reduce-scatter.25.cloned.1.call-update) | async-done | bytes 5734416
  884.2 158.8 %reduce-scatter.23.cloned.1.call-done = f32[1,320,4480]{2,1,0:T(8,128)} async-done(((f32[1,1280,4480]{2,1,0:T(8,128)}), f32[1,320,4480]{2,1,0:T(8,128)}) %reduce-scatter.23.cloned.1.call-update) | async-done | bytes 5734416
  1051.1 154.2 %reduce-scatter.21.cloned.1.call-done = f32[1,320,4480]{2,1,0:T(8,128)} async-done(((f32[1,1280,4480]{2,1,0:T(8,128)}), f32[1,320,4480]{2,1,0:T(8,128)}) %reduce-scatter.21.cloned.1.call-update) | async-done | bytes 5734416
  1208.2 159.4 %reduce-scatter.19.cloned.1.call-done = f32[1,320,4480]{2,1,0:T(8,128)} async-done(((f32[1,1280,4480]{2,1,0:T(8,128)}), f32[1,320,4480]{2,1,0:T(8,128)}) %reduce-scatter.19.cloned.1.call-update) | async-done | bytes 5734416
  1385.3 23.7 %fusion.131 = (f32[2,1120,1280]{2,1,0:T(8,128)}, bf16[1,2,1120,1280]{3,2,1,0:T(8,128)(2,1)}, f32[2,1120,1280]{2,1,0:T(8,128)}) fusion(f32[]{:T(128)} %bitcast.51, f32[2,1120,1280]{2,1,0:T(8,128)} %param.10, bf16[1,1,1120,1280]{3,2,1,0:T(8,128)(2,1)} %copy-done.3, bf16[1,1,1120,1280]{3,2,1,0:T(8,128)(2,1)} %copy-done.4, f32[2,1120,1280]{2,1,0:T(8,128)} %param.9, ...), kind=kLoop, calls=%fused_computation.141 | loop fusion | flops 57344000 | bytes 63078408 | tf_op jit(solution)/reshape | solution.py:58
  1409.3 27.2 %fusion.132 = (f32[2,320,4480]{2,1,0:T(8,128)}, bf16[1,2,320,4480]{3,2,1,0:T(8,128)(2,1)}, f32[2,320,4480]{2,1,0:T(8,128)}) fusion(f32[]{:T(128)} %bitcast.51, f32[2,320,4480]{2,1,0:T(8,128)} %param.8, bf16[1,1,320,4480]{3,2,1,0:T(8,128)(2,1)} %copy-done, bf16[1,1,320,4480]{3,2,1,0:T(8,128)(2,1)} %copy-done.2, f32[2,320,4480]{2,1,0:T(8,128)} %param.7, ...), kind=kLoop, calls=%fused_computation.142 | loop fusion | flops 57344000 | bytes 63078408 | tf_op jit(solution)/reshape | solution.py:58
  1436.6 20.0 %fusion.133 = (f32[2,320,4480]{2,1,0:T(8,128)}, bf16[1,2,320,4480]{3,2,1,0:T(8,128)(2,1)}, f32[2,320,4480]{2,1,0:T(8,128)}) fusion(f32[]{:T(128)} %bitcast.51, f32[2,320,4480]{2,1,0:T(8,128)} %param.6, bf16[1,1,320,4480]{3,2,1,0:T(8,128)(2,1)S(1)} %convert_bitcast_fusion.7, bf16[1,1,320,4480]{3,2,1,0:T(8,128)(2,1)} %copy-done.1, f32[2,320,4480]{2,1,0:T(8,128)} %param.1, ...), kind=kLoop, calls=%fused_computation.143 | loop fusion | flops 57344000 | bytes 63078408 | tf_op jit(solution)/reshape | solution.py:58
  1456.6 91.5 %all-gather.14.cloned.1.call-done = bf16[1,2,4480,1280]{3,2,1,0:T(8,128)(2,1)} async-done(((bf16[1,2,1120,1280]{3,2,1,0:T(8,128)(2,1)}), bf16[1,2,4480,1280]{3,2,1,0:T(8,128)(2,1)}) %all-gather.14.cloned.1.call-update) | async-done | bytes 22937616 | tf_op jit(solution)/reshape | solution.py:58
  1548.1 140.5 %all-gather.12.cloned.1.call-done = bf16[1,2,1280,4480]{3,2,1,0:T(8,128)(2,1)} async-done(((bf16[1,2,320,4480]{3,2,1,0:T(8,128)(2,1)}), bf16[1,2,1280,4480]{3,2,1,0:T(8,128)(2,1)}) %all-gather.12.cloned.1.call-update) | async-done | bytes 22937616 | tf_op jit(solution)/reshape | solution.py:58
  1688.6 140.5 %all-gather.10.cloned.1.call-done = bf16[1,2,1280,4480]{3,2,1,0:T(8,128)(2,1)} async-done(((bf16[1,2,320,4480]{3,2,1,0:T(8,128)(2,1)}), bf16[1,2,1280,4480]{3,2,1,0:T(8,128)(2,1)}) %all-gather.10.cloned.1.call-update) | async-done | bytes 22937616 | tf_op jit(solution)/reshape | solution.py:58
  1829.0 19.0 %copy.5 = bf16[2,1280,4480]{2,1,0:T(8,128)(2,1)} copy(bf16[2,1280,4480]{2,1,0:T(8,128)(2,1)} %bitcast.354) | data formatting | bytes 45875200
  1848.0 18.7 copy.6
  1866.8 8.2 copy.7
  (88 shorter events, 62.6 us)
Async XLA Ops:
  7.2 635.3 %reduce-scatter.29.cloned.1.call-start = ((), (), s32[]{:S(2)}) async-start(), calls=%async_computation.14 | async-start | bytes 28672000
  10.8 40.1 %slice-start.6 = ((s8[5242880]{0:T(1024)(128)(4,1)}), s8[1048576]{0:T(1024)(128)(4,1)S(1)}, s32[]{:S(2)}) async-start(s8[5242880]{0:T(1024)(128)(4,1)} %bitcast.355), calls=%async_computation.21 | async-start | bytes 2097152
  18.8 32.1 %copy-start.11 = (f32[2048]{0:T(1024)}, f32[2048]{0:T(1024)S(1)}, u32[]{:S(2)}) copy-start(f32[2048]{0:T(1024)S(1)} %add_rsqrt_fusion) | copy-start | bytes 24580
  18.8 32.1 %slice-start.7 = ((s8[5242880]{0:T(1024)(128)(4,1)}), s8[4194304]{0:T(1024)(128)(4,1)S(1)}, s32[]{:S(2)}) async-start(s8[5242880]{0:T(1024)(128)(4,1)} %bitcast.355), calls=%async_computation.22 | async-start | bytes 8388608
  144.9 32.7 %copy-start.8 = (f32[1,1,2048]{2,1,0:T(1,128)}, f32[1,1,2048]{2,1,0:T(1,128)S(1)}, u32[]{:S(2)}) copy-start(f32[1,1,2048]{2,1,0:T(1,128)S(1)} %rsqrt.38) | copy-start | bytes 24580
  145.5 32.1 %copy-start.5 = (bf16[1,1,2048,1280]{2,3,1,0:T(8,128)(2,1)S(1)}, bf16[1,1,2048,1280]{2,3,1,0:T(8,128)(2,1)}, u32[]{:S(2)}) copy-start(bf16[1,1,2048,1280]{2,3,1,0:T(8,128)(2,1)} %get-tuple-element.10) | copy-start | bytes 15728644
  145.5 62.8 %slice-start.8 = ((s8[5242880]{0:T(1024)(128)(4,1)}), s8[4194304]{0:T(1024)(128)(4,1)S(1)}, s32[]{:S(2)}) async-start(s8[5242880]{0:T(1024)(128)(4,1)} %bitcast.357), calls=%async_computation.23 | async-start | bytes 8388608
  177.6 30.7 %slice-start.9 = ((s8[5242880]{0:T(1024)(128)(4,1)}), s8[1048576]{0:T(1024)(128)(4,1)S(1)}, s32[]{:S(2)}) async-start(s8[5242880]{0:T(1024)(128)(4,1)} %bitcast.357), calls=%async_computation.24 | async-start | bytes 2097152
  314.6 37.2 %copy-start.7 = (f32[2048]{0:T(1024)S(1)}, f32[2048]{0:T(1024)}, u32[]{:S(2)}) copy-start(f32[2048]{0:T(1024)} %copy-done.6) | copy-start | bytes 24580
  314.6 37.2 %copy-start.9 = (f32[1,1,2048]{2,1,0:T(1,128)S(1)}, f32[1,1,2048]{2,1,0:T(1,128)}, u32[]{:S(2)}) copy-start(f32[1,1,2048]{2,1,0:T(1,128)} %copy-done.8) | copy-start | bytes 24580
  394.7 324.1 %reduce-scatter.27.cloned.1.call-start = ((), (), s32[]{:S(2)}) async-start(), calls=%async_computation.13 | async-start | bytes 28672000
  444.2 31.8 %copy-start.12 = (f32[2048]{0:T(1024)S(1)}, f32[2048]{0:T(1024)}, u32[]{:S(2)}) copy-start(f32[2048]{0:T(1024)} %copy-done.11) | copy-start | bytes 24580
  444.2 437.1 %reduce-scatter.25.cloned.1.call-start = ((), (), s32[]{:S(2)}) async-start(), calls=%async_computation.12 | async-start | bytes 28672000
  514.8 0.7 copy-start.10
  514.9 528.1 %reduce-scatter.23.cloned.1.call-start = ((), (), s32[]{:S(2)}) async-start(), calls=%async_computation.11 | async-start | bytes 28672000
  554.4 650.9 %reduce-scatter.21.cloned.1.call-start = ((), (), s32[]{:S(2)}) async-start(), calls=%async_computation.10 | async-start | bytes 28672000
  609.4 758.2 %reduce-scatter.19.cloned.1.call-start = ((), (), s32[]{:S(2)}) async-start(), calls=%async_computation.9 | async-start | bytes 28672000
  640.6 0.7 copy-start.13
  640.6 907.5 %all-gather.14.cloned.1.call-start = ((), (), s32[]{:S(2)}) async-start(), calls=%async_computation.8 | async-start | bytes 28672000 | tf_op jit(solution)/reshape | solution.py:58
  645.5 81.4 %copy-start.3 = (bf16[1,1,1120,1280]{3,2,1,0:T(8,128)(2,1)}, bf16[1,1,1120,1280]{3,2,1,0:T(8,128)(2,1)S(1)}, u32[]{:S(2)}) copy-start(bf16[1,1,1120,1280]{3,2,1,0:T(8,128)(2,1)S(1)} %convert_bitcast_fusion.3) | copy-start | bytes 8601604
  721.7 1.6 copy-start.4
  884.2 166.9 %copy-start = (bf16[1,1,320,4480]{3,2,1,0:T(8,128)(2,1)}, bf16[1,1,320,4480]{3,2,1,0:T(8,128)(2,1)S(1)}, u32[]{:S(2)}) copy-start(bf16[1,1,320,4480]{3,2,1,0:T(8,128)(2,1)S(1)} %convert_bitcast_fusion.5) | copy-start | bytes 8601604
  1045.9 1.6 copy-start.2
  1370.6 1.6 copy-start.1
  1409.0 279.6 %all-gather.12.cloned.1.call-start = ((), (), s32[]{:S(2)}) async-start(), calls=%async_computation.7 | async-start | bytes 28672000 | tf_op jit(solution)/reshape | solution.py:58
  1436.5 392.5 %all-gather.10.cloned.1.call-start = ((), (), s32[]{:S(2)}) async-start(), calls=%async_computation.6 | async-start | bytes 28672000 | tf_op jit(solution)/reshape | solution.py:58
  1829.0 37.7 %slice-start = ((s8[22937600]{0:T(1024)(128)(4,1)}), s8[4194304]{0:T(1024)(128)(4,1)S(1)}, s32[]{:S(2)}) async-start(s8[22937600]{0:T(1024)(128)(4,1)} %bitcast.350), calls=%async_computation.15 | async-start | bytes 8388608
  1829.0 37.7 %slice-start.1 = ((s8[22937600]{0:T(1024)(128)(4,1)}), s8[4194304]{0:T(1024)(128)(4,1)S(1)}, s32[]{:S(2)}) async-start(s8[22937600]{0:T(1024)(128)(4,1)} %bitcast.350), calls=%async_computation.16 | async-start | bytes 8388608
  1829.0 37.7 %slice-start.2 = ((s8[22937600]{0:T(1024)(128)(4,1)}), s8[4194304]{0:T(1024)(128)(4,1)S(1)}, s32[]{:S(2)}) async-start(s8[22937600]{0:T(1024)(128)(4,1)} %bitcast.350), calls=%async_computation.17 | async-start | bytes 8388608
  1848.0 18.7 slice-start.3
  1848.0 18.7 slice-start.4
  1848.0 18.7 slice-start.5
  (1 other events, 0.6 us)
Sparse Core Ops, SparseCore 0:
  394.8 162.0 reduce-scatter.28
  559.5 159.2 reduce-scatter.26
  722.0 159.2 reduce-scatter.24
  883.7 159.2 reduce-scatter.22
  1046.0 159.2 reduce-scatter.20
  1208.4 159.2 reduce-scatter.18
  1409.1 138.9 all-gather.13
  1550.2 138.3 all-gather.11
  1690.7 138.3 all-gather.9
where the time goes:
time: 1890 us; the launch traced here: 1880 us
  waiting for transfers between devices  1070 us (57%)
  matrix products  533 us (28%)
  other arithmetic  182 us (10%)
  local copies, waits for them, and re-layouts  68.6 us (4%)
    unnamed x15, waiting for transfers between devices  700 us
    reshape x3, waiting for transfers between devices, step(): t.reshape(-1, *t.shape[2:])  372 us
    dot_general x5, matrix products, layer(): gate = jnp.dot(a, w['w_gate'], preferred_element_type=jnp.float32)  182 us
    dot_general x5, matrix products, layer(): up = jnp.dot(a, w['w_up'], preferred_element_type=jnp.float32)  176 us
    dot_general x5, matrix products, matmul(): jnp.dot(a, w, preferred_element_type=jnp.float32).astype(jnp.bfloat16)  176 us
    unnamed x6, other arithmetic  78.9 us
    reshape x3, other arithmetic, step(): t.reshape(-1, *t.shape[2:])  70.9 us
    unnamed x53, local copies, waits for them, and re-layouts  68 us
  transfers between devices with their start and end apart: 9, of which 8 were waited for; matrix products, arithmetic and copies ran while one was open for 17% of the time, Pallas kernels for 0%

commit v1 on v0

v1 whole, which is shorter than its diff:
```python
import functools

import jax
import jax.numpy as jnp
from jax import lax
from jax.experimental import pallas as pl
from jax.experimental.pallas import tpu as pltpu
from jax.sharding import PartitionSpec as P

BF, F32 = jnp.bfloat16, jnp.float32
NN = (((1,), (0,)), ((), ()))
NT = (((1,), (1,)), ((), ()))
CHUNK = 256
TOKENS, UNITS = 1024, 512


def dot(a, b, dims):
    return lax.dot_general(a, b, dims, preferred_element_type=F32)


def params():
    return pltpu.CompilerParams(vmem_limit_bytes=61 * 2**20)


def cost(flops, nbytes):
    return pl.CostEstimate(flops=int(flops), bytes_accessed=int(nbytes), transcendentals=0)


def out(shape, dtype=BF):
    return jax.ShapeDtypeStruct(shape, dtype)


def once(shape, index):
    return pl.BlockSpec(shape, index, pipeline_mode=pl.Buffered(1))


def sigmoid(x):
    return 0.5 * jnp.tanh(0.5 * x) + 0.5


def chunks(n, size=CHUNK):
    return [slice(at, min(at + size, n)) for at in range(0, n, size)]


def norm(h, a, a_out):
    for r in chunks(a.shape[0]):
        wide = h[r, :].astype(F32)
        scale = lax.rsqrt(jnp.mean(wide * wide, -1, keepdims=True) + 1e-6)
        a[r, :] = (wide * scale).astype(BF)
        a_out[:, r] = a[r, :].T


def at_steps(tile, whole, last_units):
    j, last = pl.program_id(1), pl.num_programs(1) - 1
    pl.when(j < last)(lambda: tile(whole, False))
    pl.when(j == last)(lambda: tile(last_units, True))


def first_kernel(x, wg, wu, wd, a_out, hid, s_out, q_out, h_out, a, units, total, *, last_units):
    @pl.when(pl.program_id(1) == 0)
    def _():
        norm(x, a, a_out)
        total[...] = jnp.zeros_like(total)

    def tile(n, end):
        for c in chunks(n):
            gate, up = dot(a[...], wg[:, c], NN), dot(a[...], wu[:, c], NN)
            sig = sigmoid(gate)
            silu = gate * sig
            units[:, c] = (silu * up).astype(BF)
            hid[c, :] = units[:, c].T
            s_out[:, c] = silu
            q_out[:, c] = up * (sig + silu * (1 - sig))
        for c in chunks(total.shape[1]):
            part = total[:, c] + dot(units[:, :n], wd[:n, c], NN)
            if end:
                h_out[:, c] = x[:, c] + part.astype(BF)
            else:
                total[:, c] = part

    at_steps(tile, hid.shape[0], last_units)


def first(x, w_gate, w_up, w_down):
    t, d = x.shape
    f = w_gate.shape[2]
    n = pl.cdiv(f, UNITS)
    wide = pl.BlockSpec((TOKENS, UNITS), lambda i, j: (i, j))
    weight = pl.BlockSpec((None, d, UNITS), lambda i, j: (0, 0, j))
    state = pl.BlockSpec((TOKENS, d), lambda i, j: (i, 0))
    return pl.pallas_call(
        functools.partial(first_kernel, last_units=f - (n - 1) * UNITS),
        grid=(t // TOKENS, n),
        in_specs=[state, weight, weight, pl.BlockSpec((None, UNITS, d), lambda i, j: (0, j, 0))],
        out_specs=[pl.BlockSpec((d, TOKENS), lambda i, j: (0, i)), pl.BlockSpec((UNITS, TOKENS), lambda i, j: (j, i)), wide, wide, state],
        out_shape=[out((d, t)), out((f, t)), out((t, f), F32), out((t, f), F32), out((t, d))],
        scratch_shapes=[pltpu.VMEM((TOKENS, d), BF), pltpu.VMEM((TOKENS, UNITS), BF), pltpu.VMEM((TOKENS, d), F32)],
        compiler_params=params(),
        cost_estimate=cost(6 * t * d * f, 170e6),
        name="first",
    )(x, w_gate, w_up, w_down)


def second_units(a, dy, wg, wu, wd, hid, dgu, n):
    for c in chunks(n):
        gate, up = dot(a[...], wg[:, c], NN), dot(a[...], wu[:, c], NN)
        back = dot(dy[...], wd[c, :], NT).astype(BF).astype(F32)
        sig = sigmoid(gate)
        silu = gate * sig
        hid[c, :] = (silu * up).astype(BF).T
        dgu[0, :, c] = (back * (up * (sig + silu * (1 - sig)))).astype(BF)
        dgu[1, :, c] = (back * silu).astype(BF)


def second_kernel(h, dy, wg, wu, wd, a_out, hid, dgu, a, *, last_units):
    @pl.when(pl.program_id(1) == 0)
    def _():
        norm(h, a, a_out)

    at_steps(lambda n, end: second_units(a, dy, wg, wu, wd, hid, dgu, n), hid.shape[0], last_units)


def second(h, dy, w_gate, w_up, w_down):
    t, d = h.shape
    f = w_gate.shape[2]
    n = pl.cdiv(f, UNITS)
    weight = pl.BlockSpec((None, d, UNITS), lambda i, j: (1, 0, j))
    state = pl.BlockSpec((TOKENS, d), lambda i, j: (i, 0))
    return pl.pallas_call(
        functools.partial(second_kernel, last_units=f - (n - 1) * UNITS),
        grid=(t // TOKENS, n),
        in_specs=[state, state, weight, weight, pl.BlockSpec((None, UNITS, d), lambda i, j: (1, j, 0))],
        out_specs=[
            pl.BlockSpec((d, TOKENS), lambda i, j: (0, i)),
            pl.BlockSpec((UNITS, TOKENS), lambda i, j: (j, i)),
            pl.BlockSpec((2, TOKENS, UNITS), lambda i, j: (0, i, j)),
        ],
        out_shape=[out((d, t)), out((f, t)), out((2, t, f))],
        scratch_shapes=[pltpu.VMEM((TOKENS, d), BF)],
        compiler_params=params(),
        cost_estimate=cost(6 * t * d * f, 130e6),
        name="second",
    )(h, dy, w_gate, w_up, w_down)


def second_back_kernel(h, dy, wg, wu, wd, a_out, hid, dgu, d_out, a, of_gate, of_up, *, last_units):
    @pl.when(pl.program_id(1) == 0)
    def _():
        norm(h, a, a_out)
        of_gate[...] = jnp.zeros_like(of_gate)
        of_up[...] = jnp.zeros_like(of_up)

    def tile(n, end):
        second_units(a, dy, wg, wu, wd, hid, dgu, n)
        for c in chunks(of_gate.shape[1]):
            gates = of_gate[:, c] + dot(dgu[0, :, :n], wg[c, :n], NT)
            ups = of_up[:, c] + dot(dgu[1, :, :n], wu[c, :n], NT)
            if end:
                of_gate[:, c] = (gates.astype(BF) + ups.astype(BF)).astype(F32)
            else:
                of_gate[:, c], of_up[:, c] = gates, ups
        if end:
            for r in chunks(of_gate.shape[0]):
                da, wide = of_gate[r, :], h[r, :].astype(F32)
                scale = lax.rsqrt(jnp.mean(wide * wide, -1, keepdims=True) + 1e-6)
                along = jnp.mean(da * wide, -1, keepdims=True) * (scale * scale * scale)
                d_out[r, :] = dy[r, :] + (da * scale - wide * along).astype(BF)

    at_steps(tile, hid.shape[0], last_units)


def second_back(h, dy, w_gate, w_up, w_down):
    t, d = h.shape
    f = w_gate.shape[2]
    n = pl.cdiv(f, UNITS)
    weight = pl.BlockSpec((None, d, UNITS), lambda i, j: (1, 0, j))
    state = pl.BlockSpec((TOKENS, d), lambda i, j: (i, 0))
    return pl.pallas_call(
        functools.partial(second_back_kernel, last_units=f - (n - 1) * UNITS),
        grid=(t // TOKENS, n),
        in_specs=[state, state, weight, weight, pl.BlockSpec((None, UNITS, d), lambda i, j: (1, j, 0))],
        out_specs=[
            pl.BlockSpec((d, TOKENS), lambda i, j: (0, i)),
            pl.BlockSpec((UNITS, TOKENS), lambda i, j: (j, i)),
            pl.BlockSpec((2, TOKENS, UNITS), lambda i, j: (0, i, j)),
            state,
        ],
        out_shape=[out((d, t)), out((f, t)), out((2, t, f)), out((t, d))],
        scratch_shapes=[pltpu.VMEM((TOKENS, d), BF), pltpu.VMEM((TOKENS, d), F32), pltpu.VMEM((TOKENS, d), F32)],
        compiler_params=params(),
        cost_estimate=cost(10 * t * d * f, 130e6),
        name="second_back",
    )(h, dy, w_gate, w_up, w_down)


def on(x_same, core_same):
    def block(at):
        return 2 * (at[0] if x_same else 1 - at[0]) + (at[1] if core_same else 1 - at[1])

    return block


def call(kernel, at, grid, in_specs, out_specs, out_shape, operands, flops, nbytes, **kw):
    return pl.pallas_call(
        kernel,
        grid_spec=pltpu.PrefetchScalarGridSpec(num_scalar_prefetch=1, grid=grid, in_specs=in_specs, out_specs=out_specs),
        out_shape=out_shape,
        compiler_params=params(),
        cost_estimate=cost(flops, nbytes),
        **kw,
    )(at, *operands)


def hidden_back_kernel(at, w, d, s, q, hid, dgu, theirs):
    for c in chunks(w.shape[0]):
        back = dot(d[...], w[c, :], NT).astype(BF).astype(F32)
        dgu[1, :, c] = (back * s[:, c]).astype(BF)
        dgu[0, :, c] = (back * q[:, c]).astype(BF)

    @pl.when(pl.program_id(0) < pl.num_programs(0) - 1)
    def _():
        theirs[...] = dot(hid[...], d[...], NN).astype(BF)


def hidden_back(at, w_down, d_h, s, q, hid):
    t, d = d_h.shape
    f = s.shape[1]
    n = pl.cdiv(f, UNITS) - 1
    bg = f // (2 * n)
    wide = pl.BlockSpec((t, UNITS), lambda j, at: (0, j))
    hid = hid.reshape(4, n // 2, bg, t)

    def part(j, at):
        j = jnp.minimum(j, n - 1)
        return (jnp.where(j < n // 2, on(False, False)(at), on(True, False)(at)), j % (n // 2), 0, 0)

    dgu, theirs = call(
        hidden_back_kernel,
        at,
        (n + 1,),
        [
            pl.BlockSpec((None, UNITS, d), lambda j, at: (0, j, 0)),
            once((t, d), lambda j, at: (0, 0)),
            wide,
            wide,
            pl.BlockSpec((None, None, bg, t), part),
        ],
        [pl.BlockSpec((2, t, UNITS), lambda j, at: (0, 0, j)), pl.BlockSpec((None, bg, d), lambda j, at: (jnp.minimum(j, n - 1), 0, 0))],
        [out((2, t, f)), out((n, bg, d))],
        (w_down, d_h, s, q, hid),
        3 * t * d * f,
        150e6,
    )
    return dgu, theirs.reshape(2, f // 4, d)


def wide_kernel(at, *refs, terms, add):
    operands, rest = refs[: 3 * terms], refs[3 * terms :]
    rows = operands[0].shape[0]
    total = 0
    for one, two, right in zip(operands[::3], operands[1::3], operands[2::3], strict=True):
        total = total + dot(jnp.concatenate([one[...], two[...]], 0), right[...], NN)
    if add:
        got, send, keep = rest
        total = total + got[...].reshape(total.shape).astype(F32)
        send[...], keep[...] = total[:rows].astype(BF), total[rows:]
    elif terms == 2:
        send, keep = rest
        send[...], keep[...] = total[:rows].astype(BF), total[rows:]
    else:
        rest[0][...] = total.reshape(rest[0].shape).astype(BF)


def grad_wide(at, pairs, one, two, got=None, bn=1536, both=False):
    rows, t = pairs[0][0].shape[1:]
    f = pairs[0][1].shape[2]
    in_specs, operands = [], []
    for left, right in pairs:
        in_specs += [pl.BlockSpec((None, rows, t), lambda w, j, at, b=b: (b(at), 0, 0)) for b in (one, two)]
        in_specs.append(pl.BlockSpec((None, t, bn), lambda w, j, at: (w, 0, j)))
        operands += [left, left, right]
    pair = pl.BlockSpec((None, 2, rows, bn), lambda w, j, at: (w, 0, 0, j))
    single = pl.BlockSpec((None, rows, bn), lambda w, j, at: (w, 0, j))
    if got is not None:
        in_specs.append(pair)
        operands.append(got)
    if both:
        out_specs, shapes = [pair], [out((2, 2, rows, f))]
    else:
        out_specs, shapes = [single, single], [out((2, rows, f)), out((2, rows, f), F32)]
    return call(
        functools.partial(wide_kernel, terms=len(pairs), add=got is not None),
        at,
        (2, pl.cdiv(f, bn)),
        in_specs,
        out_specs,
        shapes,
        operands,
        8 * rows * t * f * len(pairs),
        60e6,
    )


def tall_kernel(at, *refs, terms, add):
    operands, rest = refs[: 2 * terms], refs[2 * terms :]
    total = 0
    for left, right in zip(operands[::2], operands[1::2], strict=True):
        total = total + dot(left[...], right[...], NN)
    if add:
        total = total + rest[0][...].astype(F32)
    send, keep = rest[-2:]
    half = pl.num_programs(0) // 2

    @pl.when(pl.program_id(0) < half)
    def _():
        send[...] = total.astype(BF)

    @pl.when(pl.program_id(0) >= half)
    def _():
        keep[...] = total


def grad_tall(at, pairs, one, two, got=None):
    rows, t = pairs[0][0].shape[1:]
    d = pairs[0][1].shape[1]
    half = 2
    bm = rows // half
    in_specs, operands = [], []
    for left, right in pairs:
        in_specs += [
            pl.BlockSpec((None, bm, t), lambda j, at: (jnp.where(j < half, one(at), two(at)), j % half, 0)),
            once(right.shape, lambda j, at: (0, 0)),
        ]
        operands += [left, right]
    if got is not None:
        in_specs.append(pl.BlockSpec((None, bm, d), lambda j, at: (j // half, j % half, 0)))
        operands.append(got)
    return call(
        functools.partial(tall_kernel, terms=len(pairs), add=got is not None),
        at,
        (2 * half,),
        in_specs,
        [pl.BlockSpec((bm, d), lambda j, at: (jnp.minimum(j, half - 1), 0)), pl.BlockSpec((bm, d), lambda j, at: (jnp.maximum(j - half, 0), 0))],
        [out((rows, d)), out((rows, d), F32)],
        operands,
        4 * rows * t * d * len(pairs),
        60e6,
    )


def squares_kernel(*refs):
    o = refs[-1]

    @pl.when(pl.program_id(0) == 0)
    def _():
        o[...] = jnp.zeros_like(o)

    total = o[...]
    for keep, far in zip(refs[:-1:2], refs[1:-1:2], strict=True):
        g = (keep[...] + far[...].astype(F32)).astype(BF).astype(F32)
        g = jnp.sum((g * g).reshape(-1, 8, g.shape[1]), 0)
        total = total + sum(g[:, c] for c in chunks(g.shape[1], 128))
    o[...] = total


def sum_of_squares(pairs):
    n = 5
    pairs = [a.reshape(-1, a.shape[-1]) for pair in pairs for a in pair]
    return pl.pallas_call(
        squares_kernel,
        grid=(n,),
        in_specs=[pl.BlockSpec((a.shape[0] // n, a.shape[1]), lambda i: (i, 0)) for a in pairs],
        out_specs=pl.BlockSpec((8, 128), lambda i: (0, 0)),
        out_shape=out((8, 128), F32),
        compiler_params=params(),
        cost_estimate=cost(1e9, 4e6 * len(pairs)),
        name="squares",
    )(*pairs)


UNITS_OF_ROWS = 5


def adam_kernel(at, factor, keep, far, w, m, v, *rest):
    w_out, m_out, v_out = rest[-3:]
    g = (keep[...] + far[...].astype(F32)).astype(BF).astype(F32) * factor[0]
    m_new = 0.9 * m[...] + 0.1 * g
    v_new = 0.95 * v[...] + 0.05 * g * g
    wide = w[...].astype(F32)
    w_out[...] = (wide - 0.02 * (m_new * lax.rsqrt(v_new + 1e-8) + 0.1 * wide)).astype(BF)
    m_out[...] = m_new
    v_out[...] = v_new


def adam(at, factor, layer, which, part, keep, far, w, m, v, before):
    rows, cols = keep.shape[1:]
    br = rows // UNITS_OF_ROWS
    low, high = part
    own = pl.BlockSpec((None, br, cols), lambda i, at: (layer, low + i, 0))
    grad = pl.BlockSpec((None, br, cols), lambda i, at: (which, low + i, 0))
    in_specs = [pl.BlockSpec(memory_space=pltpu.SMEM), grad, grad]
    in_specs += [pl.BlockSpec((None, br, cols), lambda i, at: (layer, (2 * at[0] + at[1]) * UNITS_OF_ROWS + low + i, 0)), own, own]
    operands = [factor, keep, far, w, m, v]
    aliases = {}
    if before is not None:
        aliases = {1 + len(operands): 1, 2 + len(operands): 2}
        operands += before
        in_specs += [pl.BlockSpec(memory_space=pl.ANY)] * 2
    return call(
        adam_kernel,
        at,
        (high - low,),
        in_specs,
        [pl.BlockSpec((br, cols), lambda i, at: (i, 0)), own, own],
        [out((br * (high - low), cols)), out(m.shape, F32), out(v.shape, F32)],
        operands,
        1e9,
        6e6 * (high - low),
        input_output_aliases=aliases,
    )


def place_kernel(at, *refs, count):
    for n in range(count):
        pl.when(pl.program_id(0) == n)(functools.partial(lambda n: refs[-1].__setitem__(..., refs[n][...]), n))


def place(at, layer, part, blocks, wheres, shape, before):
    low, high = part
    k = high - low
    cols = blocks[0].shape[1]
    br = blocks[0].shape[0] // k

    def spec(n):
        return pl.BlockSpec((br, cols), lambda i, j, at: (jnp.where(i < n, 0, jnp.where(i > n, k - 1, j)), 0))

    def where(i, j, at):
        b = wheres[0](at)
        for n, w in enumerate(wheres[1:], 1):
            b = jnp.where(i == n, w(at), b)
        return layer, b * UNITS_OF_ROWS + low + j, 0

    in_specs, operands, aliases = [spec(n) for n in range(len(blocks))], list(blocks), {}
    if before is not None:
        aliases = {1 + len(blocks): 0}
        in_specs.append(pl.BlockSpec(memory_space=pl.ANY))
        operands.append(before)
    return call(
        functools.partial(place_kernel, count=len(blocks)),
        at,
        (len(blocks), k),
        in_specs,
        pl.BlockSpec((None, br, cols), where),
        out(shape),
        operands,
        1e9,
        1.2e6 * k * len(blocks),
        input_output_aliases=aliases,
    )


def after(value, *others):
    return lax.optimization_barrier((value, *others))[0]


ACROSS = [(0, 2), (2, 0), (1, 3), (3, 1)]
SIBLING = [(0, 1), (1, 0), (2, 3), (3, 2)]


def across(a):
    return lax.ppermute(a, "dp", ACROSS)


def sibling(a):
    return lax.ppermute(a, "dp", SIBLING)


def step(x, dy, w_gate, w_up, w_down, m_gate, m_up, m_down, v_gate, v_up, v_down):
    dp = lax.axis_index("dp")
    at = jnp.stack([dp // 2, dp % 2]).astype(jnp.int32)
    x, dy = x[0], dy[0]
    d, f = w_gate.shape[1:]

    def blocks(a):
        return a.reshape(4, a.shape[0] // 4, a.shape[1])

    dy_far = across(dy)
    a1, hid1, s1, q1, h1 = first(x, w_gate, w_up, w_down)
    h1_far = across(h1)
    a2, hid2, dgu2, d1 = second_back(h1, dy, w_gate, w_up, w_down)

    dgu1, theirs = hidden_back(at, w_down, d1, s1, q1, hid1)
    got_down = sibling(theirs)
    (theirs,) = grad_wide(at, [(blocks(a1), dgu1)], on(False, False), on(True, False), both=True)
    got_down = after(got_down, theirs)
    got_wide = sibling(theirs)
    send, keep_down1 = grad_tall(at, [(blocks(hid1), d1)], on(False, True), on(True, True), got_down)
    far_down1 = across(send)
    got_wide = after(got_wide, keep_down1)
    send, keep_wide1 = grad_wide(at, [(blocks(a1), dgu1)], on(False, True), on(True, True), got_wide)
    far_wide1 = across(send)

    h1_far = after(h1_far, keep_wide1)
    a2f, hid2f, dgu2f = second(h1_far, dy_far, w_gate, w_up, w_down)
    send, keep_wide2 = grad_wide(at, [(blocks(a2), dgu2), (blocks(a2f), dgu2f)], on(True, False), on(True, True), bn=768)
    far_wide2 = sibling(send)
    hid2f = after(hid2f, keep_wide2)
    send, keep_down2 = grad_tall(at, [(blocks(hid2), dy), (blocks(hid2f), dy_far)], on(True, False), on(True, True))
    far_down2 = sibling(send)

    most = sum_of_squares([(keep_wide1, far_wide1), (keep_down1, far_down1), (keep_wide2, far_wide2)])
    far_down2 = after(far_down2, most)
    squares = jnp.sum(most + sum_of_squares([(keep_down2, far_down2)]))
    squares = lax.psum(squares, "dp")
    factor = jnp.minimum(1.0, 0.5 * lax.rsqrt(squares / (6 * d * f) + 1e-30)).reshape(1)

    weights = {"gate": (w_gate, m_gate, v_gate), "up": (w_up, m_up, v_up), "down": (w_down, m_down, v_down)}
    grads = [
        ("gate", 1, 0, keep_wide2, far_wide2),
        ("up", 1, 1, keep_wide2, far_wide2),
        ("down", 1, 0, keep_down2[None], far_down2[None]),
        ("gate", 0, 0, keep_wide1, far_wide1),
        ("up", 0, 1, keep_wide1, far_wide1),
        ("down", 0, 0, keep_down1[None], far_down1[None]),
    ]
    placed, moments = dict.fromkeys(weights), dict.fromkeys(weights)
    for which, part in PARTS:
        name, layer, which, keep, far = grads[which]
        w, m, v = weights[name]
        own, *moments[name] = adam(at, factor, layer, which, part, keep, far, w, m, v, moments[name])
        away = across(own)
        beside = sibling(own)
        placed[name] = place(at, layer, part, (own, beside), (on(True, True), on(True, False)), w.shape, placed[name])
        away_beside = sibling(away)
        placed[name] = place(at, layer, part, (away,), (on(False, True),), w.shape, placed[name])
        placed[name] = place(at, layer, part, (away_beside,), (on(False, False),), w.shape, placed[name])
    return (*placed.values(), *(p[0] for p in moments.values()), *(p[1] for p in moments.values()))


PARTS = [(0, (0, 1)), (0, (1, 5)), (1, (0, 5)), (2, (0, 5)), (3, (0, 5)), (4, (0, 5)), (5, (0, 3)), (5, (3, 5))]


def solution(mesh):
    tokens, whole, rows = P(("rep", "dp")), P(), P(None, "dp")

    return jax.shard_map(
        step,
        mesh=mesh,
        in_specs=(tokens,) * 2 + (whole,) * 3 + (rows,) * 6,
        out_specs=(P("rep"),) * 3 + (P("rep", "dp"),) * 6,
        check_vma=False,
    )
```

time: 1890 us -> 1340 us (0.71)
  Pallas kernels: 0 us -> 803 us
  waiting for transfers between devices: 1070 us -> 498 us
  matrix products: 533 us -> 0 us
  other arithmetic: 182 us -> 1.96 us
  local copies, waits for them, and re-layouts: 68.6 us -> 2.57 us
  starting transfers between devices: 0.84 us -> 19.9 us
    pallas_call x0 -> x43, Pallas kernels: none -> 803 us  [the longest x38 455 us: call(): pl.pallas_call(kernel, grid_spec=pltpu.PrefetchScalarGridSpec(num_scalar_...]
    unnamed x15 -> x0, waiting for transfers between devices: 700 us -> none
    dot_general x15 -> x0, matrix products: 533 us -> none  [the longest x5 182 us: layer(): gate = jnp.dot(a, w['w_gate'], preferred_element_type=jnp.float32)]
    ppermute x0 -> x32, waiting for transfers between devices: none -> 498 us  [the longest x12 475 us: across(): return lax.ppermute(a, 'dp', ACROSS)]
    reshape x3 -> x0, waiting for transfers between devices: 372 us -> none  [step(): t.reshape(-1, *t.shape[2:])]
    unnamed x6 -> x0, other arithmetic: 78.9 us -> none
    reshape x3 -> x0, other arithmetic: 70.9 us -> none  [step(): t.reshape(-1, *t.shape[2:])]
    unnamed x53 -> x10, local copies, waits for them, and re-layouts: 68 us -> 2.57 us
  transfers between devices with their start and end apart: 9 -> 32, of which waited for: 8 -> 9; matrix products, arithmetic and copies ran while one was open for 17% -> 0% of each run, Pallas kernels for 0% -> 33%
where the time goes in v1:
time: 1340 us; the launch traced here: 1330 us
  Pallas kernels  803 us (60%)
  waiting for transfers between devices  498 us (37%)
  starting transfers between devices  19.9 us (1%)
    ppermute x12, waiting for transfers between devices, across(): return lax.ppermute(a, 'dp', ACROSS)  475 us
    pallas_call x38, Pallas kernels, call(): pl.pallas_call(kernel, grid_spec=pltpu.PrefetchScalarGridSpec(num_scalar_...  455 us
    pallas_call x1, Pallas kernels, second_back(): pl.pallas_call(functools.partial(second_back_kernel, last_units=f - (n -...  143 us
    pallas_call x1, Pallas kernels, first(): pl.pallas_call(functools.partial(first_kernel, last_units=f - (n - 1) * U...  91.8 us
    pallas_call x1, Pallas kernels, second(): pl.pallas_call(functools.partial(second_kernel, last_units=f - (n - 1) *...  90.2 us
  transfers between devices with their start and end apart: 32, of which 9 were waited for; matrix products, arithmetic and copies ran while one was open for 0% of the time, Pallas kernels for 33%

profile of v1, /device:TPU:0, one launch (start us, length us, event | category | flops | bytes accessed | tf_op | source)
XLA Modules:
  0.0 1334.8 jit_solution(13340763934271081013)
XLA Ops:
  1.3 91.8 %first.1 = (bf16[1280,2048]{1,0:T(8,128)(2,1)}, bf16[4480,2048]{1,0:T(8,128)(2,1)}, f32[2048,4480]{1,0:T(8,128)}, f32[2048,4480]{1,0:T(8,128)}, bf16[2048,1280]{1,0:T(8,128)(2,1)}) custom-call(bf16[2048,1280]{1,0:T(8,128)(2,1)} %bitcast.29, bf16[2,1280,4480]{2,1,0:T(8,128)(2,1)} %w.12, bf16[2,1280,4480]{2,1,0:T(8,128)(2,1)} %w.14, bf16[2,4480,1280]{2,1,0:T(8,128)(2,1)} %w.17), custom_call_target="tpu_custom_call" | custom-call | flops 70464307200 | bytes 170000000 | tf_op jit(solution)/shard_map/first/pallas_call | solution.py:91
  93.1 143.3 %second_back.1 = (bf16[1280,2048]{1,0:T(8,128)(2,1)}, bf16[4480,2048]{1,0:T(8,128)(2,1)}, bf16[2,2048,4480]{2,1,0:T(8,128)(2,1)}, bf16[2048,1280]{1,0:T(8,128)(2,1)}) custom-call(bf16[2048,1280]{1,0:T(8,128)(2,1)} %get-tuple-element.61.h, bf16[2048,1280]{1,0:T(8,128)(2,1)} %bitcast.30, bf16[2,1280,4480]{2,1,0:T(8,128)(2,1)} %w.12, ...), custom_call_target="tpu_custom_call" | custom-call | flops 117440512000 | bytes 130000000 | tf_op jit(solution)/shard_map/second_back/pallas_call | solution.py:178
  236.4 54.5 %shard_map.178 = (bf16[2,2048,4480]{2,1,0:T(8,128)(2,1)}, bf16[8,280,1280]{2,1,0:T(8,128)(2,1)}) custom-call(s32[2]{0:T(128)} %pad_add_fusion.at, bf16[2,4480,1280]{2,1,0:T(8,128)(2,1)} %w.17, bf16[2048,1280]{1,0:T(8,128)(2,1)} %get-tuple-element.62.d.refs_1_, f32[2048,4480]{1,0:T(8,128)} %get-tuple-element.63.s, f32[2048,4480]{1,0:T(8,128)} %get-tuple-element.64.q, ...), custom_call_target="tpu_custom_call" | custom-call | flops 35232153600 | bytes 150000000 | tf_op jit(solution)/shard_map/pallas_call | solution.py:204
  290.9 31.1 %shard_map.179 = bf16[2,2,320,4480]{3,2,1,0:T(8,128)(2,1)} custom-call(s32[2]{0:T(128)} %pad_add_fusion.at, bf16[4,320,2048]{2,1,0:T(8,128)(2,1)} %bitcast.39, bf16[4,320,2048]{2,1,0:T(8,128)(2,1)} %bitcast.40, bf16[2,2048,4480]{2,1,0:T(8,128)(2,1)} %get-tuple-element.66.refs_2_), custom_call_target="tpu_custom_call" | custom-call | flops 23488102400 | bytes 60000000 | tf_op jit(solution)/shard_map/pallas_call | solution.py:204
  325.8 22.7 %collective-permute-done.1.refs_2_ = bf16[2,1120,1280]{2,1,0:T(8,128)(2,1)} collective-permute-done((bf16[2,1120,1280]{2,1,0:T(8,128)(2,1)}, bf16[2,1120,1280]{2,1,0:T(8,128)(2,1)}, u32[]{:S(2)}, u32[]{:S(2)}) %collective-permute-start.1) | collective-permute-done | bytes 5734432 | tf_op jit(solution)/shard_map/ppermute | solution.py:475
  348.6 19.7 %shard_map.180 = (bf16[1120,1280]{1,0:T(8,128)(2,1)}, f32[1120,1280]{1,0:T(8,128)}) custom-call(s32[2]{0:T(128)} %pad_add_fusion.at, bf16[4,1120,2048]{2,1,0:T(8,128)(2,1)} %bitcast.35, bf16[2048,1280]{1,0:T(8,128)(2,1)} %get-tuple-element.62.d.refs_1_, bf16[2,1120,1280]{2,1,0:T(8,128)(2,1)} %collective-permute-done.1.refs_2_), custom_call_target="tpu_custom_call" | custom-call | flops 11744051200 | bytes 60000000 | tf_op jit(solution)/shard_map/pallas_call | solution.py:204
  368.3 32.2 %shard_map.181 = (bf16[2,320,4480]{2,1,0:T(8,128)(2,1)}, f32[2,320,4480]{2,1,0:T(8,128)}) custom-call(s32[2]{0:T(128)} %pad_add_fusion.at, bf16[4,320,2048]{2,1,0:T(8,128)(2,1)} %bitcast.41, bf16[4,320,2048]{2,1,0:T(8,128)(2,1)} %bitcast.42, bf16[2,2048,4480]{2,1,0:T(8,128)(2,1)} %get-tuple-element.66.refs_2_, ...), custom_call_target="tpu_custom_call" | custom-call | flops 23488102400 | bytes 60000000 | tf_op jit(solution)/shard_map/pallas_call | solution.py:204
  403.3 36.7 %collective-permute-done.4.h = bf16[2048,1280]{1,0:T(8,128)(2,1)} collective-permute-done((bf16[2048,1280]{1,0:T(8,128)(2,1)}, bf16[2048,1280]{1,0:T(8,128)(2,1)}, u32[]{:S(2)}, u32[]{:S(2)}) %collective-permute-start.4) | collective-permute-done | bytes 5242912 | tf_op jit(solution)/shard_map/ppermute | solution.py:471
  440.0 112.4 %collective-permute-done.5.dy.refs_3_ = bf16[2048,1280]{1,0:T(8,128)(2,1)} collective-permute-done((bf16[2048,1280]{1,0:T(8,128)(2,1)}, bf16[2048,1280]{1,0:T(8,128)(2,1)}, u32[]{:S(2)}, u32[]{:S(2)}) %collective-permute-start.5) | collective-permute-done | bytes 5242912 | tf_op jit(solution)/shard_map/ppermute | solution.py:471
  552.4 90.2 %second.1 = (bf16[1280,2048]{1,0:T(8,128)(2,1)}, bf16[4480,2048]{1,0:T(8,128)(2,1)}, bf16[2,2048,4480]{2,1,0:T(8,128)(2,1)}) custom-call(bf16[2048,1280]{1,0:T(8,128)(2,1)} %collective-permute-done.4.h, bf16[2048,1280]{1,0:T(8,128)(2,1)} %collective-permute-done.5.dy.refs_3_, bf16[2,1280,4480]{2,1,0:T(8,128)(2,1)} %w.12, bf16[2,1280,4480]{2,1,0:T(8,128)(2,1)} %w.14, ...), custom_call_target="tpu_custom_call" | custom-call | flops 70464307200 | bytes 130000000 | tf_op jit(solution)/shard_map/second/pallas_call | solution.py:129
  642.6 57.6 %shard_map.182 = (bf16[2,320,4480]{2,1,0:T(8,128)(2,1)}, f32[2,320,4480]{2,1,0:T(8,128)}) custom-call(s32[2]{0:T(128)} %pad_add_fusion.at, bf16[4,320,2048]{2,1,0:T(8,128)(2,1)} %bitcast.37, bf16[4,320,2048]{2,1,0:T(8,128)(2,1)} %bitcast.38, bf16[2,2048,4480]{2,1,0:T(8,128)(2,1)} %get-tuple-element.75.refs_2_, bf16[4,320,2048]{2,1,0:T(8,128)(2,1)} %bitcast.43, ...), custom_call_target="tpu_custom_call" | custom-call | flops 46976204800 | bytes 60000000 | tf_op jit(solution)/shard_map/pallas_call | solution.py:204
  702.3 33.5 %shard_map.183 = (bf16[1120,1280]{1,0:T(8,128)(2,1)}, f32[1120,1280]{1,0:T(8,128)}) custom-call(s32[2]{0:T(128)} %pad_add_fusion.at, bf16[4,1120,2048]{2,1,0:T(8,128)(2,1)} %bitcast.33, bf16[2048,1280]{1,0:T(8,128)(2,1)} %bitcast.32, bf16[4,1120,2048]{2,1,0:T(8,128)(2,1)} %bitcast.36, bf16[2048,1280]{1,0:T(8,128)(2,1)} %collective-permute-done.5.dy.refs_3_), custom_call_target="tpu_custom_call" | custom-call | flops 23488102400 | bytes 60000000 | tf_op jit(solution)/shard_map/pallas_call | solution.py:204
  736.0 29.3 %collective-permute-done.3.refs_3_ = bf16[1120,1280]{1,0:T(8,128)(2,1)S(1)} collective-permute-done((bf16[1120,1280]{1,0:T(8,128)(2,1)}, bf16[1120,1280]{1,0:T(8,128)(2,1)S(1)}, u32[]{:S(2)}, u32[]{:S(2)}) %collective-permute-start.3) | collective-permute-done | bytes 2867232 | tf_op jit(solution)/shard_map/ppermute | solution.py:471
  766.8 16.6 %squares.2 = f32[8,128]{1,0:T(8,128)} custom-call(f32[640,4480]{1,0:T(8,128)} %bitcast.22, bf16[640,4480]{1,0:T(8,128)(2,1)} %bitcast.9.refs_1_, f32[1120,1280]{1,0:T(8,128)} %get-tuple-element.69.refs_2_, bf16[1120,1280]{1,0:T(8,128)(2,1)} %copy-done, f32[640,4480]{1,0:T(8,128)} %bitcast.21, bf16[640,4480]{1,0:T(8,128)(2,1)} %bitcast.13.refs_5_), custom_call_target="tpu_custom_call" | custom-call | flops 1000000000 | bytes 24000000 | tf_op jit(solution)/shard_map/squares/pallas_call | solution.py:369
  790.6 7.5 psum.7
  798.8 15.4 %shard_map.204 = (bf16[1120,1280]{1,0:T(8,128)(2,1)}, f32[2,1120,1280]{2,1,0:T(8,128)}, f32[2,1120,1280]{2,1,0:T(8,128)}) custom-call(s32[2]{0:T(128)} %pad_add_fusion.at, f32[1]{0:T(128)} %bitcast.16.factor, f32[1,1120,1280]{2,1,0:T(8,128)} %bitcast.27, bf16[1,1120,1280]{2,1,0:T(8,128)(2,1)} %bitcast.20.far, bf16[2,4480,1280]{2,1,0:T(8,128)(2,1)} %w.17, ...), custom_call_target="tpu_custom_call" | custom-call | flops 1000000000 | bytes 30000000 | tf_op jit(solution)/shard_map/pallas_call | solution.py:204
  814.2 10.3 shard_map.205
  824.5 6.6 shard_map.206
  839.7 32.2 %collective-permute-done.14.refs_0_ = bf16[64,4480]{1,0:T(8,128)(2,1)} collective-permute-done((bf16[64,4480]{1,0:T(8,128)(2,1)}, bf16[64,4480]{1,0:T(8,128)(2,1)}, u32[]{:S(2)}, u32[]{:S(2)}) %collective-permute-start.14) | collective-permute-done | bytes 573472 | tf_op jit(solution)/shard_map/ppermute | solution.py:471
  871.8 11.6 shard_map.185
  883.4 15.4 %shard_map.186 = (bf16[320,4480]{1,0:T(8,128)(2,1)}, f32[2,320,4480]{2,1,0:T(8,128)}, f32[2,320,4480]{2,1,0:T(8,128)}) custom-call(s32[2]{0:T(128)} %pad_add_fusion.at, f32[1]{0:T(128)} %bitcast.16.factor, f32[2,320,4480]{2,1,0:T(8,128)} %get-tuple-element.71.keep, ...), custom_call_target="tpu_custom_call", output_to_operand_aliasing={{1}: (7, {}), {2}: (8, {})} | custom-call | flops 1000000000 | bytes 30000000 | tf_op jit(solution)/shard_map/pallas_call | solution.py:204
  901.9 15.4 %shard_map.196 = (bf16[320,4480]{1,0:T(8,128)(2,1)}, f32[2,320,4480]{2,1,0:T(8,128)}, f32[2,320,4480]{2,1,0:T(8,128)}) custom-call(s32[2]{0:T(128)} %pad_add_fusion.at, f32[1]{0:T(128)} %bitcast.16.factor, f32[2,320,4480]{2,1,0:T(8,128)} %get-tuple-element.79.keep, bf16[2,320,4480]{2,1,0:T(8,128)(2,1)} %collective-permute-done.6.far, ...), custom_call_target="tpu_custom_call" | custom-call | flops 1000000000 | bytes 30000000 | tf_op jit(solution)/shard_map/pallas_call | solution.py:204
  917.9 15.4 %shard_map.197 = (bf16[320,4480]{1,0:T(8,128)(2,1)}, f32[2,320,4480]{2,1,0:T(8,128)}, f32[2,320,4480]{2,1,0:T(8,128)}) custom-call(s32[2]{0:T(128)} %pad_add_fusion.at, f32[1]{0:T(128)} %bitcast.16.factor, f32[2,320,4480]{2,1,0:T(8,128)} %get-tuple-element.71.keep, ...), custom_call_target="tpu_custom_call", output_to_operand_aliasing={{1}: (7, {}), {2}: (8, {})} | custom-call | flops 1000000000 | bytes 30000000 | tf_op jit(solution)/shard_map/pallas_call | solution.py:204
  934.2 85.1 %collective-permute-done.11.refs_0_ = bf16[256,4480]{1,0:T(8,128)(2,1)} collective-permute-done((bf16[256,4480]{1,0:T(8,128)(2,1)}, bf16[256,4480]{1,0:T(8,128)(2,1)}, u32[]{:S(2)}, u32[]{:S(2)}) %collective-permute-start.11) | collective-permute-done | bytes 2293792 | tf_op jit(solution)/shard_map/ppermute | solution.py:471
  1021.3 59.4 %collective-permute-done.17.refs_0_ = bf16[320,4480]{1,0:T(8,128)(2,1)} collective-permute-done((bf16[320,4480]{1,0:T(8,128)(2,1)}, bf16[320,4480]{1,0:T(8,128)(2,1)}, u32[]{:S(2)}, u32[]{:S(2)}) %collective-permute-start.17) | collective-permute-done | bytes 2867232 | tf_op jit(solution)/shard_map/ppermute | solution.py:471
  1081.3 60.9 %collective-permute-done.20.refs_0_ = bf16[320,4480]{1,0:T(8,128)(2,1)} collective-permute-done((bf16[320,4480]{1,0:T(8,128)(2,1)}, bf16[320,4480]{1,0:T(8,128)(2,1)}, u32[]{:S(2)}, u32[]{:S(2)}) %collective-permute-start.20) | collective-permute-done | bytes 2867232 | tf_op jit(solution)/shard_map/ppermute | solution.py:471
  1142.2 59.5 %collective-permute-done.29.refs_0_ = bf16[1120,1280]{1,0:T(8,128)(2,1)} collective-permute-done((bf16[1120,1280]{1,0:T(8,128)(2,1)}, bf16[1120,1280]{1,0:T(8,128)(2,1)}, u32[]{:S(2)}, u32[]{:S(2)}) %collective-permute-start.29) | collective-permute-done | bytes 2867232 | tf_op jit(solution)/shard_map/ppermute | solution.py:471
  1210.8 8.0 shard_map.190.refs_1_
  1223.4 9.2 shard_map.198.refs_1_
  1238.1 9.2 shard_map.207.refs_1_
  1257.9 9.2 shard_map.193.refs_1_
  1278.1 9.2 shard_map.201.refs_1_
  (88 shorter events, 121.8 us)
Async XLA Ops:
  322.0 46.3 %collective-permute-start = (bf16[2,2,320,4480]{3,2,1,0:T(8,128)(2,1)}, bf16[2,2,320,4480]{3,2,1,0:T(8,128)(2,1)}, u32[]{:S(2)}, u32[]{:S(2)}) collective-permute-start(bf16[2,2,320,4480]{3,2,1,0:T(8,128)(2,1)} %shard_map.179), channel_id=1, source_target_pairs={{0,1},{1,0},{2,3},{3,2},{4,5},{5,4},{6,7},{7,6}} | collective-permute-start | bytes 34406408 | tf_op jit(solution)/shard_map/ppermute | solution.py:475
  322.8 25.7 %collective-permute-start.1 = (bf16[2,1120,1280]{2,1,0:T(8,128)(2,1)}, bf16[2,1120,1280]{2,1,0:T(8,128)(2,1)}, u32[]{:S(2)}, u32[]{:S(2)}) collective-permute-start(bf16[2,1120,1280]{2,1,0:T(8,128)(2,1)} %bitcast.28), channel_id=1, source_target_pairs={{0,1},{1,0},{2,3},{3,2},{4,5},{5,4},{6,7},{7,6}} | collective-permute-start | bytes 17203208 | tf_op jit(solution)/shard_map/ppermute | solution.py:475
  322.8 117.2 %collective-permute-start.4 = (bf16[2048,1280]{1,0:T(8,128)(2,1)}, bf16[2048,1280]{1,0:T(8,128)(2,1)}, u32[]{:S(2)}, u32[]{:S(2)}) collective-permute-start(bf16[2048,1280]{1,0:T(8,128)(2,1)} %get-tuple-element.61.h), channel_id=1, source_target_pairs={{0,2},{2,0},{1,3},{3,1},{4,6},{6,4},{5,7},{7,5}} | collective-permute-start | bytes 15728648 | tf_op jit(solution)/shard_map/ppermute | solution.py:471
  325.8 226.6 %collective-permute-start.5 = (bf16[2048,1280]{1,0:T(8,128)(2,1)}, bf16[2048,1280]{1,0:T(8,128)(2,1)}, u32[]{:S(2)}, u32[]{:S(2)}) collective-permute-start(bf16[2048,1280]{1,0:T(8,128)(2,1)} %bitcast.31), channel_id=1, source_target_pairs={{0,2},{2,0},{1,3},{3,1},{4,6},{6,4},{5,7},{7,5}} | collective-permute-start | bytes 15728648 | tf_op jit(solution)/shard_map/ppermute | solution.py:471
  400.5 364.8 %collective-permute-start.2 = (bf16[2,320,4480]{2,1,0:T(8,128)(2,1)}, bf16[2,320,4480]{2,1,0:T(8,128)(2,1)}, u32[]{:S(2)}, u32[]{:S(2)}) collective-permute-start(bf16[2,320,4480]{2,1,0:T(8,128)(2,1)} %get-tuple-element.72), channel_id=1, source_target_pairs={{0,2},{2,0},{1,3},{3,1},{4,6},{6,4},{5,7},{7,5}} | collective-permute-start | bytes 17203208 | tf_op jit(solution)/shard_map/ppermute | solution.py:471
  700.2 65.0 %collective-permute-start.6 = (bf16[2,320,4480]{2,1,0:T(8,128)(2,1)}, bf16[2,320,4480]{2,1,0:T(8,128)(2,1)}, u32[]{:S(2)}, u32[]{:S(2)}) collective-permute-start(bf16[2,320,4480]{2,1,0:T(8,128)(2,1)} %get-tuple-element.80), channel_id=1, source_target_pairs={{0,1},{1,0},{2,3},{3,2},{4,5},{5,4},{6,7},{7,6}} | collective-permute-start | bytes 17203208 | tf_op jit(solution)/shard_map/ppermute | solution.py:475
  700.2 65.0 %collective-permute-start.3 = (bf16[1120,1280]{1,0:T(8,128)(2,1)}, bf16[1120,1280]{1,0:T(8,128)(2,1)S(1)}, u32[]{:S(2)}, u32[]{:S(2)}) collective-permute-start(bf16[1120,1280]{1,0:T(8,128)(2,1)} %get-tuple-element.73), channel_id=1, source_target_pairs={{0,2},{2,0},{1,3},{3,1},{4,6},{6,4},{5,7},{7,5}} | collective-permute-start | bytes 8601608 | tf_op jit(solution)/shard_map/ppermute | solution.py:471
  735.8 47.6 %collective-permute-start.7 = (bf16[1120,1280]{1,0:T(8,128)(2,1)}, bf16[1120,1280]{1,0:T(8,128)(2,1)}, u32[]{:S(2)}, u32[]{:S(2)}) collective-permute-start(bf16[1120,1280]{1,0:T(8,128)(2,1)} %get-tuple-element.85), channel_id=1, source_target_pairs={{0,1},{1,0},{2,3},{3,2},{4,5},{5,4},{6,7},{7,6}} | collective-permute-start | bytes 8601608 | tf_op jit(solution)/shard_map/ppermute | solution.py:475
  831.1 68.7 %collective-permute-start.23 = (bf16[448,1280]{1,0:T(8,128)(2,1)}, bf16[448,1280]{1,0:T(8,128)(2,1)S(1)}, u32[]{:S(2)}, u32[]{:S(2)}) collective-permute-start(bf16[448,1280]{1,0:T(8,128)(2,1)} %get-tuple-element.102.refs_0_), channel_id=1, source_target_pairs={{0,2},{2,0},{1,3},{3,1},{4,6},{6,4},{5,7},{7,5}} | collective-permute-start | bytes 3440648 | tf_op jit(solution)/shard_map/ppermute | solution.py:471
  837.1 34.7 %collective-permute-start.14 = (bf16[64,4480]{1,0:T(8,128)(2,1)}, bf16[64,4480]{1,0:T(8,128)(2,1)}, u32[]{:S(2)}, u32[]{:S(2)}) collective-permute-start(bf16[64,4480]{1,0:T(8,128)(2,1)} %get-tuple-element.93.refs_0_), channel_id=1, source_target_pairs={{0,2},{2,0},{1,3},{3,1},{4,6},{6,4},{5,7},{7,5}} | collective-permute-start | bytes 1720328 | tf_op jit(solution)/shard_map/ppermute | solution.py:471
  838.3 79.1 %collective-permute-start.26 = (bf16[672,1280]{1,0:T(8,128)(2,1)}, bf16[672,1280]{1,0:T(8,128)(2,1)}, u32[]{:S(2)}, u32[]{:S(2)}) collective-permute-start(bf16[672,1280]{1,0:T(8,128)(2,1)} %get-tuple-element.103.refs_0_), channel_id=1, source_target_pairs={{0,2},{2,0},{1,3},{3,1},{4,6},{6,4},{5,7},{7,5}} | collective-permute-start | bytes 5160968 | tf_op jit(solution)/shard_map/ppermute | solution.py:471
  839.2 94.2 %collective-permute-start.28 = (bf16[672,1280]{1,0:T(8,128)(2,1)}, bf16[672,1280]{1,0:T(8,128)(2,1)}, u32[]{:S(2)}, u32[]{:S(2)}) collective-permute-start(bf16[672,1280]{1,0:T(8,128)(2,1)} %get-tuple-element.103.refs_0_), channel_id=1, source_target_pairs={{0,1},{1,0},{2,3},{3,2},{4,5},{5,4},{6,7},{7,6}} | collective-permute-start | bytes 5160968 | tf_op jit(solution)/shard_map/ppermute | solution.py:475
  839.2 59.7 %collective-permute-start.16 = (bf16[64,4480]{1,0:T(8,128)(2,1)}, bf16[64,4480]{1,0:T(8,128)(2,1)S(1)}, u32[]{:S(2)}, u32[]{:S(2)}) collective-permute-start(bf16[64,4480]{1,0:T(8,128)(2,1)} %get-tuple-element.93.refs_0_), channel_id=1, source_target_pairs={{0,1},{1,0},{2,3},{3,2},{4,5},{5,4},{6,7},{7,6}} | collective-permute-start | bytes 1720328 | tf_op jit(solution)/shard_map/ppermute | solution.py:475
  871.8 30.1 %collective-permute-start.15 = (bf16[64,4480]{1,0:T(8,128)(2,1)}, bf16[64,4480]{1,0:T(8,128)(2,1)}, u32[]{:S(2)}, u32[]{:S(2)}) collective-permute-start(bf16[64,4480]{1,0:T(8,128)(2,1)} %collective-permute-done.14.refs_0_), channel_id=1, source_target_pairs={{0,1},{1,0},{2,3},{3,2},{4,5},{5,4},{6,7},{7,6}} | collective-permute-start | bytes 1720328 | tf_op jit(solution)/shard_map/ppermute | solution.py:475
  898.9 121.3 %collective-permute-start.8 = (bf16[320,4480]{1,0:T(8,128)(2,1)}, bf16[320,4480]{1,0:T(8,128)(2,1)}, u32[]{:S(2)}, u32[]{:S(2)}) collective-permute-start(bf16[320,4480]{1,0:T(8,128)(2,1)} %get-tuple-element.91.refs_0_), channel_id=1, source_target_pairs={{0,2},{2,0},{1,3},{3,1},{4,6},{6,4},{5,7},{7,5}} | collective-permute-start | bytes 8601608 | tf_op jit(solution)/shard_map/ppermute | solution.py:471
  900.8 118.5 %collective-permute-start.11 = (bf16[256,4480]{1,0:T(8,128)(2,1)}, bf16[256,4480]{1,0:T(8,128)(2,1)}, u32[]{:S(2)}, u32[]{:S(2)}) collective-permute-start(bf16[256,4480]{1,0:T(8,128)(2,1)} %get-tuple-element.92.refs_0_), channel_id=1, source_target_pairs={{0,2},{2,0},{1,3},{3,1},{4,6},{6,4},{5,7},{7,5}} | collective-permute-start | bytes 6881288 | tf_op jit(solution)/shard_map/ppermute | solution.py:471
  901.9 117.4 %collective-permute-start.13 = (bf16[256,4480]{1,0:T(8,128)(2,1)}, bf16[256,4480]{1,0:T(8,128)(2,1)}, u32[]{:S(2)}, u32[]{:S(2)}) collective-permute-start(bf16[256,4480]{1,0:T(8,128)(2,1)} %get-tuple-element.92.refs_0_), channel_id=1, source_target_pairs={{0,1},{1,0},{2,3},{3,2},{4,5},{5,4},{6,7},{7,6}} | collective-permute-start | bytes 6881288 | tf_op jit(solution)/shard_map/ppermute | solution.py:475
  917.4 103.9 %collective-permute-start.10 = (bf16[320,4480]{1,0:T(8,128)(2,1)S(1)}, bf16[320,4480]{1,0:T(8,128)(2,1)}, u32[]{:S(2)}, u32[]{:S(2)}) collective-permute-start(bf16[320,4480]{1,0:T(8,128)(2,1)S(1)} %copy-done.1), channel_id=1, source_target_pairs={{0,1},{1,0},{2,3},{3,2},{4,5},{5,4},{6,7},{7,6}} | collective-permute-start | bytes 8601608 | tf_op jit(solution)/shard_map/ppermute | solution.py:475
  933.3 147.4 %collective-permute-start.17 = (bf16[320,4480]{1,0:T(8,128)(2,1)}, bf16[320,4480]{1,0:T(8,128)(2,1)}, u32[]{:S(2)}, u32[]{:S(2)}) collective-permute-start(bf16[320,4480]{1,0:T(8,128)(2,1)} %get-tuple-element.96.refs_0_), channel_id=1, source_target_pairs={{0,2},{2,0},{1,3},{3,1},{4,6},{6,4},{5,7},{7,5}} | collective-permute-start | bytes 8601608 | tf_op jit(solution)/shard_map/ppermute | solution.py:471
  1019.3 61.4 %collective-permute-start.19 = (bf16[320,4480]{1,0:T(8,128)(2,1)}, bf16[320,4480]{1,0:T(8,128)(2,1)}, u32[]{:S(2)}, u32[]{:S(2)}) collective-permute-start(bf16[320,4480]{1,0:T(8,128)(2,1)} %get-tuple-element.96.refs_0_), channel_id=1, source_target_pairs={{0,1},{1,0},{2,3},{3,2},{4,5},{5,4},{6,7},{7,6}} | collective-permute-start | bytes 8601608 | tf_op jit(solution)/shard_map/ppermute | solution.py:475
  1019.3 122.9 %collective-permute-start.20 = (bf16[320,4480]{1,0:T(8,128)(2,1)}, bf16[320,4480]{1,0:T(8,128)(2,1)}, u32[]{:S(2)}, u32[]{:S(2)}) collective-permute-start(bf16[320,4480]{1,0:T(8,128)(2,1)} %get-tuple-element.97.refs_0_), channel_id=1, source_target_pairs={{0,2},{2,0},{1,3},{3,1},{4,6},{6,4},{5,7},{7,5}} | collective-permute-start | bytes 8601608 | tf_op jit(solution)/shard_map/ppermute | solution.py:471
  1020.2 181.5 %collective-permute-start.29 = (bf16[1120,1280]{1,0:T(8,128)(2,1)}, bf16[1120,1280]{1,0:T(8,128)(2,1)}, u32[]{:S(2)}, u32[]{:S(2)}) collective-permute-start(bf16[1120,1280]{1,0:T(8,128)(2,1)} %get-tuple-element.104.refs_0_), channel_id=1, source_target_pairs={{0,2},{2,0},{1,3},{3,1},{4,6},{6,4},{5,7},{7,5}} | collective-permute-start | bytes 8601608 | tf_op jit(solution)/shard_map/ppermute | solution.py:471
  1021.3 180.3 %collective-permute-start.22 = (bf16[320,4480]{1,0:T(8,128)(2,1)}, bf16[320,4480]{1,0:T(8,128)(2,1)}, u32[]{:S(2)}, u32[]{:S(2)}) collective-permute-start(bf16[320,4480]{1,0:T(8,128)(2,1)} %get-tuple-element.97.refs_0_), channel_id=1, source_target_pairs={{0,1},{1,0},{2,3},{3,2},{4,5},{5,4},{6,7},{7,6}} | collective-permute-start | bytes 8601608 | tf_op jit(solution)/shard_map/ppermute | solution.py:475
  1080.7 121.5 %collective-permute-start.31 = (bf16[1120,1280]{1,0:T(8,128)(2,1)}, bf16[1120,1280]{1,0:T(8,128)(2,1)}, u32[]{:S(2)}, u32[]{:S(2)}) collective-permute-start(bf16[1120,1280]{1,0:T(8,128)(2,1)} %get-tuple-element.104.refs_0_), channel_id=1, source_target_pairs={{0,1},{1,0},{2,3},{3,2},{4,5},{5,4},{6,7},{7,6}} | collective-permute-start | bytes 8601608 | tf_op jit(solution)/shard_map/ppermute | solution.py:475
  1080.8 121.5 %collective-permute-start.12 = (bf16[256,4480]{1,0:T(8,128)(2,1)}, bf16[256,4480]{1,0:T(8,128)(2,1)}, u32[]{:S(2)}, u32[]{:S(2)}) collective-permute-start(bf16[256,4480]{1,0:T(8,128)(2,1)} %collective-permute-done.11.refs_0_), channel_id=1, source_target_pairs={{0,1},{1,0},{2,3},{3,2},{4,5},{5,4},{6,7},{7,6}} | collective-permute-start | bytes 6881288 | tf_op jit(solution)/shard_map/ppermute | solution.py:475
  1142.2 90.4 %collective-permute-start.21 = (bf16[320,4480]{1,0:T(8,128)(2,1)}, bf16[320,4480]{1,0:T(8,128)(2,1)}, u32[]{:S(2)}, u32[]{:S(2)}) collective-permute-start(bf16[320,4480]{1,0:T(8,128)(2,1)} %collective-permute-done.20.refs_0_), channel_id=1, source_target_pairs={{0,1},{1,0},{2,3},{3,2},{4,5},{5,4},{6,7},{7,6}} | collective-permute-start | bytes 8601608 | tf_op jit(solution)/shard_map/ppermute | solution.py:475
  1201.7 55.7 %collective-permute-start.30 = (bf16[1120,1280]{1,0:T(8,128)(2,1)}, bf16[1120,1280]{1,0:T(8,128)(2,1)S(1)}, u32[]{:S(2)}, u32[]{:S(2)}) collective-permute-start(bf16[1120,1280]{1,0:T(8,128)(2,1)} %collective-permute-done.29.refs_0_), channel_id=1, source_target_pairs={{0,1},{1,0},{2,3},{3,2},{4,5},{5,4},{6,7},{7,6}} | collective-permute-start | bytes 8601608 | tf_op jit(solution)/shard_map/ppermute | solution.py:475
  1201.7 118.9 %collective-permute-start.9 = (bf16[320,4480]{1,0:T(8,128)(2,1)}, bf16[320,4480]{1,0:T(8,128)(2,1)}, u32[]{:S(2)}, u32[]{:S(2)}) collective-permute-start(bf16[320,4480]{1,0:T(8,128)(2,1)} %collective-permute-done.8.refs_0_), channel_id=1, source_target_pairs={{0,1},{1,0},{2,3},{3,2},{4,5},{5,4},{6,7},{7,6}} | collective-permute-start | bytes 8601608 | tf_op jit(solution)/shard_map/ppermute | solution.py:475
  1202.2 123.9 %collective-permute-start.18 = (bf16[320,4480]{1,0:T(8,128)(2,1)}, bf16[320,4480]{1,0:T(8,128)(2,1)}, u32[]{:S(2)}, u32[]{:S(2)}) collective-permute-start(bf16[320,4480]{1,0:T(8,128)(2,1)} %collective-permute-done.17.refs_0_), channel_id=1, source_target_pairs={{0,1},{1,0},{2,3},{3,2},{4,5},{5,4},{6,7},{7,6}} | collective-permute-start | bytes 8601608 | tf_op jit(solution)/shard_map/ppermute | solution.py:475
  1202.2 106.5 %collective-permute-start.27 = (bf16[672,1280]{1,0:T(8,128)(2,1)}, bf16[672,1280]{1,0:T(8,128)(2,1)}, u32[]{:S(2)}, u32[]{:S(2)}) collective-permute-start(bf16[672,1280]{1,0:T(8,128)(2,1)} %collective-permute-done.26.refs_0_), channel_id=1, source_target_pairs={{0,1},{1,0},{2,3},{3,2},{4,5},{5,4},{6,7},{7,6}} | collective-permute-start | bytes 5160968 | tf_op jit(solution)/shard_map/ppermute | solution.py:475
  1232.6 80.3 %collective-permute-start.25 = (bf16[448,1280]{1,0:T(8,128)(2,1)}, bf16[448,1280]{1,0:T(8,128)(2,1)}, u32[]{:S(2)}, u32[]{:S(2)}) collective-permute-start(bf16[448,1280]{1,0:T(8,128)(2,1)} %get-tuple-element.102.refs_0_), channel_id=1, source_target_pairs={{0,1},{1,0},{2,3},{3,2},{4,5},{5,4},{6,7},{7,6}} | collective-permute-start | bytes 3440648 | tf_op jit(solution)/shard_map/ppermute | solution.py:475
  1257.4 74.2 %collective-permute-start.24 = (bf16[448,1280]{1,0:T(8,128)(2,1)}, bf16[448,1280]{1,0:T(8,128)(2,1)}, u32[]{:S(2)}, u32[]{:S(2)}) collective-permute-start(bf16[448,1280]{1,0:T(8,128)(2,1)} %copy-done.3), channel_id=1, source_target_pairs={{0,1},{1,0},{2,3},{3,2},{4,5},{5,4},{6,7},{7,6}} | collective-permute-start | bytes 3440648 | tf_op jit(solution)/shard_map/ppermute | solution.py:475
  (5 other events, 29.8 us)

commit v2 on v0

v2 whole, which is shorter than its diff:
```python
import functools

import jax
import jax.numpy as jnp
from jax import lax
from jax.experimental import pallas as pl
from jax.experimental.pallas import tpu as pltpu
from jax.sharding import PartitionSpec as P

BF, F32 = jnp.bfloat16, jnp.float32
NN = (((1,), (0,)), ((), ()))
NT = (((1,), (1,)), ((), ()))
CHUNK = 256
TOKENS, UNITS = 1024, 512


def dot(a, b, dims):
    return lax.dot_general(a, b, dims, preferred_element_type=F32)


def params():
    return pltpu.CompilerParams(vmem_limit_bytes=61 * 2**20)


def cost(flops, nbytes):
    return pl.CostEstimate(flops=int(flops), bytes_accessed=int(nbytes), transcendentals=0)


def out(shape, dtype=BF):
    return jax.ShapeDtypeStruct(shape, dtype)


def once(shape, index):
    return pl.BlockSpec(shape, index, pipeline_mode=pl.Buffered(1))


def call(kernel, at, grid, in_specs, out_specs, out_shape, operands, flops, nbytes, scratch=(), **kw):
    return pl.pallas_call(
        kernel,
        grid_spec=pltpu.PrefetchScalarGridSpec(
            num_scalar_prefetch=1, grid=grid, in_specs=in_specs, out_specs=out_specs, scratch_shapes=scratch
        ),
        out_shape=out_shape,
        compiler_params=params(),
        cost_estimate=cost(flops, nbytes),
        **kw,
    )(at, *operands)


def sigmoid(x):
    return 0.5 * jnp.tanh(0.5 * x) + 0.5


def chunks(n, size=CHUNK):
    return [slice(at, min(at + size, n)) for at in range(0, n, size)]


def loop(n, size, body):
    lax.fori_loop(0, n, lambda i, _: body(pl.ds(pl.multiple_of(i * size, size), size)), None)


def norm(h, a, a_out):
    def rows(r):
        wide = h[r, :].astype(F32)
        scale = lax.rsqrt(jnp.mean(wide * wide, -1, keepdims=True) + 1e-6)
        a[r, :] = (wide * scale).astype(BF)
        a_out[:, r] = a[r, :].T

    loop(a.shape[0] // CHUNK, CHUNK, rows)


def only(a, n, axis):
    return jnp.where(lax.broadcasted_iota(jnp.int32, a.shape, axis) < n, a, jnp.zeros_like(a))


def first_kernel(at, x, wg, wu, wd, m, v, a_out, hid, s_out, q_out, h_out, half, a, units, total, *, f):
    j = pl.program_id(1)
    left = f - j * UNITS
    half[...] = jnp.where(at[2] == 0, m[...], v[...])

    @pl.when(j == 0)
    def _():
        norm(x, a, a_out)
        total[...] = jnp.zeros_like(total)

    for c in chunks(UNITS):
        gate, up = dot(a[...], wg[:, c], NN), dot(a[...], wu[:, c], NN)
        sig = sigmoid(gate)
        silu = gate * sig
        units[:, c] = only((silu * up).astype(BF), left - c.start, 1)
        hid[c, :] = units[:, c].T
        s_out[:, c] = silu
        q_out[:, c] = up * (sig + silu * (1 - sig))
    for c in chunks(total.shape[1]):
        total[:, c] += dot(units[...], only(wd[:, c], left, 0), NN)

    @pl.when(j == pl.num_programs(1) - 1)
    def _():
        def rows(r):
            h_out[r, :] = x[r, :] + total[r, :].astype(BF)

        loop(x.shape[0] // CHUNK, CHUNK, rows)


def first(at, x, w_gate, w_up, w_down, m, v):
    t, d = x.shape
    f = w_gate.shape[2]
    n = pl.cdiv(f, UNITS)
    wide = pl.BlockSpec((TOKENS, UNITS), lambda i, j, at: (i, j))
    weight = pl.BlockSpec((None, d, UNITS), lambda i, j, at: (0, 0, j))
    state = pl.BlockSpec((TOKENS, d), lambda i, j, at: (i, 0))
    cols = UNITS * TOKENS // t

    def moment(rep):
        return pl.BlockSpec((None, m.shape[1], cols), lambda i, j, at: (1, 0, jnp.where(at[2] == rep, i * n + j, 0)))

    return call(
        functools.partial(first_kernel, f=f),
        at,
        (t // TOKENS, n),
        [state, weight, weight, pl.BlockSpec((None, UNITS, d), lambda i, j, at: (0, j, 0)), moment(0), moment(1)],
        [
            pl.BlockSpec((d, TOKENS), lambda i, j, at: (0, i)),
            pl.BlockSpec((UNITS, TOKENS), lambda i, j, at: (j, i)),
            wide,
            wide,
            state,
            pl.BlockSpec((m.shape[1], cols), lambda i, j, at: (0, i * n + j)),
        ],
        [out((d, t)), out((f, t)), out((t, f), F32), out((t, f), F32), out((t, d)), out(m.shape[1:], F32)],
        (x, w_gate, w_up, w_down, m, v),
        6 * t * d * f,
        190e6,
        scratch=[pltpu.VMEM((TOKENS, d), BF), pltpu.VMEM((TOKENS, UNITS), BF), pltpu.VMEM((TOKENS, d), F32)],
    )


def second_units(a, dy, wg, wu, wd, hid, dgu, left):
    for c in chunks(UNITS):
        gate, up = dot(a[...], wg[:, c], NN), dot(a[...], wu[:, c], NN)
        back = dot(dy[...], wd[c, :], NT).astype(BF).astype(F32)
        sig = sigmoid(gate)
        silu = gate * sig
        hid[c, :] = (silu * up).astype(BF).T
        dgu[0, :, c] = only((back * (up * (sig + silu * (1 - sig)))).astype(BF), left - c.start, 1)
        dgu[1, :, c] = only((back * silu).astype(BF), left - c.start, 1)


def second_kernel(at, h, dy, wg, wu, wd, a_before, dgu_before, a_out, dgu, hid, a, *, f):
    j = pl.program_id(1)

    @pl.when(j == 0)
    def _():
        norm(h, a, a_out)

    second_units(a, dy, wg, wu, wd, hid, dgu, f - j * UNITS)


def second_back_kernel(at, h, dy, wg, wu, wd, a_out, dgu, hid, d_out, a, of_gate, of_up, *, f):
    j = pl.program_id(1)
    left = f - j * UNITS

    @pl.when(j == 0)
    def _():
        norm(h, a, a_out)
        of_gate[...] = jnp.zeros_like(of_gate)
        of_up[...] = jnp.zeros_like(of_up)

    second_units(a, dy, wg, wu, wd, hid, dgu, left)
    for c in chunks(of_gate.shape[1]):
        of_gate[:, c] += dot(dgu[0], only(wg[c, :], left, 1), NT)
        of_up[:, c] += dot(dgu[1], only(wu[c, :], left, 1), NT)

    @pl.when(j == pl.num_programs(1) - 1)
    def _():
        def rows(r):
            da = (of_gate[r, :].astype(BF) + of_up[r, :].astype(BF)).astype(F32)
            wide = h[r, :].astype(F32)
            scale = lax.rsqrt(jnp.mean(wide * wide, -1, keepdims=True) + 1e-6)
            along = jnp.mean(da * wide, -1, keepdims=True) * (scale * scale * scale)
            d_out[r, :] = dy[r, :] + (da * scale - wide * along).astype(BF)

        loop(h.shape[0] // CHUNK, CHUNK, rows)


def second(at, h, dy, w_gate, w_up, w_down, before=None):
    t, d = h.shape
    f = w_gate.shape[2]
    weight = pl.BlockSpec((None, d, UNITS), lambda i, j, at: (1, 0, j))
    state = pl.BlockSpec((TOKENS, d), lambda i, j, at: (i, 0))
    far = before is not None
    which = (lambda at: 1 - at[0]) if far else (lambda at: at[0])
    in_specs = [state, state, weight, weight, pl.BlockSpec((None, UNITS, d), lambda i, j, at: (1, j, 0))]
    out_specs = [
        pl.BlockSpec((None, d, TOKENS), lambda i, j, at: (which(at), 0, i)),
        pl.BlockSpec((None, 2, TOKENS, UNITS), lambda i, j, at: (which(at), 0, i, j)),
        pl.BlockSpec((UNITS, TOKENS), lambda i, j, at: (j, i)),
    ]
    shapes = [out((2, d, t)), out((2, 2, t, f)), out((f, t))]
    scratch = [pltpu.VMEM((TOKENS, d), BF)]
    operands = [h, dy, w_gate, w_up, w_down]
    aliases = {}
    if far:
        aliases = {6: 0, 7: 1}
        in_specs += [pl.BlockSpec(memory_space=pl.ANY)] * 2
        operands += before
    else:
        out_specs.append(state)
        shapes.append(out((t, d)))
        scratch += [pltpu.VMEM((TOKENS, d), F32)] * 2
    return pl.pallas_call(
        functools.partial(second_kernel if far else second_back_kernel, f=f),
        grid_spec=pltpu.PrefetchScalarGridSpec(
            num_scalar_prefetch=1,
            grid=(t // TOKENS, pl.cdiv(f, UNITS)),
            in_specs=in_specs,
            out_specs=out_specs,
            scratch_shapes=scratch,
        ),
        out_shape=shapes,
        input_output_aliases=aliases,
        compiler_params=params(),
        cost_estimate=cost((6 if far else 10) * t * d * f, 130e6),
        name="second" if far else "second_back",
    )(at, *operands)


def on(x_same, core_same):
    def block(at):
        return 2 * (at[0] if x_same else 1 - at[0]) + (at[1] if core_same else 1 - at[1])

    return block


def hidden_back_kernel(at, w, d, s, q, one, two, dgu, theirs):
    for c in chunks(UNITS):
        back = dot(d[...], w[c, :], NT).astype(BF).astype(F32)
        dgu[1, :, c] = (back * s[:, c]).astype(BF)
        dgu[0, :, c] = (back * q[:, c]).astype(BF)
    left = jnp.concatenate([one[...], two[...]], 0)
    for which in range(2):
        theirs[which] = dot(left, dgu[which], NN).reshape(theirs.shape[1:]).astype(BF)


def hidden_back(at, w_down, d_h, s, q, a):
    t, d = d_h.shape
    f = s.shape[1]
    rows = a.shape[1]
    wide = pl.BlockSpec((t, UNITS), lambda j, at: (0, j))
    return call(
        hidden_back_kernel,
        at,
        (pl.cdiv(f, UNITS),),
        [
            pl.BlockSpec((None, UNITS, d), lambda j, at: (0, j, 0)),
            once((t, d), lambda j, at: (0, 0)),
            wide,
            wide,
            once((None, rows, t), lambda j, at: (on(False, False)(at), 0, 0)),
            once((None, rows, t), lambda j, at: (on(True, False)(at), 0, 0)),
        ],
        [pl.BlockSpec((2, t, UNITS), lambda j, at: (0, 0, j)), pl.BlockSpec((2, 2, rows, UNITS), lambda j, at: (0, 0, 0, j))],
        [out((2, t, f)), out((2, 2, rows, f))],
        (w_down, d_h, s, q, a, a),
        4 * t * d * f,
        160e6,
    )


def wide_kernel(at, one, two, right, got, send, keep):
    rows = one.shape[0]
    total = dot(jnp.concatenate([one[...], two[...]], 0), right[...], NN)
    total = total + got[...].reshape(total.shape).astype(F32)
    send[...], keep[...] = total[:rows].astype(BF), total[rows:]


def grad_wide(at, left, right, one, two, got):
    rows, t = left.shape[1:]
    f = right.shape[2]
    bn = 1536
    return call(
        wide_kernel,
        at,
        (2, pl.cdiv(f, bn)),
        [once((None, rows, t), lambda w, j, at, b=b: (b(at), 0, 0)) for b in (one, two)]
        + [pl.BlockSpec((None, t, bn), lambda w, j, at: (w, 0, j)), pl.BlockSpec((None, 2, rows, bn), lambda w, j, at: (w, 0, 0, j))],
        [pl.BlockSpec((None, rows, bn), lambda w, j, at: (w, 0, j))] * 2,
        [out((2, rows, f)), out((2, rows, f), F32)],
        (left, left, right, got),
        8 * rows * t * f,
        60e6,
    )


def whole_kernel(at, left0, left1, right0, right1, send_far, keep_far, send, keep, total):
    x, c = at[0], at[1]
    rows = send.shape[0]

    def product(r):
        return (dot(left0[r, :], right0[...], NN) + dot(left1[r, :], right1[...], NN)).reshape(-1, *total.shape[1:])

    @pl.when(pl.program_id(0) == 0)
    def _():
        total[...] = product(slice(None))
        send_far[...], keep_far[...] = total[2 * (1 - x) + 1 - c].astype(BF), total[2 * (1 - x) + c]
        send[...], keep[...] = total[2 * x + 1 - c].astype(BF), total[2 * x + c]

    @pl.when(pl.program_id(0) == 1)
    def _():
        total[:2] = product(pl.ds(pl.multiple_of(x * 2 * rows, 2 * rows), 2 * rows))
        send[...], keep[...] = total[1 - c].astype(BF), total[c]


def grad_whole(at, left, right):
    d, t = left.shape[1:]
    f = right.shape[3]
    rows, bn = d // 4, 768
    n = pl.cdiv(f, bn)
    far = pl.BlockSpec((rows, bn), lambda w, j, at: (0, jnp.where(w == 0, j, n - 1)))
    same = pl.BlockSpec((None, rows, bn), lambda w, j, at: (w, 0, j))
    return call(
        whole_kernel,
        at,
        (2, n),
        [once((None, d, t), lambda w, j, at, x=x: (x, 0, 0)) for x in range(2)]
        + [pl.BlockSpec((None, None, t, bn), lambda w, j, at, x=x: (x, w, 0, j)) for x in range(2)],
        [far, far, same, same],
        [out((rows, f)), out((rows, f), F32), out((2, rows, f)), out((2, rows, f), F32)],
        (left, left, right, right),
        6 * d * t * f,
        120e6,
        scratch=[pltpu.VMEM((4, rows, bn), F32)],
    )


def tall_kernel(at, *refs, terms, add, keeps):
    operands, rest = refs[: 2 * terms], refs[2 * terms :]
    half = pl.num_programs(0) // 2
    total = 0
    for left, right in zip(operands[::2], operands[1::2], strict=True):
        total = total + dot(left[...], right[...], NN)
    if add:
        total = total + rest[0][...].astype(F32)
    if not keeps:
        rest[-1][...] = total.astype(BF)
        return

    @pl.when(pl.program_id(0) < half)
    def _():
        rest[-2][...] = total.astype(BF)

    @pl.when(pl.program_id(0) >= half)
    def _():
        rest[-1][...] = total


def grad_tall(at, pairs, one, two, got=None, keeps=True, half=2):
    rows, t = pairs[0][0].shape[1:]
    d = pairs[0][1].shape[1]
    bm = rows // half
    in_specs, operands = [], []
    for left, right in pairs:
        in_specs += [
            pl.BlockSpec((None, bm, t), lambda j, at: (jnp.where(j < half, one(at), two(at)), j % half, 0)),
            once(right.shape, lambda j, at: (0, 0)),
        ]
        operands += [left, right]
    if got is not None:
        in_specs.append(pl.BlockSpec((None, bm, d), lambda j, at: (j // half, j % half, 0)))
        operands.append(got)
    if keeps:
        out_specs = [pl.BlockSpec((bm, d), lambda j, at: (jnp.minimum(j, half - 1), 0)), pl.BlockSpec((bm, d), lambda j, at: (jnp.maximum(j - half, 0), 0))]
        shapes = [out((rows, d)), out((rows, d), F32)]
    else:
        out_specs = [pl.BlockSpec((None, bm, d), lambda j, at: (j // half, j % half, 0))]
        shapes = [out((2, rows, d))]
    return call(
        functools.partial(tall_kernel, terms=len(pairs), add=got is not None, keeps=keeps),
        at,
        (2 * half,),
        in_specs,
        out_specs,
        shapes,
        operands,
        4 * rows * t * d * len(pairs),
        60e6,
    )


def squares_of(keep, far):
    g = (keep[...] + far[...].astype(F32)).astype(BF).astype(F32)
    g = jnp.sum((g * g).reshape(-1, 8, g.shape[-1]), 0)
    return sum(g[:, c] for c in chunks(g.shape[1], 128))


def squares_kernel(*refs):
    o = refs[-1]

    @pl.when(pl.program_id(0) == 0)
    def _():
        o[...] = jnp.zeros_like(o)

    o[...] += sum(squares_of(keep, far) for keep, far in zip(refs[:-1:2], refs[1:-1:2], strict=True))


def sum_of_squares(pairs, n):
    specs = []
    for a, _ in pairs:
        br = a.shape[-2] // n
        if a.ndim == 2:
            spec = pl.BlockSpec((br, a.shape[1]), lambda i: (i, 0))
        else:
            spec = pl.BlockSpec((a.shape[0], br, a.shape[2]), lambda i: (0, i, 0))
        specs += [spec, spec]
    return pl.pallas_call(
        squares_kernel,
        grid=(n,),
        in_specs=specs,
        out_specs=pl.BlockSpec((8, 128), lambda i: (0, 0)),
        out_shape=out((8, 128), F32),
        compiler_params=params(),
        cost_estimate=cost(1e9, 4e6 * len(specs)),
        name="squares",
    )(*[a for pair in pairs for a in pair])


UNITS_OF_ROWS = 5


def updated(g, w, m, v):
    m = 0.9 * m + 0.1 * g
    v = 0.95 * v + 0.05 * g * g
    wide = w.astype(F32)
    return (wide - 0.02 * (m * lax.rsqrt(v + 1e-8) + 0.1 * wide)).astype(BF), m, v


def gradient(factor, keep, far):
    return (keep[...] + far[...].astype(F32)).astype(BF).astype(F32) * factor[0]


def adam_kernel(at, factor, keep, far, w, m, v, *rest):
    w_out, m_out, v_out, w_new = rest[-4:]
    w_out[...], m_out[...], v_out[...] = updated(gradient(factor, keep, far), w[...], m[...], v[...])
    w_new[...] = w_out[...]


def adam(at, factor, layer, which, part, keep, far, w, m, v, before):
    rows, cols = keep.shape[1:]
    br = rows // UNITS_OF_ROWS
    low, high = part
    own = pl.BlockSpec((None, br, cols), lambda i, at: (layer, low + i, 0))
    grad = pl.BlockSpec((None, br, cols), lambda i, at: (which, low + i, 0))
    there = pl.BlockSpec((None, br, cols), lambda i, at: (layer, (2 * at[0] + at[1]) * UNITS_OF_ROWS + low + i, 0))
    return call(
        adam_kernel,
        at,
        (high - low,),
        [pl.BlockSpec(memory_space=pltpu.SMEM), grad, grad, there, own, own] + [pl.BlockSpec(memory_space=pl.ANY)] * len(before),
        [pl.BlockSpec((br, cols), lambda i, at: (i, 0)), own, own, there],
        [out((br * (high - low), cols)), out(m.shape, F32), out(v.shape, F32), out(w.shape)],
        [factor, keep, far, w, m, v, *before],
        1e9,
        6e6 * (high - low),
        input_output_aliases={7: 1, 8: 2, 9: 3} if before else {},
    )


def adam_far_kernel(at, factor, keep, far, w, crossed, handed, before, w_out, w_new):
    m, v = jnp.where(at[2] == 0, crossed[...], handed[...]), jnp.where(at[2] == 0, handed[...], crossed[...])
    w_out[...], _, _ = updated(gradient(factor, keep, far), w[...], m, v)
    w_new[...] = w_out[...]


def adam_far(at, factor, layer, keep, far, w, crossed, handed, before):
    rows, cols = keep.shape
    br = rows // UNITS_OF_ROWS
    flat = pl.BlockSpec((br, cols), lambda i, at: (i, 0))
    there = pl.BlockSpec((None, br, cols), lambda i, at: (layer, (2 * (1 - at[0]) + at[1]) * UNITS_OF_ROWS + i, 0))
    return call(
        adam_far_kernel,
        at,
        (UNITS_OF_ROWS,),
        [pl.BlockSpec(memory_space=pltpu.SMEM), flat, flat, there, flat, flat, pl.BlockSpec(memory_space=pl.ANY)],
        [flat, there],
        [out((rows, cols)), out(w.shape)],
        [factor, keep, far, w, crossed, handed, before],
        1e9,
        30e6,
        input_output_aliases={7: 1},
    )


def place_kernel(at, *refs, count):
    for n in range(count):
        pl.when(pl.program_id(0) == n)(functools.partial(lambda n: refs[-1].__setitem__(..., refs[n][...]), n))


def place(at, layer, part, blocks, wheres, before):
    low, high = part
    k = high - low
    cols = blocks[0].shape[1]
    br = blocks[0].shape[0] // k

    def spec(n):
        return pl.BlockSpec((br, cols), lambda i, j, at: (jnp.where(i < n, 0, jnp.where(i > n, k - 1, j)), 0))

    def where(i, j, at):
        b = wheres[0](at)
        for n, w in enumerate(wheres[1:], 1):
            b = jnp.where(i == n, w(at), b)
        return layer, b * UNITS_OF_ROWS + low + j, 0

    return call(
        functools.partial(place_kernel, count=len(blocks)),
        at,
        (len(blocks), k),
        [spec(n) for n in range(len(blocks))] + [pl.BlockSpec(memory_space=pl.ANY)],
        pl.BlockSpec((None, br, cols), where),
        out(before.shape),
        [*blocks, before],
        1e9,
        1.2e6 * k * len(blocks),
        input_output_aliases={1 + len(blocks): 0},
    )


def after(value, *others):
    return lax.optimization_barrier((value, *others))[0]


ACROSS = [(0, 2), (2, 0), (1, 3), (3, 1)]
SIBLING = [(0, 1), (1, 0), (2, 3), (3, 2)]


def across(a):
    return lax.ppermute(a, "dp", ACROSS)


def sibling(a):
    return lax.ppermute(a, "dp", SIBLING)


def step(x, dy, w_gate, w_up, w_down, m_gate, m_up, m_down, v_gate, v_up, v_down):
    dp = lax.axis_index("dp")
    at = jnp.stack([dp // 2, dp % 2, lax.axis_index("rep")]).astype(jnp.int32)
    x, dy = x[0], dy[0]
    d, f = w_gate.shape[1:]

    def blocks(a):
        return a.reshape(4, a.shape[0] // 4, a.shape[1])

    dy_far = across(dy)
    a1, hid1, s1, q1, h1, half = first(at, x, w_gate, w_up, w_down, m_gate, v_gate)
    h1_far = across(h1)
    crossed = across(half)
    handed = lax.ppermute(crossed, "rep", [(0, 1), (1, 0)])
    a2, dgu2, hid2, d1 = second(at, h1, dy, w_gate, w_up, w_down)

    dgu1, theirs = hidden_back(at, w_down, d1, s1, q1, blocks(a1))
    got_wide = sibling(theirs)
    pairs = [(blocks(hid1), after(d1, theirs))]
    (theirs,) = grad_tall(at, pairs, on(False, False), on(True, False), keeps=False)
    got_down = sibling(theirs)
    got_wide = after(got_wide, theirs)
    send, keep_wide1 = grad_wide(at, blocks(a1), dgu1, on(False, True), on(True, True), got_wide)
    far_wide1 = across(send)
    got_down = after(got_down, keep_wide1)
    send, keep_down1 = grad_tall(at, pairs, on(False, True), on(True, True), got_down)
    far_down1 = across(send)

    h1_far = after(h1_far, keep_down1)
    a2, dgu2, hid2f = second(at, h1_far, dy_far, w_gate, w_up, w_down, [a2, dgu2])
    send, keep_other, send_wide, keep_wide2 = grad_whole(at, a2, dgu2)
    far_other, far_wide2 = sibling(send), sibling(send_wide)
    pairs = [(blocks(hid2), dy), (blocks(after(hid2f, keep_wide2)), dy_far)]
    send, keep_down2 = grad_tall(at, pairs, on(True, False), on(True, True))
    far_down2 = sibling(send)

    most = sum_of_squares([(keep_wide2, far_wide2), (keep_down1, far_down1), (keep_wide1, far_wide1)], 10)
    far_down2 = after(far_down2, most)
    squares = jnp.sum(most + sum_of_squares([(keep_down2, far_down2)], 5))
    squares = lax.psum(squares, "dp")
    factor = jnp.minimum(1.0, 0.5 * lax.rsqrt(squares / (6 * d * f) + 1e-30)).reshape(1)

    weights = {"gate": (w_gate, m_gate, v_gate), "up": (w_up, m_up, v_up), "down": (w_down, m_down, v_down)}
    grads = {
        "gate1": (1, 0, keep_wide2, far_wide2),
        "up1": (1, 1, keep_wide2, far_wide2),
        "down1": (1, 0, keep_down2[None], far_down2[None]),
        "gate0": (0, 0, keep_wide1, far_wide1),
        "up0": (0, 1, keep_wide1, far_wide1),
        "down0": (0, 0, keep_down1[None], far_down1[None]),
    }
    new = dict.fromkeys(weights, ())

    def update(which, part):
        name = which[:-1]
        own, *new[name] = adam(at, factor, *grads[which][:2], part, *grads[which][2:], *weights[name], new[name])
        return own

    def put(which, part, *blocks):
        name = which[:-1]
        *moments, w = new[name]
        where, arrays = zip(*blocks, strict=True)
        new[name] = [*moments, place(at, grads[which][0], part, arrays, where, w)]

    whole = (0, UNITS_OF_ROWS)
    own = update("gate1", whole)
    *moments, w = new["gate"]
    away, w = adam_far(at, factor, 1, keep_other, far_other, w_gate, crossed, handed, w)
    new["gate"] = [*moments, w]
    put("gate1", whole, (on(True, False), sibling(own)), (on(False, False), sibling(away)))

    parts = []
    for n, (which, part) in enumerate(PARTS):
        own = update(which, part)
        parts.append((across(own), sibling(own)))
        if n in LATER:
            continue
        for n, (away, beside) in enumerate(parts):
            if away is not None:
                which, part = PARTS[n]
                put(which, part, (on(True, False), beside))
                put(which, part, (on(False, True), away))
                put(which, part, (on(False, False), sibling(away)))
                parts[n] = None, None
    return tuple(new[name][i] for i in (2, 0, 1) for name in weights)


PARTS = [("up1", (0, 1)), ("up1", (1, 5)), ("down1", (0, 5)), ("gate0", (0, 5)), ("up0", (0, 5)), ("down0", (0, 3)), ("down0", (3, 5))]
LATER = (0, 5)


def solution(mesh):
    tokens, whole, rows = P(("rep", "dp")), P(), P(None, "dp")

    return jax.shard_map(
        step,
        mesh=mesh,
        in_specs=(tokens,) * 2 + (whole,) * 3 + (rows,) * 6,
        out_specs=(P("rep"),) * 3 + (P("rep", "dp"),) * 6,
        check_vma=False,
    )
```

time: 1890 us -> 1390 us (0.74)
  Pallas kernels: 0 us -> 829 us
  waiting for transfers between devices: 1070 us -> 512 us
  matrix products: 533 us -> 0 us
  other arithmetic: 182 us -> 1.87 us
  local copies, waits for them, and re-layouts: 68.6 us -> 2.6 us
  starting transfers between devices: 0.84 us -> 20.3 us
    pallas_call x0 -> x42, Pallas kernels: none -> 829 us  [the longest x38 567 us: call(): pl.pallas_call(kernel, grid_spec=pltpu.PrefetchScalarGridSpec(num_scalar_...]
    unnamed x15 -> x0, waiting for transfers between devices: 700 us -> none
    dot_general x15 -> x0, matrix products: 533 us -> none  [the longest x5 182 us: layer(): gate = jnp.dot(a, w['w_gate'], preferred_element_type=jnp.float32)]
    ppermute x0 -> x34, waiting for transfers between devices: none -> 512 us  [the longest x12 502 us: across(): return lax.ppermute(a, 'dp', ACROSS)]
    reshape x3 -> x0, waiting for transfers between devices: 372 us -> none  [step(): t.reshape(-1, *t.shape[2:])]
    unnamed x6 -> x0, other arithmetic: 78.9 us -> none
    reshape x3 -> x0, other arithmetic: 70.9 us -> none  [step(): t.reshape(-1, *t.shape[2:])]
    unnamed x53 -> x8, local copies, waits for them, and re-layouts: 68 us -> 2.6 us
  transfers between devices with their start and end apart: 9 -> 34, of which waited for: 8 -> 7; matrix products, arithmetic and copies ran while one was open for 17% -> 0% of each run, Pallas kernels for 0% -> 38%
where the time goes in v2:
time: 1390 us; the launch traced here: 1370 us
  Pallas kernels  829 us (60%)
  waiting for transfers between devices  512 us (37%)
  starting transfers between devices  20.3 us (1%)
    pallas_call x38, Pallas kernels, call(): pl.pallas_call(kernel, grid_spec=pltpu.PrefetchScalarGridSpec(num_scalar_...  567 us
    ppermute x12, waiting for transfers between devices, across(): return lax.ppermute(a, 'dp', ACROSS)  502 us
    pallas_call x2, Pallas kernels, second(): pl.pallas_call(functools.partial(second_kernel if far else second_back_ke...  238 us
  transfers between devices with their start and end apart: 34, of which 7 were waited for; matrix products, arithmetic and copies ran while one was open for 0% of the time, Pallas kernels for 38%

profile of v2, /device:TPU:0, one launch (start us, length us, event | category | flops | bytes accessed | tf_op | source)
XLA Modules:
  0.0 1374.5 jit_solution(1721824863451409175)
XLA Ops:
  1.2 95.5 %shard_map.178 = (bf16[1280,2048]{1,0:T(8,128)(2,1)}, bf16[4480,2048]{1,0:T(8,128)(2,1)}, f32[2048,4480]{1,0:T(8,128)}, f32[2048,4480]{1,0:T(8,128)}, bf16[2048,1280]{1,0:T(8,128)(2,1)}, /*index=5*/f32[320,4480]{1,0:T(8,128)}) custom-call(s32[3]{0:T(128)} %pad_add_fusion.at, bf16[2048,1280]{1,0:T(8,128)(2,1)} %bitcast.19, bf16[2,1280,4480]{2,1,0:T(8,128)(2,1)} %w.13, ...), custom_call_target="tpu_custom_call" | custom-call | flops 70464307200 | bytes 190000000 | tf_op jit(solution)/shard_map/pallas_call | solution.py:38
  96.7 146.5 %second_back.1 = (bf16[2,1280,2048]{2,1,0:T(8,128)(2,1)}, bf16[2,2,2048,4480]{3,2,1,0:T(8,128)(2,1)}, bf16[4480,2048]{1,0:T(8,128)(2,1)}, bf16[2048,1280]{1,0:T(8,128)(2,1)}) custom-call(s32[3]{0:T(128)} %pad_add_fusion.at, bf16[2048,1280]{1,0:T(8,128)(2,1)} %get-tuple-element.74.h, bf16[2048,1280]{1,0:T(8,128)(2,1)} %bitcast.20, bf16[2,1280,4480]{2,1,0:T(8,128)(2,1)} %w.13, ...), custom_call_target="tpu_custom_call" | custom-call | flops 117440512000 | bytes 130000000 | tf_op jit(solution)/shard_map/second_back/pallas_call | solution.py:211
  243.1 63.9 %shard_map.179 = (bf16[2,2048,4480]{2,1,0:T(8,128)(2,1)}, bf16[2,2,320,4480]{3,2,1,0:T(8,128)(2,1)}) custom-call(s32[3]{0:T(128)} %pad_add_fusion.at, bf16[2,4480,1280]{2,1,0:T(8,128)(2,1)} %w.19, bf16[2048,1280]{1,0:T(8,128)(2,1)} %get-tuple-element.81.d.refs_1_, f32[2048,4480]{1,0:T(8,128)} %get-tuple-element.77.s, f32[2048,4480]{1,0:T(8,128)} %get-tuple-element.78.q, ...), custom_call_target="tpu_custom_call" | custom-call | flops 46976204800 | bytes 160000000 | tf_op jit(solution)/shard_map/pallas_call | solution.py:38
  307.8 17.6 %shard_map.180 = bf16[2,1120,1280]{2,1,0:T(8,128)(2,1)} custom-call(s32[3]{0:T(128)} %pad_add_fusion.at, bf16[4,1120,2048]{2,1,0:T(8,128)(2,1)} %bitcast.24, bf16[2048,1280]{1,0:T(8,128)(2,1)} %get-tuple-element.81.d.refs_1_), custom_call_target="tpu_custom_call" | custom-call | flops 11744051200 | bytes 60000000 | tf_op jit(solution)/shard_map/pallas_call | solution.py:38
  330.5 32.2 %shard_map.181 = (bf16[2,320,4480]{2,1,0:T(8,128)(2,1)}, f32[2,320,4480]{2,1,0:T(8,128)}) custom-call(s32[3]{0:T(128)} %pad_add_fusion.at, bf16[4,320,2048]{2,1,0:T(8,128)(2,1)} %bitcast.29, bf16[4,320,2048]{2,1,0:T(8,128)(2,1)} %bitcast.30, bf16[2,2048,4480]{2,1,0:T(8,128)(2,1)} %get-tuple-element.82.right, bf16[2,2,320,4480]{3,2,1,0:T(8,128)(2,1)} %collective-permute-done.2.got), custom_call_target="tpu_custom_call" | custom-call | flops 23488102400 | bytes 60000000 | tf_op jit(solution)/shard_map/pallas_call | solution.py:38
  362.7 19.7 %shard_map.182 = (bf16[1120,1280]{1,0:T(8,128)(2,1)}, f32[1120,1280]{1,0:T(8,128)}) custom-call(s32[3]{0:T(128)} %pad_add_fusion.at, bf16[4,1120,2048]{2,1,0:T(8,128)(2,1)} %bitcast.25, bf16[2048,1280]{1,0:T(8,128)(2,1)} %get-tuple-element.81.d.refs_1_, bf16[2,1120,1280]{2,1,0:T(8,128)(2,1)} %collective-permute-done.1.refs_2_), custom_call_target="tpu_custom_call" | custom-call | flops 11744051200 | bytes 60000000 | tf_op jit(solution)/shard_map/pallas_call | solution.py:38
  382.4 60.3 %collective-permute-done.h = bf16[2048,1280]{1,0:T(8,128)(2,1)} collective-permute-done((bf16[2048,1280]{1,0:T(8,128)(2,1)}, bf16[2048,1280]{1,0:T(8,128)(2,1)}, u32[]{:S(2)}, u32[]{:S(2)}) %collective-permute-start) | collective-permute-done | bytes 5242912 | tf_op jit(solution)/shard_map/ppermute | solution.py:536
  442.7 112.4 %collective-permute-done.3.dy.refs_3_ = bf16[2048,1280]{1,0:T(8,128)(2,1)} collective-permute-done((bf16[2048,1280]{1,0:T(8,128)(2,1)}, bf16[2048,1280]{1,0:T(8,128)(2,1)}, u32[]{:S(2)}, u32[]{:S(2)}) %collective-permute-start.3) | collective-permute-done | bytes 5242912 | tf_op jit(solution)/shard_map/ppermute | solution.py:536
  555.0 91.9 %second.1 = (bf16[2,1280,2048]{2,1,0:T(8,128)(2,1)}, bf16[2,2,2048,4480]{3,2,1,0:T(8,128)(2,1)}, bf16[4480,2048]{1,0:T(8,128)(2,1)}) custom-call(s32[3]{0:T(128)} %pad_add_fusion.at, bf16[2048,1280]{1,0:T(8,128)(2,1)} %collective-permute-done.h, bf16[2048,1280]{1,0:T(8,128)(2,1)} %collective-permute-done.3.dy.refs_3_, ...), custom_call_target="tpu_custom_call", output_to_operand_aliasing={{0}: (6, {}), {1}: (7, {})} | custom-call | flops 70464307200 | bytes 130000000 | tf_op jit(solution)/shard_map/second/pallas_call | solution.py:211
  647.0 86.5 %shard_map.183 = (bf16[320,4480]{1,0:T(8,128)(2,1)}, f32[320,4480]{1,0:T(8,128)}, bf16[2,320,4480]{2,1,0:T(8,128)(2,1)}, f32[2,320,4480]{2,1,0:T(8,128)}) custom-call(s32[3]{0:T(128)} %pad_add_fusion.at, bf16[2,1280,2048]{2,1,0:T(8,128)(2,1)} %get-tuple-element.90.left0.left1, bf16[2,1280,2048]{2,1,0:T(8,128)(2,1)} %get-tuple-element.90.left0.left1, ...), custom_call_target="tpu_custom_call" | custom-call | flops 70464307200 | bytes 120000000 | tf_op jit(solution)/shard_map/pallas_call | solution.py:38
  737.6 33.4 %shard_map.184 = (bf16[1120,1280]{1,0:T(8,128)(2,1)}, f32[1120,1280]{1,0:T(8,128)}) custom-call(s32[3]{0:T(128)} %pad_add_fusion.at, bf16[4,1120,2048]{2,1,0:T(8,128)(2,1)} %bitcast.23, bf16[2048,1280]{1,0:T(8,128)(2,1)} %bitcast.22, bf16[4,1120,2048]{2,1,0:T(8,128)(2,1)} %bitcast.26, bf16[2048,1280]{1,0:T(8,128)(2,1)} %collective-permute-done.3.dy.refs_3_), custom_call_target="tpu_custom_call" | custom-call | flops 23488102400 | bytes 60000000 | tf_op jit(solution)/shard_map/pallas_call | solution.py:38
  771.0 150.5 %collective-permute-done.5.refs_3_ = bf16[1120,1280]{1,0:T(8,128)(2,1)S(1)} collective-permute-done((bf16[1120,1280]{1,0:T(8,128)(2,1)}, bf16[1120,1280]{1,0:T(8,128)(2,1)S(1)}, u32[]{:S(2)}, u32[]{:S(2)}) %collective-permute-start.5) | collective-permute-done | bytes 2867232 | tf_op jit(solution)/shard_map/ppermute | solution.py:536
  923.0 17.6 %squares.2 = f32[8,128]{1,0:T(8,128)} custom-call(f32[2,320,4480]{2,1,0:T(8,128)} %get-tuple-element.92.refs_0_.keep, bf16[2,320,4480]{2,1,0:T(8,128)(2,1)} %collective-permute-done.4.refs_1_.far, f32[1120,1280]{1,0:T(8,128)} %get-tuple-element.86.refs_2_, bf16[1120,1280]{1,0:T(8,128)(2,1)} %copy-done, f32[2,320,4480]{2,1,0:T(8,128)} %get-tuple-element.84.refs_4_.keep, ...), custom_call_target="tpu_custom_call" | custom-call | flops 1000000000 | bytes 24000000 | tf_op jit(solution)/shard_map/squares/pallas_call | solution.py:415
  940.6 5.9 squares.3
  947.9 7.6 psum.7
  961.7 12.7 shard_map.193
  975.2 16.5 %shard_map.204 = (bf16[1120,1280]{1,0:T(8,128)(2,1)}, f32[2,1120,1280]{2,1,0:T(8,128)}, f32[2,1120,1280]{2,1,0:T(8,128)}, bf16[2,4480,1280]{2,1,0:T(8,128)(2,1)}) custom-call(s32[3]{0:T(128)} %pad_add_fusion.at, f32[1]{0:T(128)} %bitcast.9.factor, f32[1,1120,1280]{2,1,0:T(8,128)} %bitcast.18, bf16[1,1120,1280]{2,1,0:T(8,128)(2,1)} %bitcast.13.far, ...), custom_call_target="tpu_custom_call" | custom-call | flops 1000000000 | bytes 30000000 | tf_op jit(solution)/shard_map/pallas_call | solution.py:38
  992.9 16.5 %shard_map.185 = (bf16[320,4480]{1,0:T(8,128)(2,1)}, f32[2,320,4480]{2,1,0:T(8,128)}, f32[2,320,4480]{2,1,0:T(8,128)}, bf16[2,1280,4480]{2,1,0:T(8,128)(2,1)}) custom-call(s32[3]{0:T(128)} %pad_add_fusion.at, f32[1]{0:T(128)} %bitcast.9.factor, f32[2,320,4480]{2,1,0:T(8,128)} %get-tuple-element.92.refs_0_.keep, ...), custom_call_target="tpu_custom_call" | custom-call | flops 1000000000 | bytes 30000000 | tf_op jit(solution)/shard_map/pallas_call | solution.py:38
  1009.4 14.7 %shard_map.186 = (bf16[320,4480]{1,0:T(8,128)(2,1)}, bf16[2,1280,4480]{2,1,0:T(8,128)(2,1)}) custom-call(s32[3]{0:T(128)} %pad_add_fusion.at, f32[1]{0:T(128)} %bitcast.9.factor, f32[320,4480]{1,0:T(8,128)} %get-tuple-element.105.keep, bf16[320,4480]{1,0:T(8,128)(2,1)} %collective-permute-done.9.far, ...), custom_call_target="tpu_custom_call", output_to_operand_aliasing={{1}: (7, {})} | custom-call | flops 1000000000 | bytes 30000000 | tf_op jit(solution)/shard_map/pallas_call | solution.py:38
  1024.7 9.9 collective-permute-done.21.refs_0_
  1035.4 63.7 %collective-permute-done.19.refs_0_ = bf16[64,4480]{1,0:T(8,128)(2,1)} collective-permute-done((bf16[64,4480]{1,0:T(8,128)(2,1)}, bf16[64,4480]{1,0:T(8,128)(2,1)}, u32[]{:S(2)}, u32[]{:S(2)}) %collective-permute-start.19) | collective-permute-done | bytes 573472 | tf_op jit(solution)/shard_map/ppermute | solution.py:536
  1101.3 9.2 shard_map.187.rest_2_
  1110.5 16.5 %shard_map.188 = (bf16[320,4480]{1,0:T(8,128)(2,1)}, f32[2,320,4480]{2,1,0:T(8,128)}, f32[2,320,4480]{2,1,0:T(8,128)}, bf16[2,1280,4480]{2,1,0:T(8,128)(2,1)}) custom-call(s32[3]{0:T(128)} %pad_add_fusion.at, f32[1]{0:T(128)} %bitcast.9.factor, ...), custom_call_target="tpu_custom_call", output_to_operand_aliasing={{1}: (7, {}), {2}: (8, {}), {3}: (9, {})} | custom-call | flops 1000000000 | bytes 30000000 | tf_op jit(solution)/shard_map/pallas_call | solution.py:38
  1150.5 16.7 %shard_map.200 = (bf16[320,4480]{1,0:T(8,128)(2,1)}, f32[2,320,4480]{2,1,0:T(8,128)}, f32[2,320,4480]{2,1,0:T(8,128)}, bf16[2,1280,4480]{2,1,0:T(8,128)(2,1)}) custom-call(s32[3]{0:T(128)} %pad_add_fusion.at, f32[1]{0:T(128)} %bitcast.9.factor, ...), custom_call_target="tpu_custom_call", output_to_operand_aliasing={{1}: (7, {}), {2}: (8, {}), {3}: (9, {})} | custom-call | flops 1000000000 | bytes 30000000 | tf_op jit(solution)/shard_map/pallas_call | solution.py:38
  1184.1 11.0 shard_map.208
  1195.1 7.2 shard_map.209
  1204.6 79.4 %collective-permute-done.28.refs_0_ = bf16[448,1280]{1,0:T(8,128)(2,1)} collective-permute-done((bf16[448,1280]{1,0:T(8,128)(2,1)}, bf16[448,1280]{1,0:T(8,128)(2,1)}, u32[]{:S(2)}, u32[]{:S(2)}) %collective-permute-start.28) | collective-permute-done | bytes 1146912 | tf_op jit(solution)/shard_map/ppermute | solution.py:536
  1284.5 35.4 %collective-permute-done.31.refs_0_ = bf16[672,1280]{1,0:T(8,128)(2,1)} collective-permute-done((bf16[672,1280]{1,0:T(8,128)(2,1)}, bf16[672,1280]{1,0:T(8,128)(2,1)}, u32[]{:S(2)}, u32[]{:S(2)}) %collective-permute-start.31) | collective-permute-done | bytes 1720352 | tf_op jit(solution)/shard_map/ppermute | solution.py:536
  1320.5 5.5 shard_map.189.refs_1_
  1326.0 5.5 shard_map.190.refs_1_
  1350.8 5.5 shard_map.191
  1368.8 5.5 shard_map.203
  (89 shorter events, 99.9 us)
Async XLA Ops:
  325.4 37.2 %collective-permute-start.1 = (bf16[2,1120,1280]{2,1,0:T(8,128)(2,1)}, bf16[2,1120,1280]{2,1,0:T(8,128)(2,1)}, u32[]{:S(2)}, u32[]{:S(2)}) collective-permute-start(bf16[2,1120,1280]{2,1,0:T(8,128)(2,1)} %shard_map.180), channel_id=1, source_target_pairs={{0,1},{1,0},{2,3},{3,2},{4,5},{5,4},{6,7},{7,6}} | collective-permute-start | bytes 17203208 | tf_op jit(solution)/shard_map/ppermute | solution.py:540
  325.4 117.3 %collective-permute-start = (bf16[2048,1280]{1,0:T(8,128)(2,1)}, bf16[2048,1280]{1,0:T(8,128)(2,1)}, u32[]{:S(2)}, u32[]{:S(2)}) collective-permute-start(bf16[2048,1280]{1,0:T(8,128)(2,1)} %get-tuple-element.74.h), channel_id=1, source_target_pairs={{0,2},{2,0},{1,3},{3,1},{4,6},{6,4},{5,7},{7,5}} | collective-permute-start | bytes 15728648 | tf_op jit(solution)/shard_map/ppermute | solution.py:536
  328.5 226.6 %collective-permute-start.3 = (bf16[2048,1280]{1,0:T(8,128)(2,1)}, bf16[2048,1280]{1,0:T(8,128)(2,1)}, u32[]{:S(2)}, u32[]{:S(2)}) collective-permute-start(bf16[2048,1280]{1,0:T(8,128)(2,1)} %bitcast.21), channel_id=1, source_target_pairs={{0,2},{2,0},{1,3},{3,1},{4,6},{6,4},{5,7},{7,5}} | collective-permute-start | bytes 15728648 | tf_op jit(solution)/shard_map/ppermute | solution.py:536
  328.5 407.1 %collective-permute-start.10 = (f32[320,4480]{1,0:T(8,128)}, f32[320,4480]{1,0:T(8,128)}, u32[]{:S(2)}, u32[]{:S(2)}) collective-permute-start(f32[320,4480]{1,0:T(8,128)} %get-tuple-element.107), channel_id=1, source_target_pairs={{0,2},{2,0},{1,3},{3,1},{4,6},{6,4},{5,7},{7,5}} | collective-permute-start | bytes 17203208 | tf_op jit(solution)/shard_map/ppermute | solution.py:536
  733.5 187.9 %collective-permute-start.4 = (bf16[2,320,4480]{2,1,0:T(8,128)(2,1)}, bf16[2,320,4480]{2,1,0:T(8,128)(2,1)}, u32[]{:S(2)}, u32[]{:S(2)}) collective-permute-start(bf16[2,320,4480]{2,1,0:T(8,128)(2,1)} %get-tuple-element.93), channel_id=1, source_target_pairs={{0,1},{1,0},{2,3},{3,2},{4,5},{5,4},{6,7},{7,6}} | collective-permute-start | bytes 17203208 | tf_op jit(solution)/shard_map/ppermute | solution.py:540
  733.5 187.9 %collective-permute-start.6 = (bf16[2,320,4480]{2,1,0:T(8,128)(2,1)}, bf16[2,320,4480]{2,1,0:T(8,128)(2,1)}, u32[]{:S(2)}, u32[]{:S(2)}) collective-permute-start(bf16[2,320,4480]{2,1,0:T(8,128)(2,1)} %get-tuple-element.95), channel_id=1, source_target_pairs={{0,2},{2,0},{1,3},{3,1},{4,6},{6,4},{5,7},{7,5}} | collective-permute-start | bytes 17203208 | tf_op jit(solution)/shard_map/ppermute | solution.py:536
  735.6 185.9 %collective-permute-start.5 = (bf16[1120,1280]{1,0:T(8,128)(2,1)}, bf16[1120,1280]{1,0:T(8,128)(2,1)S(1)}, u32[]{:S(2)}, u32[]{:S(2)}) collective-permute-start(bf16[1120,1280]{1,0:T(8,128)(2,1)} %get-tuple-element.94), channel_id=1, source_target_pairs={{0,2},{2,0},{1,3},{3,1},{4,6},{6,4},{5,7},{7,5}} | collective-permute-start | bytes 8601608 | tf_op jit(solution)/shard_map/ppermute | solution.py:536
  735.6 273.8 %collective-permute-start.11 = (f32[320,4480]{1,0:T(8,128)}, f32[320,4480]{1,0:T(8,128)}, u32[]{:S(2)}, u32[]{:S(2)}) collective-permute-start(f32[320,4480]{1,0:T(8,128)} %collective-permute-done.10.crossed), channel_id=1, source_target_pairs={{0,4},{4,0},{1,5},{5,1},{2,6},{6,2},{3,7},{7,3}} | collective-permute-start | bytes 17203208 | tf_op jit(solution)/shard_map/ppermute | solution.py:556
  771.0 169.7 %collective-permute-start.7 = (bf16[1120,1280]{1,0:T(8,128)(2,1)}, bf16[1120,1280]{1,0:T(8,128)(2,1)}, u32[]{:S(2)}, u32[]{:S(2)}) collective-permute-start(bf16[1120,1280]{1,0:T(8,128)(2,1)} %get-tuple-element.100), channel_id=1, source_target_pairs={{0,1},{1,0},{2,3},{3,2},{4,5},{5,4},{6,7},{7,6}} | collective-permute-start | bytes 8601608 | tf_op jit(solution)/shard_map/ppermute | solution.py:540
  921.4 88.0 %collective-permute-start.9 = (bf16[320,4480]{1,0:T(8,128)(2,1)}, bf16[320,4480]{1,0:T(8,128)(2,1)}, u32[]{:S(2)}, u32[]{:S(2)}) collective-permute-start(bf16[320,4480]{1,0:T(8,128)(2,1)} %get-tuple-element.106), channel_id=1, source_target_pairs={{0,1},{1,0},{2,3},{3,2},{4,5},{5,4},{6,7},{7,6}} | collective-permute-start | bytes 8601608 | tf_op jit(solution)/shard_map/ppermute | solution.py:540
  974.4 124.8 %collective-permute-start.16 = (bf16[256,4480]{1,0:T(8,128)(2,1)}, bf16[256,4480]{1,0:T(8,128)(2,1)}, u32[]{:S(2)}, u32[]{:S(2)}) collective-permute-start(bf16[256,4480]{1,0:T(8,128)(2,1)} %get-tuple-element.118), channel_id=1, source_target_pairs={{0,2},{2,0},{1,3},{3,1},{4,6},{6,4},{5,7},{7,5}} | collective-permute-start | bytes 6881288 | tf_op jit(solution)/shard_map/ppermute | solution.py:536
  991.7 107.9 %collective-permute-start.25 = (bf16[1120,1280]{1,0:T(8,128)(2,1)}, bf16[1120,1280]{1,0:T(8,128)(2,1)}, u32[]{:S(2)}, u32[]{:S(2)}) collective-permute-start(bf16[1120,1280]{1,0:T(8,128)(2,1)} %get-tuple-element.125), channel_id=1, source_target_pairs={{0,2},{2,0},{1,3},{3,1},{4,6},{6,4},{5,7},{7,5}} | collective-permute-start | bytes 8601608 | tf_op jit(solution)/shard_map/ppermute | solution.py:536
  1024.2 75.5 %collective-permute-start.12 = (bf16[320,4480]{1,0:T(8,128)(2,1)}, bf16[320,4480]{1,0:T(8,128)(2,1)S(1)}, u32[]{:S(2)}, u32[]{:S(2)}) collective-permute-start(bf16[320,4480]{1,0:T(8,128)(2,1)} %get-tuple-element.109), channel_id=1, source_target_pairs={{0,1},{1,0},{2,3},{3,2},{4,5},{5,4},{6,7},{7,6}} | collective-permute-start | bytes 8601608 | tf_op jit(solution)/shard_map/ppermute | solution.py:540
  1024.2 76.1 %collective-permute-start.8 = (bf16[320,4480]{1,0:T(8,128)(2,1)}, bf16[320,4480]{1,0:T(8,128)(2,1)}, u32[]{:S(2)}, u32[]{:S(2)}) collective-permute-start(bf16[320,4480]{1,0:T(8,128)(2,1)} %get-tuple-element.104), channel_id=1, source_target_pairs={{0,1},{1,0},{2,3},{3,2},{4,5},{5,4},{6,7},{7,6}} | collective-permute-start | bytes 8601608 | tf_op jit(solution)/shard_map/ppermute | solution.py:540
  1034.6 64.6 %collective-permute-start.19 = (bf16[64,4480]{1,0:T(8,128)(2,1)}, bf16[64,4480]{1,0:T(8,128)(2,1)}, u32[]{:S(2)}, u32[]{:S(2)}) collective-permute-start(bf16[64,4480]{1,0:T(8,128)(2,1)} %get-tuple-element.119), channel_id=1, source_target_pairs={{0,2},{2,0},{1,3},{3,1},{4,6},{6,4},{5,7},{7,5}} | collective-permute-start | bytes 1720328 | tf_op jit(solution)/shard_map/ppermute | solution.py:536
  1099.2 33.5 %collective-permute-start.18 = (bf16[256,4480]{1,0:T(8,128)(2,1)}, bf16[256,4480]{1,0:T(8,128)(2,1)}, u32[]{:S(2)}, u32[]{:S(2)}) collective-permute-start(bf16[256,4480]{1,0:T(8,128)(2,1)} %get-tuple-element.118), channel_id=1, source_target_pairs={{0,1},{1,0},{2,3},{3,2},{4,5},{5,4},{6,7},{7,6}} | collective-permute-start | bytes 6881288 | tf_op jit(solution)/shard_map/ppermute | solution.py:540
  1099.2 46.8 %collective-permute-start.17 = (bf16[256,4480]{1,0:T(8,128)(2,1)}, bf16[256,4480]{1,0:T(8,128)(2,1)}, u32[]{:S(2)}, u32[]{:S(2)}) collective-permute-start(bf16[256,4480]{1,0:T(8,128)(2,1)} %collective-permute-done.16.refs_0_), channel_id=1, source_target_pairs={{0,1},{1,0},{2,3},{3,2},{4,5},{5,4},{6,7},{7,6}} | collective-permute-start | bytes 6881288 | tf_op jit(solution)/shard_map/ppermute | solution.py:540
  1099.7 67.9 %collective-permute-start.27 = (bf16[1120,1280]{1,0:T(8,128)(2,1)}, bf16[1120,1280]{1,0:T(8,128)(2,1)}, u32[]{:S(2)}, u32[]{:S(2)}) collective-permute-start(bf16[1120,1280]{1,0:T(8,128)(2,1)} %get-tuple-element.125), channel_id=1, source_target_pairs={{0,1},{1,0},{2,3},{3,2},{4,5},{5,4},{6,7},{7,6}} | collective-permute-start | bytes 8601608 | tf_op jit(solution)/shard_map/ppermute | solution.py:540
  1099.7 78.9 %collective-permute-start.26 = (bf16[1120,1280]{1,0:T(8,128)(2,1)}, bf16[1120,1280]{1,0:T(8,128)(2,1)}, u32[]{:S(2)}, u32[]{:S(2)}) collective-permute-start(bf16[1120,1280]{1,0:T(8,128)(2,1)} %collective-permute-done.25.refs_0_), channel_id=1, source_target_pairs={{0,1},{1,0},{2,3},{3,2},{4,5},{5,4},{6,7},{7,6}} | collective-permute-start | bytes 8601608 | tf_op jit(solution)/shard_map/ppermute | solution.py:540
  1100.2 26.8 %collective-permute-start.20 = (bf16[64,4480]{1,0:T(8,128)(2,1)}, bf16[64,4480]{1,0:T(8,128)(2,1)}, u32[]{:S(2)}, u32[]{:S(2)}) collective-permute-start(bf16[64,4480]{1,0:T(8,128)(2,1)} %collective-permute-done.19.refs_0_), channel_id=1, source_target_pairs={{0,1},{1,0},{2,3},{3,2},{4,5},{5,4},{6,7},{7,6}} | collective-permute-start | bytes 1720328 | tf_op jit(solution)/shard_map/ppermute | solution.py:540
  1127.0 76.9 %collective-permute-start.15 = (bf16[320,4480]{1,0:T(8,128)(2,1)}, bf16[320,4480]{1,0:T(8,128)(2,1)}, u32[]{:S(2)}, u32[]{:S(2)}) collective-permute-start(bf16[320,4480]{1,0:T(8,128)(2,1)} %get-tuple-element.111), channel_id=1, source_target_pairs={{0,1},{1,0},{2,3},{3,2},{4,5},{5,4},{6,7},{7,6}} | collective-permute-start | bytes 8601608 | tf_op jit(solution)/shard_map/ppermute | solution.py:540
  1132.7 71.7 %collective-permute-start.13 = (bf16[320,4480]{1,0:T(8,128)(2,1)}, bf16[320,4480]{1,0:T(8,128)(2,1)}, u32[]{:S(2)}, u32[]{:S(2)}) collective-permute-start(bf16[320,4480]{1,0:T(8,128)(2,1)} %get-tuple-element.111), channel_id=1, source_target_pairs={{0,2},{2,0},{1,3},{3,1},{4,6},{6,4},{5,7},{7,5}} | collective-permute-start | bytes 8601608 | tf_op jit(solution)/shard_map/ppermute | solution.py:536
  1167.2 116.9 %collective-permute-start.22 = (bf16[320,4480]{1,0:T(8,128)(2,1)}, bf16[320,4480]{1,0:T(8,128)(2,1)S(1)}, u32[]{:S(2)}, u32[]{:S(2)}) collective-permute-start(bf16[320,4480]{1,0:T(8,128)(2,1)} %get-tuple-element.121), channel_id=1, source_target_pairs={{0,2},{2,0},{1,3},{3,1},{4,6},{6,4},{5,7},{7,5}} | collective-permute-start | bytes 8601608 | tf_op jit(solution)/shard_map/ppermute | solution.py:536
  1202.3 81.7 %collective-permute-start.28 = (bf16[448,1280]{1,0:T(8,128)(2,1)}, bf16[448,1280]{1,0:T(8,128)(2,1)}, u32[]{:S(2)}, u32[]{:S(2)}) collective-permute-start(bf16[448,1280]{1,0:T(8,128)(2,1)} %get-tuple-element.130), channel_id=1, source_target_pairs={{0,2},{2,0},{1,3},{3,1},{4,6},{6,4},{5,7},{7,5}} | collective-permute-start | bytes 3440648 | tf_op jit(solution)/shard_map/ppermute | solution.py:536
  1203.9 116.5 %collective-permute-start.24 = (bf16[320,4480]{1,0:T(8,128)(2,1)}, bf16[320,4480]{1,0:T(8,128)(2,1)}, u32[]{:S(2)}, u32[]{:S(2)}) collective-permute-start(bf16[320,4480]{1,0:T(8,128)(2,1)} %get-tuple-element.121), channel_id=1, source_target_pairs={{0,1},{1,0},{2,3},{3,2},{4,5},{5,4},{6,7},{7,6}} | collective-permute-start | bytes 8601608 | tf_op jit(solution)/shard_map/ppermute | solution.py:540
  1203.9 116.0 %collective-permute-start.31 = (bf16[672,1280]{1,0:T(8,128)(2,1)}, bf16[672,1280]{1,0:T(8,128)(2,1)}, u32[]{:S(2)}, u32[]{:S(2)}) collective-permute-start(bf16[672,1280]{1,0:T(8,128)(2,1)} %get-tuple-element.131), channel_id=1, source_target_pairs={{0,2},{2,0},{1,3},{3,1},{4,6},{6,4},{5,7},{7,5}} | collective-permute-start | bytes 5160968 | tf_op jit(solution)/shard_map/ppermute | solution.py:536
  1204.3 146.5 %collective-permute-start.14 = (bf16[320,4480]{1,0:T(8,128)(2,1)}, bf16[320,4480]{1,0:T(8,128)(2,1)}, u32[]{:S(2)}, u32[]{:S(2)}) collective-permute-start(bf16[320,4480]{1,0:T(8,128)(2,1)} %collective-permute-done.13.refs_0_), channel_id=1, source_target_pairs={{0,1},{1,0},{2,3},{3,2},{4,5},{5,4},{6,7},{7,6}} | collective-permute-start | bytes 8601608 | tf_op jit(solution)/shard_map/ppermute | solution.py:540
  1284.0 35.9 %collective-permute-start.33 = (bf16[672,1280]{1,0:T(8,128)(2,1)}, bf16[672,1280]{1,0:T(8,128)(2,1)}, u32[]{:S(2)}, u32[]{:S(2)}) collective-permute-start(bf16[672,1280]{1,0:T(8,128)(2,1)} %get-tuple-element.131), channel_id=1, source_target_pairs={{0,1},{1,0},{2,3},{3,2},{4,5},{5,4},{6,7},{7,6}} | collective-permute-start | bytes 5160968 | tf_op jit(solution)/shard_map/ppermute | solution.py:540
  1284.0 84.8 %collective-permute-start.23 = (bf16[320,4480]{1,0:T(8,128)(2,1)S(1)}, bf16[320,4480]{1,0:T(8,128)(2,1)}, u32[]{:S(2)}, u32[]{:S(2)}) collective-permute-start(bf16[320,4480]{1,0:T(8,128)(2,1)S(1)} %collective-permute-done.22.refs_0_), channel_id=1, source_target_pairs={{0,1},{1,0},{2,3},{3,2},{4,5},{5,4},{6,7},{7,6}} | collective-permute-start | bytes 8601608 | tf_op jit(solution)/shard_map/ppermute | solution.py:540
  1319.9 36.4 %collective-permute-start.32 = (bf16[672,1280]{1,0:T(8,128)(2,1)}, bf16[672,1280]{1,0:T(8,128)(2,1)}, u32[]{:S(2)}, u32[]{:S(2)}) collective-permute-start(bf16[672,1280]{1,0:T(8,128)(2,1)} %collective-permute-done.31.refs_0_), channel_id=1, source_target_pairs={{0,1},{1,0},{2,3},{3,2},{4,5},{5,4},{6,7},{7,6}} | collective-permute-start | bytes 5160968 | tf_op jit(solution)/shard_map/ppermute | solution.py:540
  1319.9 40.5 %collective-permute-start.30 = (bf16[448,1280]{1,0:T(8,128)(2,1)}, bf16[448,1280]{1,0:T(8,128)(2,1)}, u32[]{:S(2)}, u32[]{:S(2)}) collective-permute-start(bf16[448,1280]{1,0:T(8,128)(2,1)} %get-tuple-element.130), channel_id=1, source_target_pairs={{0,1},{1,0},{2,3},{3,2},{4,5},{5,4},{6,7},{7,6}} | collective-permute-start | bytes 3440648 | tf_op jit(solution)/shard_map/ppermute | solution.py:540
  1320.5 45.6 %collective-permute-start.29 = (bf16[448,1280]{1,0:T(8,128)(2,1)}, bf16[448,1280]{1,0:T(8,128)(2,1)}, u32[]{:S(2)}, u32[]{:S(2)}) collective-permute-start(bf16[448,1280]{1,0:T(8,128)(2,1)} %collective-permute-done.28.refs_0_), channel_id=1, source_target_pairs={{0,1},{1,0},{2,3},{3,2},{4,5},{5,4},{6,7},{7,6}} | collective-permute-start | bytes 3440648 | tf_op jit(solution)/shard_map/ppermute | solution.py:540
  (6 other events, 143.6 us)

commit v3 on v2

--- a/solution.py
+++ b/solution.py
@@ -73,10 +73,11 @@
     return jnp.where(lax.broadcasted_iota(jnp.int32, a.shape, axis) < n, a, jnp.zeros_like(a))
 
 
-def first_kernel(at, x, wg, wu, wd, m, v, a_out, hid, s_out, q_out, h_out, half, a, units, total, *, f):
+def first_kernel(at, x, wg, wu, wd, mg, vg, mu, vu, a_out, hid, s_out, q_out, h_out, half_gate, half_up, a, units, total, *, f):
     j = pl.program_id(1)
     left = f - j * UNITS
-    half[...] = jnp.where(at[2] == 0, m[...], v[...])
+    half_gate[...] = jnp.where(at[2] == 0, mg[...], vg[...])
+    half_up[...] = jnp.where(at[2] == 0, mu[...], vu[...])
 
     @pl.when(j == 0)
     def _():
@@ -102,7 +103,8 @@
         loop(x.shape[0] // CHUNK, CHUNK, rows)
 
 
-def first(at, x, w_gate, w_up, w_down, m, v):
+def first(at, x, w_gate, w_up, w_down, moments):
+    m = moments[0]
     t, d = x.shape
     f = w_gate.shape[2]
     n = pl.cdiv(f, UNITS)
@@ -118,17 +120,17 @@
         functools.partial(first_kernel, f=f),
         at,
         (t // TOKENS, n),
-        [state, weight, weight, pl.BlockSpec((None, UNITS, d), lambda i, j, at: (0, j, 0)), moment(0), moment(1)],
+        [state, weight, weight, pl.BlockSpec((None, UNITS, d), lambda i, j, at: (0, j, 0)), *[moment(0), moment(1)] * 2],
         [
             pl.BlockSpec((d, TOKENS), lambda i, j, at: (0, i)),
             pl.BlockSpec((UNITS, TOKENS), lambda i, j, at: (j, i)),
             wide,
             wide,
             state,
-            pl.BlockSpec((m.shape[1], cols), lambda i, j, at: (0, i * n + j)),
-        ],
-        [out((d, t)), out((f, t)), out((t, f), F32), out((t, f), F32), out((t, d)), out(m.shape[1:], F32)],
-        (x, w_gate, w_up, w_down, m, v),
+        ]
+        + [pl.BlockSpec((m.shape[1], cols), lambda i, j, at: (0, i * n + j))] * 2,
+        [out((d, t)), out((f, t)), out((t, f), F32), out((t, f), F32), out((t, d))] + [out(m.shape[1:], F32)] * 2,
+        (x, w_gate, w_up, w_down, *moments),
         6 * t * d * f,
         190e6,
         scratch=[pltpu.VMEM((TOKENS, d), BF), pltpu.VMEM((TOKENS, UNITS), BF), pltpu.VMEM((TOKENS, d), F32)],
@@ -186,18 +188,19 @@
 def second(at, h, dy, w_gate, w_up, w_down, before=None):
     t, d = h.shape
     f = w_gate.shape[2]
+    far = before is not None
+    bt = TOKENS // 2 if far else TOKENS
     weight = pl.BlockSpec((None, d, UNITS), lambda i, j, at: (1, 0, j))
-    state = pl.BlockSpec((TOKENS, d), lambda i, j, at: (i, 0))
-    far = before is not None
+    state = pl.BlockSpec((bt, d), lambda i, j, at: (i, 0))
     which = (lambda at: 1 - at[0]) if far else (lambda at: at[0])
     in_specs = [state, state, weight, weight, pl.BlockSpec((None, UNITS, d), lambda i, j, at: (1, j, 0))]
     out_specs = [
-        pl.BlockSpec((None, d, TOKENS), lambda i, j, at: (which(at), 0, i)),
-        pl.BlockSpec((None, 2, TOKENS, UNITS), lambda i, j, at: (which(at), 0, i, j)),
-        pl.BlockSpec((UNITS, TOKENS), lambda i, j, at: (j, i)),
+        pl.BlockSpec((None, d, bt), lambda i, j, at: (which(at), 0, i)),
+        pl.BlockSpec((None, 2, bt, UNITS), lambda i, j, at: (which(at), 0, i, j)),
+        pl.BlockSpec((UNITS, bt), lambda i, j, at: (j, i)),
     ]
     shapes = [out((2, d, t)), out((2, 2, t, f)), out((f, t))]
-    scratch = [pltpu.VMEM((TOKENS, d), BF)]
+    scratch = [pltpu.VMEM((bt, d), BF)]
     operands = [h, dy, w_gate, w_up, w_down]
     aliases = {}
     if far:
@@ -207,12 +210,12 @@
     else:
         out_specs.append(state)
         shapes.append(out((t, d)))
-        scratch += [pltpu.VMEM((TOKENS, d), F32)] * 2
+        scratch += [pltpu.VMEM((bt, d), F32)] * 2
     return pl.pallas_call(
         functools.partial(second_kernel if far else second_back_kernel, f=f),
         grid_spec=pltpu.PrefetchScalarGridSpec(
             num_scalar_prefetch=1,
-            grid=(t // TOKENS, pl.cdiv(f, UNITS)),
+            grid=(t // bt, pl.cdiv(f, UNITS)),
             in_specs=in_specs,
             out_specs=out_specs,
             scratch_shapes=scratch,
@@ -277,7 +280,7 @@
 def grad_wide(at, left, right, one, two, got):
     rows, t = left.shape[1:]
     f = right.shape[2]
-    bn = 1536
+    bn = 768
     return call(
         wide_kernel,
         at,
@@ -292,44 +295,32 @@
     )
 
 
-def whole_kernel(at, left0, left1, right0, right1, send_far, keep_far, send, keep, total):
-    x, c = at[0], at[1]
-    rows = send.shape[0]
-
-    def product(r):
-        return (dot(left0[r, :], right0[...], NN) + dot(left1[r, :], right1[...], NN)).reshape(-1, *total.shape[1:])
-
-    @pl.when(pl.program_id(0) == 0)
-    def _():
-        total[...] = product(slice(None))
-        send_far[...], keep_far[...] = total[2 * (1 - x) + 1 - c].astype(BF), total[2 * (1 - x) + c]
-        send[...], keep[...] = total[2 * x + 1 - c].astype(BF), total[2 * x + c]
-
-    @pl.when(pl.program_id(0) == 1)
-    def _():
-        total[:2] = product(pl.ds(pl.multiple_of(x * 2 * rows, 2 * rows), 2 * rows))
-        send[...], keep[...] = total[1 - c].astype(BF), total[c]
+def whole_kernel(at, left0, left1, right0, right1, send, keep, total):
+    total[...] = (dot(left0[...], right0[...], NN) + dot(left1[...], right1[...], NN)).reshape(total.shape)
+    send[...], keep[...] = total[1 - at[1]].astype(BF), total[at[1]]
 
 
 def grad_whole(at, left, right):
     d, t = left.shape[1:]
     f = right.shape[3]
     rows, bn = d // 4, 768
-    n = pl.cdiv(f, bn)
-    far = pl.BlockSpec((rows, bn), lambda w, j, at: (0, jnp.where(w == 0, j, n - 1)))
     same = pl.BlockSpec((None, rows, bn), lambda w, j, at: (w, 0, j))
+
+    def half(w, at):
+        return jnp.where(w < 2, at[0], 1 - at[0])
+
     return call(
         whole_kernel,
         at,
-        (2, n),
-        [once((None, d, t), lambda w, j, at, x=x: (x, 0, 0)) for x in range(2)]
-        + [pl.BlockSpec((None, None, t, bn), lambda w, j, at, x=x: (x, w, 0, j)) for x in range(2)],
-        [far, far, same, same],
-        [out((rows, f)), out((rows, f), F32), out((2, rows, f)), out((2, rows, f), F32)],
+        (4, pl.cdiv(f, bn)),
+        [pl.BlockSpec((None, 2 * rows, t), lambda w, j, at, x=x: (x, half(w, at), 0)) for x in range(2)]
+        + [pl.BlockSpec((None, None, t, bn), lambda w, j, at, x=x: (x, w % 2, 0, j)) for x in range(2)],
+        [same, same],
+        [out((4, rows, f)), out((4, rows, f), F32)],
         (left, left, right, right),
-        6 * d * t * f,
+        8 * d * t * f,
         120e6,
-        scratch=[pltpu.VMEM((4, rows, bn), F32)],
+        scratch=[pltpu.VMEM((2, rows, bn), F32)],
     )
 
 
@@ -354,7 +345,7 @@
         rest[-1][...] = total
 
 
-def grad_tall(at, pairs, one, two, got=None, keeps=True, half=2):
+def grad_tall(at, pairs, one, two, got=None, keeps=True, half=4):
     rows, t = pairs[0][0].shape[1:]
     d = pairs[0][1].shape[1]
     bm = rows // half
@@ -387,44 +378,48 @@
     )
 
 
-def squares_of(keep, far):
-    g = (keep[...] + far[...].astype(F32)).astype(BF).astype(F32)
-    g = jnp.sum((g * g).reshape(-1, 8, g.shape[-1]), 0)
-    return sum(g[:, c] for c in chunks(g.shape[1], 128))
-
-
-def squares_kernel(*refs):
-    o = refs[-1]
-
-    @pl.when(pl.program_id(0) == 0)
-    def _():
-        o[...] = jnp.zeros_like(o)
-
-    o[...] += sum(squares_of(keep, far) for keep, far in zip(refs[:-1:2], refs[1:-1:2], strict=True))
-
-
-def sum_of_squares(pairs, n):
-    specs = []
-    for a, _ in pairs:
-        br = a.shape[-2] // n
-        if a.ndim == 2:
-            spec = pl.BlockSpec((br, a.shape[1]), lambda i: (i, 0))
-        else:
-            spec = pl.BlockSpec((a.shape[0], br, a.shape[2]), lambda i: (0, i, 0))
-        specs += [spec, spec]
+def squares_kernel(keep, far, o, keep_in, far_in, sems, *, n):
+    rows = keep_in.shape[1] // n
+
+    def copies(i):
+        r = pl.ds(i * rows, rows)
+        which = pl.ds(0, keep_in.shape[0])
+        return (
+            pltpu.make_async_copy(keep.at[which, r], keep_in.at[:, r], sems.at[0, i]),
+            pltpu.make_async_copy(far.at[which, r], far_in.at[:, r], sems.at[1, i]),
+        )
+
+    for i in range(n):
+        for copy in copies(i):
+            copy.start()
+    o[...] = jnp.zeros_like(o)
+    for i in range(n):
+        for copy in copies(i):
+            copy.wait()
+
+        def add(k, _, start=i * rows):
+            which, k = k // (rows // 16), k % (rows // 16)
+            r = pl.ds(pl.multiple_of(start + k * 16, 16), 16)
+            g = (keep_in[which, r, :] + far_in[which, r, :].astype(F32)).astype(BF).astype(F32)
+            g = jnp.sum((g * g).reshape(-1, 8, g.shape[-1]), 0)
+            o[...] += sum(g[:, c] for c in chunks(g.shape[1], 128))
+
+        lax.fori_loop(0, keep_in.shape[0] * (rows // 16), add, None)
+
+
+def sum_of_squares(keep, far, first):
+    n = 5
+    shape = (first, *keep.shape[1:])
     return pl.pallas_call(
-        squares_kernel,
-        grid=(n,),
-        in_specs=specs,
-        out_specs=pl.BlockSpec((8, 128), lambda i: (0, 0)),
+        functools.partial(squares_kernel, n=n),
+        in_specs=[pl.BlockSpec(memory_space=pl.ANY)] * 2,
+        out_specs=pl.BlockSpec(memory_space=pltpu.VMEM),
         out_shape=out((8, 128), F32),
+        scratch_shapes=[pltpu.VMEM(shape, F32), pltpu.VMEM(shape, BF), pltpu.SemaphoreType.DMA((2, n))],
         compiler_params=params(),
-        cost_estimate=cost(1e9, 4e6 * len(specs)),
+        cost_estimate=cost(1e9, 8e6),
         name="squares",
-    )(*[a for pair in pairs for a in pair])
-
-
-UNITS_OF_ROWS = 5
+    )(keep, far)
 
 
 def updated(g, w, m, v):
@@ -434,23 +429,27 @@
     return (wide - 0.02 * (m * lax.rsqrt(v + 1e-8) + 0.1 * wide)).astype(BF), m, v
 
 
-def gradient(factor, keep, far):
-    return (keep[...] + far[...].astype(F32)).astype(BF).astype(F32) * factor[0]
+def gradient(factor, keep, far, r):
+    return (keep[r, :] + far[r, :].astype(F32)).astype(BF).astype(F32) * factor[0]
 
 
 def adam_kernel(at, factor, keep, far, w, m, v, *rest):
     w_out, m_out, v_out, w_new = rest[-4:]
-    w_out[...], m_out[...], v_out[...] = updated(gradient(factor, keep, far), w[...], m[...], v[...])
-    w_new[...] = w_out[...]
+
+    def rows(r):
+        w_out[r, :], m_out[r, :], v_out[r, :] = updated(gradient(factor, keep, far, r), w[r, :], m[r, :], v[r, :])
+        w_new[r, :] = w_out[r, :]
+
+    loop(w.shape[0] // 16, 16, rows)
 
 
 def adam(at, factor, layer, which, part, keep, far, w, m, v, before):
     rows, cols = keep.shape[1:]
-    br = rows // UNITS_OF_ROWS
-    low, high = part
+    low, high, n = part
+    br = rows // n
     own = pl.BlockSpec((None, br, cols), lambda i, at: (layer, low + i, 0))
     grad = pl.BlockSpec((None, br, cols), lambda i, at: (which, low + i, 0))
-    there = pl.BlockSpec((None, br, cols), lambda i, at: (layer, (2 * at[0] + at[1]) * UNITS_OF_ROWS + low + i, 0))
+    there = pl.BlockSpec((None, br, cols), lambda i, at: (layer, (2 * at[0] + at[1]) * n + low + i, 0))
     return call(
         adam_kernel,
         at,
@@ -466,21 +465,26 @@
 
 
 def adam_far_kernel(at, factor, keep, far, w, crossed, handed, before, w_out, w_new):
-    m, v = jnp.where(at[2] == 0, crossed[...], handed[...]), jnp.where(at[2] == 0, handed[...], crossed[...])
-    w_out[...], _, _ = updated(gradient(factor, keep, far), w[...], m, v)
-    w_new[...] = w_out[...]
-
-
-def adam_far(at, factor, layer, keep, far, w, crossed, handed, before):
-    rows, cols = keep.shape
-    br = rows // UNITS_OF_ROWS
+    def rows(r):
+        m, v = jnp.where(at[2] == 0, crossed[r, :], handed[r, :]), jnp.where(at[2] == 0, handed[r, :], crossed[r, :])
+        w_out[r, :], _, _ = updated(gradient(factor, keep, far, r), w[r, :], m, v)
+        w_new[r, :] = w_out[r, :]
+
+    loop(w.shape[0] // 16, 16, rows)
+
+
+def adam_far(at, factor, layer, which, keep, far, w, crossed, handed, before):
+    rows, cols = keep.shape[1:]
+    n = 2
+    br = rows // n
+    grad = pl.BlockSpec((None, br, cols), lambda i, at: (which, i, 0))
     flat = pl.BlockSpec((br, cols), lambda i, at: (i, 0))
-    there = pl.BlockSpec((None, br, cols), lambda i, at: (layer, (2 * (1 - at[0]) + at[1]) * UNITS_OF_ROWS + i, 0))
+    there = pl.BlockSpec((None, br, cols), lambda i, at: (layer, (2 * (1 - at[0]) + at[1]) * n + i, 0))
     return call(
         adam_far_kernel,
         at,
-        (UNITS_OF_ROWS,),
-        [pl.BlockSpec(memory_space=pltpu.SMEM), flat, flat, there, flat, flat, pl.BlockSpec(memory_space=pl.ANY)],
+        (n,),
+        [pl.BlockSpec(memory_space=pltpu.SMEM), grad, grad, there, flat, flat, pl.BlockSpec(memory_space=pl.ANY)],
         [flat, there],
         [out((rows, cols)), out(w.shape)],
         [factor, keep, far, w, crossed, handed, before],
@@ -496,7 +500,7 @@
 
 
 def place(at, layer, part, blocks, wheres, before):
-    low, high = part
+    low, high, n = part
     k = high - low
     cols = blocks[0].shape[1]
     br = blocks[0].shape[0] // k
@@ -506,9 +510,9 @@
 
     def where(i, j, at):
         b = wheres[0](at)
-        for n, w in enumerate(wheres[1:], 1):
-            b = jnp.where(i == n, w(at), b)
-        return layer, b * UNITS_OF_ROWS + low + j, 0
+        for k, w in enumerate(wheres[1:], 1):
+            b = jnp.where(i == k, w(at), b)
+        return layer, b * n + low + j, 0
 
     return call(
         functools.partial(place_kernel, count=len(blocks)),
@@ -550,10 +554,15 @@
         return a.reshape(4, a.shape[0] // 4, a.shape[1])
 
     dy_far = across(dy)
-    a1, hid1, s1, q1, h1, half = first(at, x, w_gate, w_up, w_down, m_gate, v_gate)
+    moments = m_gate, v_gate, m_up, v_up
+    a1, hid1, s1, q1, h1, half_gate, half_up = first(at, x, w_gate, w_up, w_down, moments)
     h1_far = across(h1)
-    crossed = across(half)
-    handed = lax.ppermute(crossed, "rep", [(0, 1), (1, 0)])
+
+    def brought(half):
+        crossed = across(half)
+        return crossed, lax.ppermute(crossed, "rep", [(0, 1), (1, 0)])
+
+    far_moments = {"gate": brought(half_gate), "up": brought(half_up)}
     a2, dgu2, hid2, d1 = second(at, h1, dy, w_gate, w_up, w_down)
 
     dgu1, theirs = hidden_back(at, w_down, d1, s1, q1, blocks(a1))
@@ -565,20 +574,21 @@
     send, keep_wide1 = grad_wide(at, blocks(a1), dgu1, on(False, True), on(True, True), got_wide)
     far_wide1 = across(send)
     got_down = after(got_down, keep_wide1)
-    send, keep_down1 = grad_tall(at, pairs, on(False, True), on(True, True), got_down)
+    send, keep_down1 = grad_tall(at, pairs, on(False, True), on(True, True), got_down, half=7)
     far_down1 = across(send)
 
     h1_far = after(h1_far, keep_down1)
     a2, dgu2, hid2f = second(at, h1_far, dy_far, w_gate, w_up, w_down, [a2, dgu2])
-    send, keep_other, send_wide, keep_wide2 = grad_whole(at, a2, dgu2)
-    far_other, far_wide2 = sibling(send), sibling(send_wide)
+    send, keep_wide2 = grad_whole(at, a2, dgu2)
+    far_wide2 = sibling(send)
     pairs = [(blocks(hid2), dy), (blocks(after(hid2f, keep_wide2)), dy_far)]
-    send, keep_down2 = grad_tall(at, pairs, on(True, False), on(True, True))
+    send, keep_down2 = grad_tall(at, pairs, on(True, False), on(True, True), half=7)
     far_down2 = sibling(send)
-
-    most = sum_of_squares([(keep_wide2, far_wide2), (keep_down1, far_down1), (keep_wide1, far_wide1)], 10)
-    far_down2 = after(far_down2, most)
-    squares = jnp.sum(most + sum_of_squares([(keep_down2, far_down2)], 5))
+    keep_down1, far_down1, keep_down2, far_down2 = (a[None] for a in (keep_down1, far_down1, keep_down2, far_down2))
+    sums = [sum_of_squares(keep_wide1, far_wide1, 2), sum_of_squares(keep_down1, far_down1, 1)]
+    sums.append(sum_of_squares(keep_wide2, after(far_wide2, *sums), 2))
+    far_down2 = after(far_down2, *sums)
+    squares = jnp.sum(sum(sums) + sum_of_squares(keep_down2, far_down2, 1))
     squares = lax.psum(squares, "dp")
     factor = jnp.minimum(1.0, 0.5 * lax.rsqrt(squares / (6 * d * f) + 1e-30)).reshape(1)
 
@@ -586,10 +596,10 @@
     grads = {
         "gate1": (1, 0, keep_wide2, far_wide2),
         "up1": (1, 1, keep_wide2, far_wide2),
-        "down1": (1, 0, keep_down2[None], far_down2[None]),
+        "down1": (1, 0, keep_down2, far_down2),
         "gate0": (0, 0, keep_wide1, far_wide1),
         "up0": (0, 1, keep_wide1, far_wide1),
-        "down0": (0, 0, keep_down1[None], far_down1[None]),
+        "down0": (0, 0, keep_down1, far_down1),
     }
     new = dict.fromkeys(weights, ())
 
@@ -604,31 +614,46 @@
         where, arrays = zip(*blocks, strict=True)
         new[name] = [*moments, place(at, grads[which][0], part, arrays, where, w)]
 
-    whole = (0, UNITS_OF_ROWS)
-    own = update("gate1", whole)
-    *moments, w = new["gate"]
-    away, w = adam_far(at, factor, 1, keep_other, far_other, w_gate, crossed, handed, w)
-    new["gate"] = [*moments, w]
-    put("gate1", whole, (on(True, False), sibling(own)), (on(False, False), sibling(away)))
-
-    parts = []
-    for n, (which, part) in enumerate(PARTS):
+    def send(n):
+        which, part = PARTS[n]
         own = update(which, part)
-        parts.append((across(own), sibling(own)))
-        if n in LATER:
-            continue
-        for n, (away, beside) in enumerate(parts):
-            if away is not None:
-                which, part = PARTS[n]
-                put(which, part, (on(True, False), beside))
-                put(which, part, (on(False, True), away))
-                put(which, part, (on(False, False), sibling(away)))
-                parts[n] = None, None
+        return across(own), sibling(own)
+
+    def settle(n, away, beside):
+        which, part = PARTS[n]
+        put(which, part, (on(True, False), beside))
+        put(which, part, (on(False, True), away))
+        put(which, part, (on(False, False), sibling(away)))
+
+    def both_blocks(name, which):
+        part = (0, 2, 2)
+        own = update(name + "1", part)
+        *moments, w = new[name]
+        arrays = keep_wide2, far_wide2, weights[name][0], *far_moments[name]
+        away, w = adam_far(at, factor, 1, which, *arrays, w)
+        new[name] = [*moments, w]
+        beside, last = sibling(own), sibling(away)
+        put(name + "1", part, (on(True, False), beside), (on(False, False), last))
+
+    sent = [send(n) for n in range(len(PARTS) - 2)]
+    both_blocks("gate", 2)
+    both_blocks("up", 3)
+    for n, parts in enumerate(sent):
+        settle(n, *parts)
+    for n, parts in enumerate([send(n) for n in range(len(sent), len(PARTS))], len(sent)):
+        settle(n, *parts)
     return tuple(new[name][i] for i in (2, 0, 1) for name in weights)
 
 
-PARTS = [("up1", (0, 1)), ("up1", (1, 5)), ("down1", (0, 5)), ("gate0", (0, 5)), ("up0", (0, 5)), ("down0", (0, 3)), ("down0", (3, 5))]
-LATER = (0, 5)
+PARTS = [
+    ("down1", (0, 1, 10)),
+    ("down1", (1, 2, 10)),
+    ("down1", (1, 5, 5)),
+    ("gate0", (0, 2, 2)),
+    ("up0", (0, 2, 2)),
+    ("down0", (0, 3, 5)),
+    ("down0", (3, 5, 5)),
+]
 
 
 def solution(mesh):

time: 1390 us -> 1620 us (1.17)
  waiting for transfers between devices: 512 us -> 715 us
  Pallas kernels: 829 us -> 866 us
    ppermute x12 -> x13, waiting for transfers between devices: 502 us -> 712 us  [across(): return lax.ppermute(a, 'dp', ACROSS)]
    pallas_call x38 -> x41, Pallas kernels: 567 us -> 593 us  [call(): pl.pallas_call(kernel, grid_spec=pltpu.PrefetchScalarGridSpec(num_scalar_...]
  transfers between devices with their start and end apart: 34 -> 37, of which waited for: 7 -> 14; matrix products, arithmetic and copies ran while one was open for 0% -> 0% of each run, Pallas kernels for 38% -> 21%
where the time goes in v3:
time: 1620 us
  Pallas kernels  866 us (53%)
  waiting for transfers between devices  715 us (44%)
  starting transfers between devices  19.3 us (1%)
    ppermute x13, waiting for transfers between devices, across(): return lax.ppermute(a, 'dp', ACROSS)  712 us
    pallas_call x41, Pallas kernels, call(): pl.pallas_call(kernel, grid_spec=pltpu.PrefetchScalarGridSpec(num_scalar_...  593 us
    pallas_call x2, Pallas kernels, second(): pl.pallas_call(functools.partial(second_kernel if far else second_back_ke...  249 us
  transfers between devices with their start and end apart: 37, of which 14 were waited for; matrix products, arithmetic and copies ran while one was open for 0% of the time, Pallas kernels for 21%

profile of v3, /device:TPU:0, one launch (start us, length us, event | category | flops | bytes accessed | tf_op | source)
XLA Modules:
  0.0 1616.1 jit_solution(8887596372934763761)
XLA Ops:
  1.3 97.1 %shard_map.178 = (bf16[1280,2048]{1,0:T(8,128)(2,1)}, bf16[4480,2048]{1,0:T(8,128)(2,1)}, f32[2048,4480]{1,0:T(8,128)}, f32[2048,4480]{1,0:T(8,128)}, bf16[2048,...) custom-call(s32[3]{0:T(128)} %pad_add_fusion.at, bf16[2048,1280]{1,0:T(8,128)(2,1)} %bitcast.28, ...), custom_call_target="tpu_custom_call" | custom-call | flops 70464307200 | bytes 190000000 | tf_op jit(solution)/shard_map/pallas_call | solution.py:38
  98.4 146.4 %second_back.1 = (bf16[2,1280,2048]{2,1,0:T(8,128)(2,1)}, bf16[2,2,2048,4480]{3,2,1,0:T(8,128)(2,1)}, bf16[4480,2048]{1,0:T(8,128)(2,1)}, bf16[2048,1280]{1,0:T(8,128)(2,1)}) custom-call(s32[3]{0:T(128)} %pad_add_fusion.at, bf16[2048,1280]{1,0:T(8,128)(2,1)} %get-tuple-element.81.h, bf16[2048,1280]{1,0:T(8,128)(2,1)} %bitcast.29, bf16[2,1280,4480]{2,1,0:T(8,128)(2,1)} %w.15, ...), custom_call_target="tpu_custom_call" | custom-call | flops 117440512000 | bytes 130000000 | tf_op jit(solution)/shard_map/second_back/pallas_call | solution.py:214
  244.8 63.5 %shard_map.179 = (bf16[2,2048,4480]{2,1,0:T(8,128)(2,1)}, bf16[2,2,320,4480]{3,2,1,0:T(8,128)(2,1)}) custom-call(s32[3]{0:T(128)} %pad_add_fusion.at, bf16[2,4480,1280]{2,1,0:T(8,128)(2,1)} %w.23, bf16[2048,1280]{1,0:T(8,128)(2,1)} %get-tuple-element.88.d.refs_1_, f32[2048,4480]{1,0:T(8,128)} %get-tuple-element.83.s, f32[2048,4480]{1,0:T(8,128)} %get-tuple-element.84.q, ...), custom_call_target="tpu_custom_call" | custom-call | flops 46976204800 | bytes 160000000 | tf_op jit(solution)/shard_map/pallas_call | solution.py:38
  309.1 18.3 %shard_map.180 = bf16[2,1120,1280]{2,1,0:T(8,128)(2,1)} custom-call(s32[3]{0:T(128)} %pad_add_fusion.at, bf16[4,1120,2048]{2,1,0:T(8,128)(2,1)} %bitcast.34, bf16[2048,1280]{1,0:T(8,128)(2,1)} %get-tuple-element.88.d.refs_1_), custom_call_target="tpu_custom_call" | custom-call | flops 11744051200 | bytes 60000000 | tf_op jit(solution)/shard_map/pallas_call | solution.py:38
  330.5 33.8 %shard_map.181 = (bf16[2,320,4480]{2,1,0:T(8,128)(2,1)}, f32[2,320,4480]{2,1,0:T(8,128)}) custom-call(s32[3]{0:T(128)} %pad_add_fusion.at, bf16[4,320,2048]{2,1,0:T(8,128)(2,1)} %bitcast.38, bf16[4,320,2048]{2,1,0:T(8,128)(2,1)} %bitcast.39, bf16[2,2048,4480]{2,1,0:T(8,128)(2,1)} %get-tuple-element.85.right, bf16[2,2,320,4480]{3,2,1,0:T(8,128)(2,1)} %collective-permute-done.got), custom_call_target="tpu_custom_call" | custom-call | flops 23488102400 | bytes 60000000 | tf_op jit(solution)/shard_map/pallas_call | solution.py:38
  364.3 22.0 %shard_map.182 = (bf16[1120,1280]{1,0:T(8,128)(2,1)}, f32[1120,1280]{1,0:T(8,128)}) custom-call(s32[3]{0:T(128)} %pad_add_fusion.at, bf16[4,1120,2048]{2,1,0:T(8,128)(2,1)} %bitcast.35, bf16[2048,1280]{1,0:T(8,128)(2,1)} %get-tuple-element.88.d.refs_1_, bf16[2,1120,1280]{2,1,0:T(8,128)(2,1)} %collective-permute-done.2.refs_2_), custom_call_target="tpu_custom_call" | custom-call | flops 11744051200 | bytes 60000000 | tf_op jit(solution)/shard_map/pallas_call | solution.py:38
  386.3 58.4 %collective-permute-done.4.h = bf16[2048,1280]{1,0:T(8,128)(2,1)} collective-permute-done((bf16[2048,1280]{1,0:T(8,128)(2,1)}, bf16[2048,1280]{1,0:T(8,128)(2,1)}, u32[]{:S(2)}, u32[]{:S(2)}) %collective-permute-start.4) | collective-permute-done | bytes 5242912 | tf_op jit(solution)/shard_map/ppermute | solution.py:540
  444.7 111.7 %collective-permute-done.5.dy.refs_3_ = bf16[2048,1280]{1,0:T(8,128)(2,1)} collective-permute-done((bf16[2048,1280]{1,0:T(8,128)(2,1)}, bf16[2048,1280]{1,0:T(8,128)(2,1)}, u32[]{:S(2)}, u32[]{:S(2)}) %collective-permute-start.5) | collective-permute-done | bytes 5242912 | tf_op jit(solution)/shard_map/ppermute | solution.py:540
  556.3 103.0 %second.1 = (bf16[2,1280,2048]{2,1,0:T(8,128)(2,1)}, bf16[2,2,2048,4480]{3,2,1,0:T(8,128)(2,1)}, bf16[4480,2048]{1,0:T(8,128)(2,1)}) custom-call(s32[3]{0:T(128)} %pad_add_fusion.at, bf16[2048,1280]{1,0:T(8,128)(2,1)} %collective-permute-done.4.h, ...), custom_call_target="tpu_custom_call", output_to_operand_aliasing={{0}: (6, {}), {1}: (7, {})} | custom-call | flops 70464307200 | bytes 130000000 | tf_op jit(solution)/shard_map/second/pallas_call | solution.py:214
  659.3 113.2 %shard_map.183 = (bf16[4,320,4480]{2,1,0:T(8,128)(2,1)}, f32[4,320,4480]{2,1,0:T(8,128)}) custom-call(s32[3]{0:T(128)} %pad_add_fusion.at, bf16[2,1280,2048]{2,1,0:T(8,128)(2,1)} %get-tuple-element.98.left0.left1, bf16[2,1280,2048]{2,1,0:T(8,128)(2,1)} %get-tuple-element.98.left0.left1, bf16[2,2,2048,4480]{3,2,1,0:T(8,128)(2,1)} %get-tuple-element.99.right0.right1, ...), custom_call_target="tpu_custom_call" | custom-call | flops 93952409600 | bytes 120000000 | tf_op jit(solution)/shard_map/pallas_call | solution.py:38
  776.6 122.7 %collective-permute-done.19.crossed = f32[320,4480]{1,0:T(8,128)} collective-permute-done((f32[320,4480]{1,0:T(8,128)}, f32[320,4480]{1,0:T(8,128)}, u32[]{:S(2)}, u32[]{:S(2)}) %collective-permute-start.19) | collective-permute-done | bytes 5734432 | tf_op jit(solution)/shard_map/ppermute | solution.py:540
  901.1 121.1 %collective-permute-done.12.crossed = f32[320,4480]{1,0:T(8,128)} collective-permute-done((f32[320,4480]{1,0:T(8,128)}, f32[320,4480]{1,0:T(8,128)}, u32[]{:S(2)}, u32[]{:S(2)}) %collective-permute-start.12) | collective-permute-done | bytes 5734432 | tf_op jit(solution)/shard_map/ppermute | solution.py:540
  1024.0 33.8 %shard_map.184 = (bf16[1120,1280]{1,0:T(8,128)(2,1)}, f32[1120,1280]{1,0:T(8,128)}) custom-call(s32[3]{0:T(128)} %pad_add_fusion.at, bf16[4,1120,2048]{2,1,0:T(8,128)(2,1)} %bitcast.32, bf16[2048,1280]{1,0:T(8,128)(2,1)} %bitcast.31, bf16[4,1120,2048]{2,1,0:T(8,128)(2,1)} %bitcast.33, bf16[2048,1280]{1,0:T(8,128)(2,1)} %collective-permute-done.5.dy.refs_3_), custom_call_target="tpu_custom_call" | custom-call | flops 23488102400 | bytes 60000000 | tf_op jit(solution)/shard_map/pallas_call | solution.py:38
  1057.7 148.2 %collective-permute-done.3 = bf16[1120,1280]{1,0:T(8,128)(2,1)S(1)} collective-permute-done((bf16[1120,1280]{1,0:T(8,128)(2,1)}, bf16[1120,1280]{1,0:T(8,128)(2,1)S(1)}, u32[]{:S(2)}, u32[]{:S(2)}) %collective-permute-start.3) | collective-permute-done | bytes 2867232 | tf_op jit(solution)/shard_map/ppermute | solution.py:540
  1212.2 7.1 squares.4
  1219.4 7.1 squares.6
  1234.0 8.0 psum.7
  1250.4 12.7 shard_map.201
  1263.6 15.4 shard_map.192
  1279.0 15.5 shard_map.193
  1294.5 13.5 shard_map.194
  1308.9 8.5 collective-permute-done.28.refs_0_
  1319.4 7.9 collective-permute-done.25.refs_0_
  1331.7 15.4 shard_map.185
  1347.1 15.5 shard_map.186
  1362.6 13.5 shard_map.187
  1378.2 59.8 %collective-permute-done.15.refs_0_ = bf16[320,4480]{1,0:T(8,128)(2,1)} collective-permute-done((bf16[320,4480]{1,0:T(8,128)(2,1)}, bf16[320,4480]{1,0:T(8,128)(2,1)}, u32[]{:S(2)}, u32[]{:S(2)}) %collective-permute-start.15) | collective-permute-done | bytes 2867232 | tf_op jit(solution)/shard_map/ppermute | solution.py:540
  1466.2 11.4 shard_map.211
  1478.0 21.4 %collective-permute-done.8.refs_0_ = bf16[320,4480]{1,0:T(8,128)(2,1)} collective-permute-done((bf16[320,4480]{1,0:T(8,128)(2,1)}, bf16[320,4480]{1,0:T(8,128)(2,1)}, u32[]{:S(2)}, u32[]{:S(2)}) %collective-permute-start.8) | collective-permute-done | bytes 2867232 | tf_op jit(solution)/shard_map/ppermute | solution.py:540
  1499.5 7.0 shard_map.212
  1507.1 29.2 %collective-permute-done.34.refs_0_ = bf16[672,1280]{1,0:T(8,128)(2,1)} collective-permute-done((bf16[672,1280]{1,0:T(8,128)(2,1)}, bf16[672,1280]{1,0:T(8,128)(2,1)}, u32[]{:S(2)}, u32[]{:S(2)}) %collective-permute-start.34) | collective-permute-done | bytes 1720352 | tf_op jit(solution)/shard_map/ppermute | solution.py:540
  1536.8 22.7 %collective-permute-done.31.refs_0_ = bf16[448,1280]{1,0:T(8,128)(2,1)} collective-permute-done((bf16[448,1280]{1,0:T(8,128)(2,1)}, bf16[448,1280]{1,0:T(8,128)(2,1)}, u32[]{:S(2)}, u32[]{:S(2)}) %collective-permute-start.31) | collective-permute-done | bytes 1146912 | tf_op jit(solution)/shard_map/ppermute | solution.py:540
  (114 shorter events, 129.7 us)
Async XLA Ops:
  308.4 22.1 %collective-permute-start = (bf16[2,2,320,4480]{3,2,1,0:T(8,128)(2,1)}, bf16[2,2,320,4480]{3,2,1,0:T(8,128)(2,1)}, u32[]{:S(2)}, u32[]{:S(2)}) collective-permute-start(bf16[2,2,320,4480]{3,2,1,0:T(8,128)(2,1)} %get-tuple-element.86), channel_id=1, source_target_pairs={{0,1},{1,0},{2,3},{3,2},{4,5},{5,4},{6,7},{7,6}} | collective-permute-start | bytes 34406408 | tf_op jit(solution)/shard_map/ppermute | solution.py:544
  327.4 36.9 %collective-permute-start.2 = (bf16[2,1120,1280]{2,1,0:T(8,128)(2,1)}, bf16[2,1120,1280]{2,1,0:T(8,128)(2,1)}, u32[]{:S(2)}, u32[]{:S(2)}) collective-permute-start(bf16[2,1120,1280]{2,1,0:T(8,128)(2,1)} %shard_map.180), channel_id=1, source_target_pairs={{0,1},{1,0},{2,3},{3,2},{4,5},{5,4},{6,7},{7,6}} | collective-permute-start | bytes 17203208 | tf_op jit(solution)/shard_map/ppermute | solution.py:544
  327.4 117.3 %collective-permute-start.4 = (bf16[2048,1280]{1,0:T(8,128)(2,1)}, bf16[2048,1280]{1,0:T(8,128)(2,1)}, u32[]{:S(2)}, u32[]{:S(2)}) collective-permute-start(bf16[2048,1280]{1,0:T(8,128)(2,1)} %get-tuple-element.81.h), channel_id=1, source_target_pairs={{0,2},{2,0},{1,3},{3,1},{4,6},{6,4},{5,7},{7,5}} | collective-permute-start | bytes 15728648 | tf_op jit(solution)/shard_map/ppermute | solution.py:540
  330.5 225.9 %collective-permute-start.5 = (bf16[2048,1280]{1,0:T(8,128)(2,1)}, bf16[2048,1280]{1,0:T(8,128)(2,1)}, u32[]{:S(2)}, u32[]{:S(2)}) collective-permute-start(bf16[2048,1280]{1,0:T(8,128)(2,1)} %bitcast.30), channel_id=1, source_target_pairs={{0,2},{2,0},{1,3},{3,1},{4,6},{6,4},{5,7},{7,5}} | collective-permute-start | bytes 15728648 | tf_op jit(solution)/shard_map/ppermute | solution.py:540
  772.5 446.8 %collective-permute-start.6 = (bf16[4,320,4480]{2,1,0:T(8,128)(2,1)}, bf16[4,320,4480]{2,1,0:T(8,128)(2,1)}, u32[]{:S(2)}, u32[]{:S(2)}) collective-permute-start(bf16[4,320,4480]{2,1,0:T(8,128)(2,1)} %get-tuple-element.101), channel_id=1, source_target_pairs={{0,1},{1,0},{2,3},{3,2},{4,5},{5,4},{6,7},{7,6}} | collective-permute-start | bytes 34406408 | tf_op jit(solution)/shard_map/ppermute | solution.py:544
  772.5 126.8 %collective-permute-start.19 = (f32[320,4480]{1,0:T(8,128)}, f32[320,4480]{1,0:T(8,128)}, u32[]{:S(2)}, u32[]{:S(2)}) collective-permute-start(f32[320,4480]{1,0:T(8,128)} %get-tuple-element.123), channel_id=1, source_target_pairs={{0,2},{2,0},{1,3},{3,1},{4,6},{6,4},{5,7},{7,5}} | collective-permute-start | bytes 17203208 | tf_op jit(solution)/shard_map/ppermute | solution.py:540
  774.2 248.0 %collective-permute-start.12 = (f32[320,4480]{1,0:T(8,128)}, f32[320,4480]{1,0:T(8,128)}, u32[]{:S(2)}, u32[]{:S(2)}) collective-permute-start(f32[320,4480]{1,0:T(8,128)} %get-tuple-element.114), channel_id=1, source_target_pairs={{0,2},{2,0},{1,3},{3,1},{4,6},{6,4},{5,7},{7,5}} | collective-permute-start | bytes 17203208 | tf_op jit(solution)/shard_map/ppermute | solution.py:540
  774.6 437.6 %collective-permute-start.1 = (bf16[2,320,4480]{2,1,0:T(8,128)(2,1)}, bf16[2,320,4480]{2,1,0:T(8,128)(2,1)}, u32[]{:S(2)}, u32[]{:S(2)}) collective-permute-start(bf16[2,320,4480]{2,1,0:T(8,128)(2,1)} %get-tuple-element.91), channel_id=1, source_target_pairs={{0,2},{2,0},{1,3},{3,1},{4,6},{6,4},{5,7},{7,5}} | collective-permute-start | bytes 17203208 | tf_op jit(solution)/shard_map/ppermute | solution.py:540
  776.2 429.7 %collective-permute-start.3 = (bf16[1120,1280]{1,0:T(8,128)(2,1)}, bf16[1120,1280]{1,0:T(8,128)(2,1)S(1)}, u32[]{:S(2)}, u32[]{:S(2)}) collective-permute-start(bf16[1120,1280]{1,0:T(8,128)(2,1)} %get-tuple-element.94), channel_id=1, source_target_pairs={{0,2},{2,0},{1,3},{3,1},{4,6},{6,4},{5,7},{7,5}} | collective-permute-start | bytes 8601608 | tf_op jit(solution)/shard_map/ppermute | solution.py:540
  899.3 395.2 %collective-permute-start.20 = (f32[320,4480]{1,0:T(8,128)}, f32[320,4480]{1,0:T(8,128)}, u32[]{:S(2)}, u32[]{:S(2)}) collective-permute-start(f32[320,4480]{1,0:T(8,128)} %collective-permute-done.19.crossed), channel_id=1, source_target_pairs={{0,4},{4,0},{1,5},{5,1},{2,6},{6,2},{3,7},{7,3}} | collective-permute-start | bytes 17203208 | tf_op jit(solution)/shard_map/ppermute | solution.py:563
  1022.2 286.2 %collective-permute-start.13 = (f32[320,4480]{1,0:T(8,128)}, f32[320,4480]{1,0:T(8,128)}, u32[]{:S(2)}, u32[]{:S(2)}) collective-permute-start(f32[320,4480]{1,0:T(8,128)} %collective-permute-done.12.crossed), channel_id=1, source_target_pairs={{0,4},{4,0},{1,5},{5,1},{2,6},{6,2},{3,7},{7,3}} | collective-permute-start | bytes 17203208 | tf_op jit(solution)/shard_map/ppermute | solution.py:563
  1207.5 19.0 %collective-permute-start.7 = (bf16[1120,1280]{1,0:T(8,128)(2,1)}, bf16[1120,1280]{1,0:T(8,128)(2,1)S(1)}, u32[]{:S(2)}, u32[]{:S(2)}) collective-permute-start(bf16[1120,1280]{1,0:T(8,128)(2,1)} %get-tuple-element.107), channel_id=1, source_target_pairs={{0,1},{1,0},{2,3},{3,2},{4,5},{5,4},{6,7},{7,6}} | collective-permute-start | bytes 8601608 | tf_op jit(solution)/shard_map/ppermute | solution.py:544
  1263.1 68.2 %collective-permute-start.24 = (bf16[896,1280]{1,0:T(8,128)(2,1)}, bf16[896,1280]{1,0:T(8,128)(2,1)}, u32[]{:S(2)}, u32[]{:S(2)}) collective-permute-start(bf16[896,1280]{1,0:T(8,128)(2,1)} %get-tuple-element.135), channel_id=1, source_target_pairs={{0,1},{1,0},{2,3},{3,2},{4,5},{5,4},{6,7},{7,6}} | collective-permute-start | bytes 6881288 | tf_op jit(solution)/shard_map/ppermute | solution.py:544
  1263.1 45.5 %collective-permute-start.30 = (bf16[112,1280]{1,0:T(8,128)(2,1)}, bf16[112,1280]{1,0:T(8,128)(2,1)}, u32[]{:S(2)}, u32[]{:S(2)}) collective-permute-start(bf16[112,1280]{1,0:T(8,128)(2,1)} %get-tuple-element.137), channel_id=1, source_target_pairs={{0,1},{1,0},{2,3},{3,2},{4,5},{5,4},{6,7},{7,6}} | collective-permute-start | bytes 860168 | tf_op jit(solution)/shard_map/ppermute | solution.py:544
  1307.9 68.6 %collective-permute-start.21 = (bf16[320,4480]{1,0:T(8,128)(2,1)}, bf16[320,4480]{1,0:T(8,128)(2,1)S(1)}, u32[]{:S(2)}, u32[]{:S(2)}) collective-permute-start(bf16[320,4480]{1,0:T(8,128)(2,1)} %get-tuple-element.125), channel_id=1, source_target_pairs={{0,1},{1,0},{2,3},{3,2},{4,5},{5,4},{6,7},{7,6}} | collective-permute-start | bytes 8601608 | tf_op jit(solution)/shard_map/ppermute | solution.py:544
  1308.6 68.5 %collective-permute-start.18 = (bf16[320,4480]{1,0:T(8,128)(2,1)}, bf16[320,4480]{1,0:T(8,128)(2,1)}, u32[]{:S(2)}, u32[]{:S(2)}) collective-permute-start(bf16[320,4480]{1,0:T(8,128)(2,1)} %get-tuple-element.122), channel_id=1, source_target_pairs={{0,1},{1,0},{2,3},{3,2},{4,5},{5,4},{6,7},{7,6}} | collective-permute-start | bytes 8601608 | tf_op jit(solution)/shard_map/ppermute | solution.py:544
  1317.8 58.8 %collective-permute-start.22 = (bf16[896,1280]{1,0:T(8,128)(2,1)}, bf16[896,1280]{1,0:T(8,128)(2,1)}, u32[]{:S(2)}, u32[]{:S(2)}) collective-permute-start(bf16[896,1280]{1,0:T(8,128)(2,1)} %get-tuple-element.135), channel_id=1, source_target_pairs={{0,2},{2,0},{1,3},{3,1},{4,6},{6,4},{5,7},{7,5}} | collective-permute-start | bytes 6881288 | tf_op jit(solution)/shard_map/ppermute | solution.py:540
  1331.2 47.1 %collective-permute-start.17 = (bf16[320,4480]{1,0:T(8,128)(2,1)}, bf16[320,4480]{1,0:T(8,128)(2,1)}, u32[]{:S(2)}, u32[]{:S(2)}) collective-permute-start(bf16[320,4480]{1,0:T(8,128)(2,1)} %get-tuple-element.118), channel_id=1, source_target_pairs={{0,1},{1,0},{2,3},{3,2},{4,5},{5,4},{6,7},{7,6}} | collective-permute-start | bytes 8601608 | tf_op jit(solution)/shard_map/ppermute | solution.py:544
  1331.3 106.7 %collective-permute-start.15 = (bf16[320,4480]{1,0:T(8,128)(2,1)}, bf16[320,4480]{1,0:T(8,128)(2,1)}, u32[]{:S(2)}, u32[]{:S(2)}) collective-permute-start(bf16[320,4480]{1,0:T(8,128)(2,1)} %get-tuple-element.118), channel_id=1, source_target_pairs={{0,2},{2,0},{1,3},{3,1},{4,6},{6,4},{5,7},{7,5}} | collective-permute-start | bytes 8601608 | tf_op jit(solution)/shard_map/ppermute | solution.py:540
  1376.6 101.1 %collective-permute-start.14 = (bf16[320,4480]{1,0:T(8,128)(2,1)}, bf16[320,4480]{1,0:T(8,128)(2,1)}, u32[]{:S(2)}, u32[]{:S(2)}) collective-permute-start(bf16[320,4480]{1,0:T(8,128)(2,1)} %get-tuple-element.116), channel_id=1, source_target_pairs={{0,1},{1,0},{2,3},{3,2},{4,5},{5,4},{6,7},{7,6}} | collective-permute-start | bytes 8601608 | tf_op jit(solution)/shard_map/ppermute | solution.py:544
  1376.6 70.8 %collective-permute-start.23 = (bf16[896,1280]{1,0:T(8,128)(2,1)}, bf16[896,1280]{1,0:T(8,128)(2,1)}, u32[]{:S(2)}, u32[]{:S(2)}) collective-permute-start(bf16[896,1280]{1,0:T(8,128)(2,1)} %collective-permute-done.22.refs_0_), channel_id=1, source_target_pairs={{0,1},{1,0},{2,3},{3,2},{4,5},{5,4},{6,7},{7,6}} | collective-permute-start | bytes 6881288 | tf_op jit(solution)/shard_map/ppermute | solution.py:544
  1377.1 122.4 %collective-permute-start.8 = (bf16[320,4480]{1,0:T(8,128)(2,1)}, bf16[320,4480]{1,0:T(8,128)(2,1)}, u32[]{:S(2)}, u32[]{:S(2)}) collective-permute-start(bf16[320,4480]{1,0:T(8,128)(2,1)} %get-tuple-element.109), channel_id=1, source_target_pairs={{0,2},{2,0},{1,3},{3,1},{4,6},{6,4},{5,7},{7,5}} | collective-permute-start | bytes 8601608 | tf_op jit(solution)/shard_map/ppermute | solution.py:540
  1378.2 128.2 %collective-permute-start.11 = (bf16[320,4480]{1,0:T(8,128)(2,1)}, bf16[320,4480]{1,0:T(8,128)(2,1)}, u32[]{:S(2)}, u32[]{:S(2)}) collective-permute-start(bf16[320,4480]{1,0:T(8,128)(2,1)} %get-tuple-element.113), channel_id=1, source_target_pairs={{0,1},{1,0},{2,3},{3,2},{4,5},{5,4},{6,7},{7,6}} | collective-permute-start | bytes 8601608 | tf_op jit(solution)/shard_map/ppermute | solution.py:544
  1438.0 68.9 %collective-permute-start.10 = (bf16[320,4480]{1,0:T(8,128)(2,1)}, bf16[320,4480]{1,0:T(8,128)(2,1)}, u32[]{:S(2)}, u32[]{:S(2)}) collective-permute-start(bf16[320,4480]{1,0:T(8,128)(2,1)} %get-tuple-element.109), channel_id=1, source_target_pairs={{0,1},{1,0},{2,3},{3,2},{4,5},{5,4},{6,7},{7,6}} | collective-permute-start | bytes 8601608 | tf_op jit(solution)/shard_map/ppermute | solution.py:544
  1447.4 88.9 %collective-permute-start.16 = (bf16[320,4480]{1,0:T(8,128)(2,1)}, bf16[320,4480]{1,0:T(8,128)(2,1)S(1)}, u32[]{:S(2)}, u32[]{:S(2)}) collective-permute-start(bf16[320,4480]{1,0:T(8,128)(2,1)} %collective-permute-done.15.refs_0_), channel_id=1, source_target_pairs={{0,1},{1,0},{2,3},{3,2},{4,5},{5,4},{6,7},{7,6}} | collective-permute-start | bytes 8601608 | tf_op jit(solution)/shard_map/ppermute | solution.py:544
  1477.6 58.7 %collective-permute-start.34 = (bf16[672,1280]{1,0:T(8,128)(2,1)}, bf16[672,1280]{1,0:T(8,128)(2,1)}, u32[]{:S(2)}, u32[]{:S(2)}) collective-permute-start(bf16[672,1280]{1,0:T(8,128)(2,1)} %get-tuple-element.143), channel_id=1, source_target_pairs={{0,2},{2,0},{1,3},{3,1},{4,6},{6,4},{5,7},{7,5}} | collective-permute-start | bytes 5160968 | tf_op jit(solution)/shard_map/ppermute | solution.py:540
  1499.5 92.1 %collective-permute-start.9 = (bf16[320,4480]{1,0:T(8,128)(2,1)}, bf16[320,4480]{1,0:T(8,128)(2,1)}, u32[]{:S(2)}, u32[]{:S(2)}) collective-permute-start(bf16[320,4480]{1,0:T(8,128)(2,1)} %collective-permute-done.8.refs_0_), channel_id=1, source_target_pairs={{0,1},{1,0},{2,3},{3,2},{4,5},{5,4},{6,7},{7,6}} | collective-permute-start | bytes 8601608 | tf_op jit(solution)/shard_map/ppermute | solution.py:544
  1506.5 53.1 %collective-permute-start.31 = (bf16[448,1280]{1,0:T(8,128)(2,1)}, bf16[448,1280]{1,0:T(8,128)(2,1)}, u32[]{:S(2)}, u32[]{:S(2)}) collective-permute-start(bf16[448,1280]{1,0:T(8,128)(2,1)} %get-tuple-element.142), channel_id=1, source_target_pairs={{0,2},{2,0},{1,3},{3,1},{4,6},{6,4},{5,7},{7,5}} | collective-permute-start | bytes 3440648 | tf_op jit(solution)/shard_map/ppermute | solution.py:540
  1506.9 88.4 %collective-permute-start.36 = (bf16[672,1280]{1,0:T(8,128)(2,1)}, bf16[672,1280]{1,0:T(8,128)(2,1)}, u32[]{:S(2)}, u32[]{:S(2)}) collective-permute-start(bf16[672,1280]{1,0:T(8,128)(2,1)} %get-tuple-element.143), channel_id=1, source_target_pairs={{0,1},{1,0},{2,3},{3,2},{4,5},{5,4},{6,7},{7,6}} | collective-permute-start | bytes 5160968 | tf_op jit(solution)/shard_map/ppermute | solution.py:544
  1536.3 67.3 %collective-permute-start.35 = (bf16[672,1280]{1,0:T(8,128)(2,1)}, bf16[672,1280]{1,0:T(8,128)(2,1)}, u32[]{:S(2)}, u32[]{:S(2)}) collective-permute-start(bf16[672,1280]{1,0:T(8,128)(2,1)} %collective-permute-done.34.refs_0_), channel_id=1, source_target_pairs={{0,1},{1,0},{2,3},{3,2},{4,5},{5,4},{6,7},{7,6}} | collective-permute-start | bytes 5160968 | tf_op jit(solution)/shard_map/ppermute | solution.py:544
  1536.3 71.4 %collective-permute-start.33 = (bf16[448,1280]{1,0:T(8,128)(2,1)}, bf16[448,1280]{1,0:T(8,128)(2,1)}, u32[]{:S(2)}, u32[]{:S(2)}) collective-permute-start(bf16[448,1280]{1,0:T(8,128)(2,1)} %get-tuple-element.142), channel_id=1, source_target_pairs={{0,1},{1,0},{2,3},{3,2},{4,5},{5,4},{6,7},{7,6}} | collective-permute-start | bytes 3440648 | tf_op jit(solution)/shard_map/ppermute | solution.py:544
  1559.6 53.7 %collective-permute-start.32 = (bf16[448,1280]{1,0:T(8,128)(2,1)}, bf16[448,1280]{1,0:T(8,128)(2,1)}, u32[]{:S(2)}, u32[]{:S(2)}) collective-permute-start(bf16[448,1280]{1,0:T(8,128)(2,1)} %collective-permute-done.31.refs_0_), channel_id=1, source_target_pairs={{0,1},{1,0},{2,3},{3,2},{4,5},{5,4},{6,7},{7,6}} | collective-permute-start | bytes 3440648 | tf_op jit(solution)/shard_map/ppermute | solution.py:544
  (16 other events, 181.2 us)

commit v4 on v3

--- a/solution.py
+++ b/solution.py
@@ -19,7 +19,7 @@
 
 
 def params():
-    return pltpu.CompilerParams(vmem_limit_bytes=61 * 2**20)
+    return pltpu.CompilerParams(vmem_limit_bytes=67043328)
 
 
 def cost(flops, nbytes):
@@ -73,11 +73,44 @@
     return jnp.where(lax.broadcasted_iota(jnp.int32, a.shape, axis) < n, a, jnp.zeros_like(a))
 
 
-def first_kernel(at, x, wg, wu, wd, mg, vg, mu, vu, a_out, hid, s_out, q_out, h_out, half_gate, half_up, a, units, total, *, f):
-    j = pl.program_id(1)
+PIECES, EARLY = 5, 6
+
+
+def copied(at, step, moments, early, late, held, in_sems, out_sems):
+    cols = held.shape[2]
+    n = 2 * PIECES
+
+    def columns(block):
+        return pl.ds(pl.multiple_of(block * cols, 128), cols)
+
+    def came_in(p):
+        return pltpu.make_async_copy(moments[0].at[1, :, columns(0)], held.at[p % 2], in_sems.at[p % 2])
+
+    def went_out(p):
+        return pltpu.make_async_copy(held.at[p % 2], early.at[:, columns(0)], out_sems.at[p % 2])
+
+    pl.when((step >= 2) & (step < n + 2))(lambda: went_out(step).wait())
+    for which in range(2):
+        for rep in range(2):
+
+            @pl.when((step >= which * PIECES) & (step < (which + 1) * PIECES) & (at[2] == rep))
+            def _(source=moments[2 * which + rep], block=step - which * PIECES):
+                pltpu.make_async_copy(source.at[1, :, columns(block)], held.at[step % 2], in_sems.at[step % 2]).start()
+
+    before = step - 1
+    pl.when((before >= 0) & (before < n))(lambda: came_in(before).wait())
+    for low, high, target in ((0, EARLY, early), (EARLY, n, late)):
+
+        @pl.when((before >= low) & (before < high))
+        def _(target=target, block=before - low):
+            pltpu.make_async_copy(held.at[before % 2], target.at[:, columns(block)], out_sems.at[before % 2]).start()
+
+
+def first_kernel(at, x, wg, wu, wd, *refs, f):
+    moments, (a_out, hid, s_out, q_out, h_out, early, late, a, units, total, *held) = refs[:4], refs[4:]
+    i, j = pl.program_id(0), pl.program_id(1)
     left = f - j * UNITS
-    half_gate[...] = jnp.where(at[2] == 0, mg[...], vg[...])
-    half_up[...] = jnp.where(at[2] == 0, mu[...], vu[...])
+    copied(at, i * pl.num_programs(1) + j, moments, early, late, *held)
 
     @pl.when(j == 0)
     def _():
@@ -107,20 +140,15 @@
     m = moments[0]
     t, d = x.shape
     f = w_gate.shape[2]
-    n = pl.cdiv(f, UNITS)
     wide = pl.BlockSpec((TOKENS, UNITS), lambda i, j, at: (i, j))
     weight = pl.BlockSpec((None, d, UNITS), lambda i, j, at: (0, 0, j))
     state = pl.BlockSpec((TOKENS, d), lambda i, j, at: (i, 0))
-    cols = UNITS * TOKENS // t
-
-    def moment(rep):
-        return pl.BlockSpec((None, m.shape[1], cols), lambda i, j, at: (1, 0, jnp.where(at[2] == rep, i * n + j, 0)))
-
     return call(
         functools.partial(first_kernel, f=f),
         at,
-        (t // TOKENS, n),
-        [state, weight, weight, pl.BlockSpec((None, UNITS, d), lambda i, j, at: (0, j, 0)), *[moment(0), moment(1)] * 2],
+        (t // TOKENS, pl.cdiv(f, UNITS)),
+        [state, weight, weight, pl.BlockSpec((None, UNITS, d), lambda i, j, at: (0, j, 0))]
+        + [pl.BlockSpec(memory_space=pl.ANY)] * 4,
         [
             pl.BlockSpec((d, TOKENS), lambda i, j, at: (0, i)),
             pl.BlockSpec((UNITS, TOKENS), lambda i, j, at: (j, i)),
@@ -128,24 +156,33 @@
             wide,
             state,
         ]
-        + [pl.BlockSpec((m.shape[1], cols), lambda i, j, at: (0, i * n + j))] * 2,
-        [out((d, t)), out((f, t)), out((t, f), F32), out((t, f), F32), out((t, d))] + [out(m.shape[1:], F32)] * 2,
+        + [pl.BlockSpec(memory_space=pl.ANY)] * 2,
+        [out((d, t)), out((f, t)), out((t, f), F32), out((t, f), F32), out((t, d))]
+        + [out((m.shape[1], n * f // PIECES), F32) for n in (EARLY, 2 * PIECES - EARLY)],
         (x, w_gate, w_up, w_down, *moments),
         6 * t * d * f,
         190e6,
-        scratch=[pltpu.VMEM((TOKENS, d), BF), pltpu.VMEM((TOKENS, UNITS), BF), pltpu.VMEM((TOKENS, d), F32)],
+        scratch=[
+            pltpu.VMEM((TOKENS, d), BF),
+            pltpu.VMEM((TOKENS, UNITS), BF),
+            pltpu.VMEM((TOKENS, d), F32),
+            pltpu.VMEM((2, m.shape[1], f // PIECES), F32),
+            pltpu.SemaphoreType.DMA((2,)),
+            pltpu.SemaphoreType.DMA((2,)),
+        ],
     )
 
 
 def second_units(a, dy, wg, wu, wd, hid, dgu, left):
     for c in chunks(UNITS):
-        gate, up = dot(a[...], wg[:, c], NN), dot(a[...], wu[:, c], NN)
-        back = dot(dy[...], wd[c, :], NT).astype(BF).astype(F32)
-        sig = sigmoid(gate)
-        silu = gate * sig
-        hid[c, :] = (silu * up).astype(BF).T
-        dgu[0, :, c] = only((back * (up * (sig + silu * (1 - sig)))).astype(BF), left - c.start, 1)
-        dgu[1, :, c] = only((back * silu).astype(BF), left - c.start, 1)
+        for r in chunks(a.shape[0], a.shape[0] // (1 if c.start == 0 else 4)):
+            gate, up = dot(a[r, :], wg[:, c], NN), dot(a[r, :], wu[:, c], NN)
+            back = dot(dy[r, :], wd[c, :], NT).astype(BF).astype(F32)
+            sig = sigmoid(gate)
+            silu = gate * sig
+            hid[c, r] = (silu * up).astype(BF).T
+            dgu[0, r, c] = only((back * (up * (sig + silu * (1 - sig)))).astype(BF), left - c.start, 1)
+            dgu[1, r, c] = only((back * silu).astype(BF), left - c.start, 1)
 
 
 def second_kernel(at, h, dy, wg, wu, wd, a_before, dgu_before, a_out, dgu, hid, a, *, f):
@@ -189,7 +226,7 @@
     t, d = h.shape
     f = w_gate.shape[2]
     far = before is not None
-    bt = TOKENS // 2 if far else TOKENS
+    bt = TOKENS
     weight = pl.BlockSpec((None, d, UNITS), lambda i, j, at: (1, 0, j))
     state = pl.BlockSpec((bt, d), lambda i, j, at: (i, 0))
     which = (lambda at: 1 - at[0]) if far else (lambda at: at[0])
@@ -378,48 +415,48 @@
     )
 
 
-def squares_kernel(keep, far, o, keep_in, far_in, sems, *, n):
-    rows = keep_in.shape[1] // n
-
-    def copies(i):
+def squares_kernel(*refs, shapes, n):
+    arrays, o, held, sems = refs[: len(shapes)], refs[len(shapes)], refs[len(shapes) + 1 : -1], refs[-1]
+
+    def copies(k, i):
+        rows = shapes[k][1] // n
         r = pl.ds(i * rows, rows)
-        which = pl.ds(0, keep_in.shape[0])
-        return (
-            pltpu.make_async_copy(keep.at[which, r], keep_in.at[:, r], sems.at[0, i]),
-            pltpu.make_async_copy(far.at[which, r], far_in.at[:, r], sems.at[1, i]),
-        )
-
-    for i in range(n):
-        for copy in copies(i):
-            copy.start()
+        return pltpu.make_async_copy(arrays[k].at[pl.ds(0, shapes[k][0]), r], held[k].at[:, r], sems.at[k, i])
+
+    everything = [(k, i) for k in range(0, len(shapes), 2) for i in range(n)]
+    for k, i in everything:
+        copies(k, i).start()
+        copies(k + 1, i).start()
     o[...] = jnp.zeros_like(o)
-    for i in range(n):
-        for copy in copies(i):
-            copy.wait()
-
-        def add(k, _, start=i * rows):
-            which, k = k // (rows // 16), k % (rows // 16)
-            r = pl.ds(pl.multiple_of(start + k * 16, 16), 16)
-            g = (keep_in[which, r, :] + far_in[which, r, :].astype(F32)).astype(BF).astype(F32)
+    for k, i in everything:
+        copies(k, i).wait()
+        copies(k + 1, i).wait()
+        rows = shapes[k][1] // n
+
+        def add(t, _, k=k, start=i * rows, size=rows // 16):
+            r = pl.ds(pl.multiple_of(start + t % size * 16, 16), 16)
+            g = (held[k][t // size, r, :] + held[k + 1][t // size, r, :].astype(F32)).astype(BF).astype(F32)
             g = jnp.sum((g * g).reshape(-1, 8, g.shape[-1]), 0)
             o[...] += sum(g[:, c] for c in chunks(g.shape[1], 128))
 
-        lax.fori_loop(0, keep_in.shape[0] * (rows // 16), add, None)
-
-
-def sum_of_squares(keep, far, first):
+        lax.fori_loop(0, shapes[k][0] * (rows // 16), add, None)
+
+
+def sum_of_squares(*pairs):
     n = 5
-    shape = (first, *keep.shape[1:])
+    arrays = [a for pair in pairs for a in pair[:2]]
+    shapes = [(pair[2], *a.shape[1:]) for pair in pairs for a in pair[:2]]
+    held = [pltpu.VMEM(shape, a.dtype) for shape, a in zip(shapes, arrays, strict=True)]
     return pl.pallas_call(
-        functools.partial(squares_kernel, n=n),
-        in_specs=[pl.BlockSpec(memory_space=pl.ANY)] * 2,
+        functools.partial(squares_kernel, shapes=shapes, n=n),
+        in_specs=[pl.BlockSpec(memory_space=pl.ANY)] * len(arrays),
         out_specs=pl.BlockSpec(memory_space=pltpu.VMEM),
         out_shape=out((8, 128), F32),
-        scratch_shapes=[pltpu.VMEM(shape, F32), pltpu.VMEM(shape, BF), pltpu.SemaphoreType.DMA((2, n))],
+        scratch_shapes=[*held, pltpu.SemaphoreType.DMA((len(arrays), n))],
         compiler_params=params(),
-        cost_estimate=cost(1e9, 8e6),
+        cost_estimate=cost(1e9, 4e6 * len(arrays)),
         name="squares",
-    )(keep, far)
+    )(*arrays)
 
 
 def updated(g, w, m, v):
@@ -464,33 +501,48 @@
     )
 
 
-def adam_far_kernel(at, factor, keep, far, w, crossed, handed, before, w_out, w_new):
-    def rows(r):
-        m, v = jnp.where(at[2] == 0, crossed[r, :], handed[r, :]), jnp.where(at[2] == 0, handed[r, :], crossed[r, :])
-        w_out[r, :], _, _ = updated(gradient(factor, keep, far, r), w[r, :], m, v)
-        w_new[r, :] = w_out[r, :]
-
-    loop(w.shape[0] // 16, 16, rows)
-
-
-def adam_far(at, factor, layer, which, keep, far, w, crossed, handed, before):
+def adam_far_kernel(at, factor, keep, far, w, *refs, start):
+    *moments, before, w_out, w_new = refs
+    first = at[2] == 0
+
+    def update(crossed, handed):
+        def rows(r):
+            m, v = jnp.where(first, crossed[r, :], handed[r, :]), jnp.where(first, handed[r, :], crossed[r, :])
+            w_out[r, :], _, _ = updated(gradient(factor, keep, far, r), w[r, :], m, v)
+            w_new[r, :] = w_out[r, :]
+
+        loop(w.shape[0] // 32, 32, rows)
+
+    if len(moments) == 2:
+        update(*moments)
+    else:
+        early = pl.program_id(1) + start < EARLY
+        pl.when(early)(lambda: update(*moments[:2]))
+        pl.when(~early)(lambda: update(*moments[2:]))
+
+
+def adam_far(at, factor, layer, which, start, keep, far, w, moments, before):
     rows, cols = keep.shape[1:]
     n = 2
-    br = rows // n
-    grad = pl.BlockSpec((None, br, cols), lambda i, at: (which, i, 0))
-    flat = pl.BlockSpec((br, cols), lambda i, at: (i, 0))
-    there = pl.BlockSpec((None, br, cols), lambda i, at: (layer, (2 * (1 - at[0]) + at[1]) * n + i, 0))
+    br, bc = rows // n, cols // PIECES
+    grad = pl.BlockSpec((None, br, bc), lambda i, j, at: (which, i, j))
+    flat = pl.BlockSpec((br, bc), lambda i, j, at: (i, j))
+    there = pl.BlockSpec((None, br, bc), lambda i, j, at: (layer, (2 * (1 - at[0]) + at[1]) * n + i, j))
+    early = pl.BlockSpec((br, bc), lambda i, j, at: (i, jnp.minimum(j + start, EARLY - 1)))
+    late = pl.BlockSpec((br, bc), lambda i, j, at: (i, jnp.maximum(j + start - EARLY, 0)))
+    specs = ([early] * 2 if start < EARLY else []) + ([late] * 2 if start + PIECES > EARLY else [])
+    moments = moments[: len(specs)]
     return call(
-        adam_far_kernel,
+        functools.partial(adam_far_kernel, start=start),
         at,
-        (n,),
-        [pl.BlockSpec(memory_space=pltpu.SMEM), grad, grad, there, flat, flat, pl.BlockSpec(memory_space=pl.ANY)],
+        (n, PIECES),
+        [pl.BlockSpec(memory_space=pltpu.SMEM), grad, grad, there, *specs, pl.BlockSpec(memory_space=pl.ANY)],
         [flat, there],
         [out((rows, cols)), out(w.shape)],
-        [factor, keep, far, w, crossed, handed, before],
+        [factor, keep, far, w, *moments, before],
         1e9,
         30e6,
-        input_output_aliases={7: 1},
+        input_output_aliases={5 + len(specs): 1},
     )
 
 
@@ -555,14 +607,14 @@
 
     dy_far = across(dy)
     moments = m_gate, v_gate, m_up, v_up
-    a1, hid1, s1, q1, h1, half_gate, half_up = first(at, x, w_gate, w_up, w_down, moments)
+    a1, hid1, s1, q1, h1, early, late = first(at, x, w_gate, w_up, w_down, moments)
     h1_far = across(h1)
 
     def brought(half):
         crossed = across(half)
         return crossed, lax.ppermute(crossed, "rep", [(0, 1), (1, 0)])
 
-    far_moments = {"gate": brought(half_gate), "up": brought(half_up)}
+    far_moments = (*brought(early), *brought(late))
     a2, dgu2, hid2, d1 = second(at, h1, dy, w_gate, w_up, w_down)
 
     dgu1, theirs = hidden_back(at, w_down, d1, s1, q1, blocks(a1))
@@ -585,12 +637,12 @@
     send, keep_down2 = grad_tall(at, pairs, on(True, False), on(True, True), half=7)
     far_down2 = sibling(send)
     keep_down1, far_down1, keep_down2, far_down2 = (a[None] for a in (keep_down1, far_down1, keep_down2, far_down2))
-    sums = [sum_of_squares(keep_wide1, far_wide1, 2), sum_of_squares(keep_down1, far_down1, 1)]
-    sums.append(sum_of_squares(keep_wide2, after(far_wide2, *sums), 2))
-    far_down2 = after(far_down2, *sums)
-    squares = jnp.sum(sum(sums) + sum_of_squares(keep_down2, far_down2, 1))
-    squares = lax.psum(squares, "dp")
-    factor = jnp.minimum(1.0, 0.5 * lax.rsqrt(squares / (6 * d * f) + 1e-30)).reshape(1)
+    squares = sum_of_squares((keep_wide1, far_wide1, 2), (keep_down1, far_down1, 1), (keep_wide2, far_wide2, 2))
+    far_down2 = after(far_down2, squares)
+    squares = squares + sum_of_squares((keep_down2, far_down2, 1))
+    squares = squares + sibling(squares)
+    squares = squares + across(squares)
+    factor = jnp.minimum(1.0, 0.5 * lax.rsqrt(jnp.sum(squares) / (6 * d * f) + 1e-30)).reshape(1)
 
     weights = {"gate": (w_gate, m_gate, v_gate), "up": (w_up, m_up, v_up), "down": (w_down, m_down, v_down)}
     grads = {
@@ -619,29 +671,28 @@
         own = update(which, part)
         return across(own), sibling(own)
 
-    def settle(n, away, beside):
-        which, part = PARTS[n]
-        put(which, part, (on(True, False), beside))
-        put(which, part, (on(False, True), away))
-        put(which, part, (on(False, False), sibling(away)))
+    def settle(sent):
+        for n, (_, beside) in sent.items():
+            put(*PARTS[n], (on(True, False), beside))
+        for n, (away, _) in sent.items():
+            put(*PARTS[n], (on(False, True), away))
+            put(*PARTS[n], (on(False, False), sibling(away)))
 
     def both_blocks(name, which):
         part = (0, 2, 2)
         own = update(name + "1", part)
         *moments, w = new[name]
-        arrays = keep_wide2, far_wide2, weights[name][0], *far_moments[name]
-        away, w = adam_far(at, factor, 1, which, *arrays, w)
+        arrays = keep_wide2, far_wide2, weights[name][0], far_moments
+        away, w = adam_far(at, factor, 1, which, (which - 2) * PIECES, *arrays, w)
         new[name] = [*moments, w]
         beside, last = sibling(own), sibling(away)
         put(name + "1", part, (on(True, False), beside), (on(False, False), last))
 
-    sent = [send(n) for n in range(len(PARTS) - 2)]
+    sent = {n: send(n) for n in range(len(PARTS) - 2)}
     both_blocks("gate", 2)
     both_blocks("up", 3)
-    for n, parts in enumerate(sent):
-        settle(n, *parts)
-    for n, parts in enumerate([send(n) for n in range(len(sent), len(PARTS))], len(sent)):
-        settle(n, *parts)
+    settle(sent)
+    settle({n: send(n) for n in range(len(sent), len(PARTS))})
     return tuple(new[name][i] for i in (2, 0, 1) for name in weights)
 
 

time: 1620 us -> 1460 us (0.901)
  waiting for transfers between devices: 715 us -> 567 us
    ppermute x13 -> x14, waiting for transfers between devices: 712 us -> 559 us  [across(): return lax.ppermute(a, 'dp', ACROSS)]
  transfers between devices with their start and end apart: 37 -> 39, of which waited for: 14 -> 15; matrix products, arithmetic and copies ran while one was open for 0% -> 0% of each run, Pallas kernels for 21% -> 37%
where the time goes in v4:
time: 1460 us; the launch traced here: 1450 us
  Pallas kernels  850 us (58%)
  waiting for transfers between devices  567 us (39%)
  starting transfers between devices  29.6 us (2%)
    pallas_call x41, Pallas kernels, call(): pl.pallas_call(kernel, grid_spec=pltpu.PrefetchScalarGridSpec(num_scalar_...  594 us
    ppermute x14, waiting for transfers between devices, across(): return lax.ppermute(a, 'dp', ACROSS)  559 us
    pallas_call x2, Pallas kernels, second(): pl.pallas_call(functools.partial(second_kernel if far else second_back_ke...  237 us
  transfers between devices with their start and end apart: 39, of which 15 were waited for; matrix products, arithmetic and copies ran while one was open for 0% of the time, Pallas kernels for 37%

profile of v4, /device:TPU:0, one launch (start us, length us, event | category | flops | bytes accessed | tf_op | source)
XLA Modules:
  0.0 1451.1 jit_solution(16441975994870331948)
XLA Ops:
  1.3 94.3 %shard_map.178 = (bf16[1280,2048]{1,0:T(8,128)(2,1)}, bf16[4480,2048]{1,0:T(8,128)(2,1)}, f32[2048,4480]{1,0:T(8,128)}, f32[2048,4480]{1,0:T(8,128)}, bf16[2048,...) custom-call(s32[3]{0:T(128)} %pad_add_fusion.at, bf16[2048,1280]{1,0:T(8,128)(2,1)} %bitcast.21, ...), custom_call_target="tpu_custom_call" | custom-call | flops 70464307200 | bytes 190000000 | tf_op jit(solution)/shard_map/pallas_call | solution.py:38
  95.6 145.8 %second_back.1 = (bf16[2,1280,2048]{2,1,0:T(8,128)(2,1)}, bf16[2,2,2048,4480]{3,2,1,0:T(8,128)(2,1)}, bf16[4480,2048]{1,0:T(8,128)(2,1)}, bf16[2048,1280]{1,0:T(8,128)(2,1)}) custom-call(s32[3]{0:T(128)} %pad_add_fusion.at, bf16[2048,1280]{1,0:T(8,128)(2,1)} %get-tuple-element.80.h, bf16[2048,1280]{1,0:T(8,128)(2,1)} %bitcast.22, bf16[2,1280,4480]{2,1,0:T(8,128)(2,1)} %w.15, ...), custom_call_target="tpu_custom_call" | custom-call | flops 117440512000 | bytes 130000000 | tf_op jit(solution)/shard_map/second_back/pallas_call | solution.py:251
  241.3 63.8 %shard_map.179 = (bf16[2,2048,4480]{2,1,0:T(8,128)(2,1)}, bf16[2,2,320,4480]{3,2,1,0:T(8,128)(2,1)}) custom-call(s32[3]{0:T(128)} %pad_add_fusion.at, bf16[2,4480,1280]{2,1,0:T(8,128)(2,1)} %w.23, bf16[2048,1280]{1,0:T(8,128)(2,1)} %get-tuple-element.87.d.refs_1_, f32[2048,4480]{1,0:T(8,128)} %get-tuple-element.82.s, f32[2048,4480]{1,0:T(8,128)} %get-tuple-element.83.q, ...), custom_call_target="tpu_custom_call" | custom-call | flops 46976204800 | bytes 160000000 | tf_op jit(solution)/shard_map/pallas_call | solution.py:38
  305.8 18.3 %shard_map.180 = bf16[2,1120,1280]{2,1,0:T(8,128)(2,1)} custom-call(s32[3]{0:T(128)} %pad_add_fusion.at, bf16[4,1120,2048]{2,1,0:T(8,128)(2,1)} %bitcast.26, bf16[2048,1280]{1,0:T(8,128)(2,1)} %get-tuple-element.87.d.refs_1_), custom_call_target="tpu_custom_call" | custom-call | flops 11744051200 | bytes 60000000 | tf_op jit(solution)/shard_map/pallas_call | solution.py:38
  329.3 33.8 %shard_map.181 = (bf16[2,320,4480]{2,1,0:T(8,128)(2,1)}, f32[2,320,4480]{2,1,0:T(8,128)}) custom-call(s32[3]{0:T(128)} %pad_add_fusion.at, bf16[4,320,2048]{2,1,0:T(8,128)(2,1)} %bitcast.31, bf16[4,320,2048]{2,1,0:T(8,128)(2,1)} %bitcast.32, bf16[2,2048,4480]{2,1,0:T(8,128)(2,1)} %get-tuple-element.84.right, bf16[2,2,320,4480]{3,2,1,0:T(8,128)(2,1)} %collective-permute-done.got), custom_call_target="tpu_custom_call" | custom-call | flops 23488102400 | bytes 60000000 | tf_op jit(solution)/shard_map/pallas_call | solution.py:38
  363.0 22.0 %shard_map.182 = (bf16[1120,1280]{1,0:T(8,128)(2,1)}, f32[1120,1280]{1,0:T(8,128)}) custom-call(s32[3]{0:T(128)} %pad_add_fusion.at, bf16[4,1120,2048]{2,1,0:T(8,128)(2,1)} %bitcast.27, bf16[2048,1280]{1,0:T(8,128)(2,1)} %get-tuple-element.87.d.refs_1_, bf16[2,1120,1280]{2,1,0:T(8,128)(2,1)} %collective-permute-done.2.refs_2_), custom_call_target="tpu_custom_call" | custom-call | flops 11744051200 | bytes 60000000 | tf_op jit(solution)/shard_map/pallas_call | solution.py:38
  385.0 56.4 %collective-permute-done.4.h = bf16[2048,1280]{1,0:T(8,128)(2,1)} collective-permute-done((bf16[2048,1280]{1,0:T(8,128)(2,1)}, bf16[2048,1280]{1,0:T(8,128)(2,1)}, u32[]{:S(2)}, u32[]{:S(2)}) %collective-permute-start.4) | collective-permute-done | bytes 5242912 | tf_op jit(solution)/shard_map/ppermute | solution.py:592
  441.5 112.4 %collective-permute-done.5.dy.refs_3_ = bf16[2048,1280]{1,0:T(8,128)(2,1)} collective-permute-done((bf16[2048,1280]{1,0:T(8,128)(2,1)}, bf16[2048,1280]{1,0:T(8,128)(2,1)}, u32[]{:S(2)}, u32[]{:S(2)}) %collective-permute-start.5) | collective-permute-done | bytes 5242912 | tf_op jit(solution)/shard_map/ppermute | solution.py:592
  553.8 91.1 %second.1 = (bf16[2,1280,2048]{2,1,0:T(8,128)(2,1)}, bf16[2,2,2048,4480]{3,2,1,0:T(8,128)(2,1)}, bf16[4480,2048]{1,0:T(8,128)(2,1)}) custom-call(s32[3]{0:T(128)} %pad_add_fusion.at, bf16[2048,1280]{1,0:T(8,128)(2,1)} %collective-permute-done.4.h, ...), custom_call_target="tpu_custom_call", output_to_operand_aliasing={{0}: (6, {}), {1}: (7, {})} | custom-call | flops 70464307200 | bytes 130000000 | tf_op jit(solution)/shard_map/second/pallas_call | solution.py:251
  644.9 113.0 %shard_map.183 = (bf16[4,320,4480]{2,1,0:T(8,128)(2,1)}, f32[4,320,4480]{2,1,0:T(8,128)}) custom-call(s32[3]{0:T(128)} %pad_add_fusion.at, bf16[2,1280,2048]{2,1,0:T(8,128)(2,1)} %get-tuple-element.97.left0.left1, bf16[2,1280,2048]{2,1,0:T(8,128)(2,1)} %get-tuple-element.97.left0.left1, bf16[2,2,2048,4480]{3,2,1,0:T(8,128)(2,1)} %get-tuple-element.98.right0.right1, ...), custom_call_target="tpu_custom_call" | custom-call | flops 93952409600 | bytes 120000000 | tf_op jit(solution)/shard_map/pallas_call | solution.py:38
  763.4 96.7 %collective-permute-done.21.refs_2_ = f32[320,3584]{1,0:T(8,128)} collective-permute-done((f32[320,3584]{1,0:T(8,128)}, f32[320,3584]{1,0:T(8,128)}, u32[]{:S(2)}, u32[]{:S(2)}) %collective-permute-start.21) | collective-permute-done | bytes 4587552 | tf_op jit(solution)/shard_map/ppermute | solution.py:592
  862.1 33.8 %shard_map.184 = (bf16[1120,1280]{1,0:T(8,128)(2,1)}, f32[1120,1280]{1,0:T(8,128)}) custom-call(s32[3]{0:T(128)} %pad_add_fusion.at, bf16[4,1120,2048]{2,1,0:T(8,128)(2,1)} %bitcast.25, bf16[2048,1280]{1,0:T(8,128)(2,1)} %bitcast.24, bf16[4,1120,2048]{2,1,0:T(8,128)(2,1)} %bitcast.28, bf16[2048,1280]{1,0:T(8,128)(2,1)} %collective-permute-done.5.dy.refs_3_), custom_call_target="tpu_custom_call" | custom-call | flops 23488102400 | bytes 60000000 | tf_op jit(solution)/shard_map/pallas_call | solution.py:38
  895.9 148.3 %collective-permute-done.3 = bf16[1120,1280]{1,0:T(8,128)(2,1)} collective-permute-done((bf16[1120,1280]{1,0:T(8,128)(2,1)}, bf16[1120,1280]{1,0:T(8,128)(2,1)}, u32[]{:S(2)}, u32[]{:S(2)}) %collective-permute-start.3) | collective-permute-done | bytes 2867232 | tf_op jit(solution)/shard_map/ppermute | solution.py:592
  1044.2 14.9 %squares.2 = f32[8,128]{1,0:T(8,128)} custom-call(f32[2,320,4480]{2,1,0:T(8,128)} %get-tuple-element.89.refs_0_.keep, bf16[2,320,4480]{2,1,0:T(8,128)(2,1)} %collective-permute-done.1.refs_1_.far, f32[1,1120,1280]{2,1,0:T(8,128)} %bitcast.18, bf16[1,1120,1280]{2,1,0:T(8,128)(2,1)} %bitcast.8.refs_3_.far, f32[4,320,4480]{2,1,0:T(8,128)} %get-tuple-element.99.refs_4_.keep, ...), custom_call_target="tpu_custom_call" | custom-call | flops 1000000000 | bytes 24000000 | tf_op jit(solution)/shard_map/squares/pallas_call | solution.py:450
  1059.1 4.6 squares.3
  1078.3 12.7 shard_map.201
  1091.5 15.4 %shard_map.192 = (bf16[320,4480]{1,0:T(8,128)(2,1)}, f32[2,320,4480]{2,1,0:T(8,128)}, f32[2,320,4480]{2,1,0:T(8,128)}, bf16[2,1280,4480]{2,1,0:T(8,128)(2,1)}) custom-call(s32[3]{0:T(128)} %pad_add_fusion.at, f32[1]{0:T(128)} %bitcast.13.factor, f32[2,320,4480]{2,1,0:T(8,128)} %get-tuple-element.89.refs_0_.keep, ...), custom_call_target="tpu_custom_call" | custom-call | flops 1000000000 | bytes 12000000 | tf_op jit(solution)/shard_map/pallas_call | solution.py:38
  1106.9 15.5 %shard_map.193 = (bf16[320,4480]{1,0:T(8,128)(2,1)}, f32[2,320,4480]{2,1,0:T(8,128)}, f32[2,320,4480]{2,1,0:T(8,128)}, bf16[2,1280,4480]{2,1,0:T(8,128)(2,1)}) custom-call(s32[3]{0:T(128)} %pad_add_fusion.at, f32[1]{0:T(128)} %bitcast.13.factor, ...), custom_call_target="tpu_custom_call", output_to_operand_aliasing={{1}: (7, {}), {2}: (8, {}), {3}: (9, {})} | custom-call | flops 1000000000 | bytes 12000000 | tf_op jit(solution)/shard_map/pallas_call | solution.py:38
  1122.4 15.5 %shard_map.194 = (bf16[320,4480]{1,0:T(8,128)(2,1)}, bf16[2,1280,4480]{2,1,0:T(8,128)(2,1)}) custom-call(s32[3]{0:T(128)} %pad_add_fusion.at, f32[1]{0:T(128)} %bitcast.13.factor, f32[4,320,4480]{2,1,0:T(8,128)} %get-tuple-element.99.refs_4_.keep, bf16[4,320,4480]{2,1,0:T(8,128)(2,1)} %collective-permute-done.6.refs_5_.far, ...), custom_call_target="tpu_custom_call", output_to_operand_aliasing={{1}: (9, {})} | custom-call | flops 1000000000 | bytes 30000000 | tf_op jit(solution)/shard_map/pallas_call | solution.py:38
  1149.8 52.9 %collective-permute-done.26.refs_0_ = bf16[112,1280]{1,0:T(8,128)(2,1)S(1)} collective-permute-done((bf16[112,1280]{1,0:T(8,128)(2,1)}, bf16[112,1280]{1,0:T(8,128)(2,1)S(1)}, u32[]{:S(2)}, u32[]{:S(2)}) %collective-permute-start.26) | collective-permute-done | bytes 286752 | tf_op jit(solution)/shard_map/ppermute | solution.py:592
  1208.6 15.4 %shard_map.185 = (bf16[320,4480]{1,0:T(8,128)(2,1)}, f32[2,320,4480]{2,1,0:T(8,128)}, f32[2,320,4480]{2,1,0:T(8,128)}, bf16[2,1280,4480]{2,1,0:T(8,128)(2,1)}) custom-call(s32[3]{0:T(128)} %pad_add_fusion.at, f32[1]{0:T(128)} %bitcast.13.factor, f32[2,320,4480]{2,1,0:T(8,128)} %get-tuple-element.89.refs_0_.keep, ...), custom_call_target="tpu_custom_call" | custom-call | flops 1000000000 | bytes 12000000 | tf_op jit(solution)/shard_map/pallas_call | solution.py:38
  1224.0 15.5 %shard_map.186 = (bf16[320,4480]{1,0:T(8,128)(2,1)}, f32[2,320,4480]{2,1,0:T(8,128)}, f32[2,320,4480]{2,1,0:T(8,128)}, bf16[2,1280,4480]{2,1,0:T(8,128)(2,1)}) custom-call(s32[3]{0:T(128)} %pad_add_fusion.at, f32[1]{0:T(128)} %bitcast.13.factor, ...), custom_call_target="tpu_custom_call", output_to_operand_aliasing={{1}: (7, {}), {2}: (8, {}), {3}: (9, {})} | custom-call | flops 1000000000 | bytes 12000000 | tf_op jit(solution)/shard_map/pallas_call | solution.py:38
  1239.5 14.8 %shard_map.187 = (bf16[320,4480]{1,0:T(8,128)(2,1)}, bf16[2,1280,4480]{2,1,0:T(8,128)(2,1)}) custom-call(s32[3]{0:T(128)} %pad_add_fusion.at, f32[1]{0:T(128)} %bitcast.13.factor, f32[4,320,4480]{2,1,0:T(8,128)} %get-tuple-element.99.refs_4_.keep, bf16[4,320,4480]{2,1,0:T(8,128)(2,1)} %collective-permute-done.6.refs_5_.far, ...), custom_call_target="tpu_custom_call", output_to_operand_aliasing={{1}: (7, {})} | custom-call | flops 1000000000 | bytes 30000000 | tf_op jit(solution)/shard_map/pallas_call | solution.py:38
  1255.0 17.1 %collective-permute-done.17.refs_0_ = bf16[320,4480]{1,0:T(8,128)(2,1)} collective-permute-done((bf16[320,4480]{1,0:T(8,128)(2,1)}, bf16[320,4480]{1,0:T(8,128)(2,1)}, u32[]{:S(2)}, u32[]{:S(2)}) %collective-permute-start.17) | collective-permute-done | bytes 2867232 | tf_op jit(solution)/shard_map/ppermute | solution.py:592
  1277.3 4.5 shard_map.204.refs_1_
  1300.2 11.4 shard_map.211
  1313.4 20.1 %collective-permute-done.10.refs_0_ = bf16[320,4480]{1,0:T(8,128)(2,1)} collective-permute-done((bf16[320,4480]{1,0:T(8,128)(2,1)}, bf16[320,4480]{1,0:T(8,128)(2,1)}, u32[]{:S(2)}, u32[]{:S(2)}) %collective-permute-start.10) | collective-permute-done | bytes 2867232 | tf_op jit(solution)/shard_map/ppermute | solution.py:592
  1333.5 7.0 shard_map.212
  1342.5 27.9 %collective-permute-done.35.refs_0_ = bf16[672,1280]{1,0:T(8,128)(2,1)} collective-permute-done((bf16[672,1280]{1,0:T(8,128)(2,1)}, bf16[672,1280]{1,0:T(8,128)(2,1)}, u32[]{:S(2)}, u32[]{:S(2)}) %collective-permute-start.35) | collective-permute-done | bytes 1720352 | tf_op jit(solution)/shard_map/ppermute | solution.py:592
  1370.9 23.5 %collective-permute-done.33.refs_0_ = bf16[448,1280]{1,0:T(8,128)(2,1)} collective-permute-done((bf16[448,1280]{1,0:T(8,128)(2,1)}, bf16[448,1280]{1,0:T(8,128)(2,1)}, u32[]{:S(2)}, u32[]{:S(2)}) %collective-permute-start.33) | collective-permute-done | bytes 1146912 | tf_op jit(solution)/shard_map/ppermute | solution.py:592
  1394.4 6.8 shard_map.195.refs_1_
  1408.5 6.8 shard_map.188.refs_1_
  (105 shorter events, 117.9 us)
Async XLA Ops:
  305.2 24.1 %collective-permute-start = (bf16[2,2,320,4480]{3,2,1,0:T(8,128)(2,1)}, bf16[2,2,320,4480]{3,2,1,0:T(8,128)(2,1)}, u32[]{:S(2)}, u32[]{:S(2)}) collective-permute-start(bf16[2,2,320,4480]{3,2,1,0:T(8,128)(2,1)} %get-tuple-element.85), channel_id=1, source_target_pairs={{0,1},{1,0},{2,3},{3,2},{4,5},{5,4},{6,7},{7,6}} | collective-permute-start | bytes 34406408 | tf_op jit(solution)/shard_map/ppermute | solution.py:596
  324.1 38.9 %collective-permute-start.2 = (bf16[2,1120,1280]{2,1,0:T(8,128)(2,1)}, bf16[2,1120,1280]{2,1,0:T(8,128)(2,1)}, u32[]{:S(2)}, u32[]{:S(2)}) collective-permute-start(bf16[2,1120,1280]{2,1,0:T(8,128)(2,1)} %shard_map.180), channel_id=1, source_target_pairs={{0,1},{1,0},{2,3},{3,2},{4,5},{5,4},{6,7},{7,6}} | collective-permute-start | bytes 17203208 | tf_op jit(solution)/shard_map/ppermute | solution.py:596
  324.1 117.3 %collective-permute-start.4 = (bf16[2048,1280]{1,0:T(8,128)(2,1)}, bf16[2048,1280]{1,0:T(8,128)(2,1)}, u32[]{:S(2)}, u32[]{:S(2)}) collective-permute-start(bf16[2048,1280]{1,0:T(8,128)(2,1)} %get-tuple-element.80.h), channel_id=1, source_target_pairs={{0,2},{2,0},{1,3},{3,1},{4,6},{6,4},{5,7},{7,5}} | collective-permute-start | bytes 15728648 | tf_op jit(solution)/shard_map/ppermute | solution.py:592
  327.2 226.6 %collective-permute-start.5 = (bf16[2048,1280]{1,0:T(8,128)(2,1)}, bf16[2048,1280]{1,0:T(8,128)(2,1)}, u32[]{:S(2)}, u32[]{:S(2)}) collective-permute-start(bf16[2048,1280]{1,0:T(8,128)(2,1)} %bitcast.23), channel_id=1, source_target_pairs={{0,2},{2,0},{1,3},{3,1},{4,6},{6,4},{5,7},{7,5}} | collective-permute-start | bytes 15728648 | tf_op jit(solution)/shard_map/ppermute | solution.py:592
  327.3 434.6 %collective-permute-start.14 = (f32[320,5376]{1,0:T(8,128)}, f32[320,5376]{1,0:T(8,128)}, u32[]{:S(2)}, u32[]{:S(2)}) collective-permute-start(f32[320,5376]{1,0:T(8,128)} %get-tuple-element.112), channel_id=1, source_target_pairs={{0,2},{2,0},{1,3},{3,1},{4,6},{6,4},{5,7},{7,5}} | collective-permute-start | bytes 20643848 | tf_op jit(solution)/shard_map/ppermute | solution.py:592
  757.9 286.3 %collective-permute-start.6 = (bf16[4,320,4480]{2,1,0:T(8,128)(2,1)}, bf16[4,320,4480]{2,1,0:T(8,128)(2,1)}, u32[]{:S(2)}, u32[]{:S(2)}) collective-permute-start(bf16[4,320,4480]{2,1,0:T(8,128)(2,1)} %get-tuple-element.100), channel_id=1, source_target_pairs={{0,1},{1,0},{2,3},{3,2},{4,5},{5,4},{6,7},{7,6}} | collective-permute-start | bytes 34406408 | tf_op jit(solution)/shard_map/ppermute | solution.py:596
  757.9 102.2 %collective-permute-start.21 = (f32[320,3584]{1,0:T(8,128)}, f32[320,3584]{1,0:T(8,128)}, u32[]{:S(2)}, u32[]{:S(2)}) collective-permute-start(f32[320,3584]{1,0:T(8,128)} %get-tuple-element.121), channel_id=1, source_target_pairs={{0,2},{2,0},{1,3},{3,1},{4,6},{6,4},{5,7},{7,5}} | collective-permute-start | bytes 13762568 | tf_op jit(solution)/shard_map/ppermute | solution.py:592
  759.9 284.3 %collective-permute-start.1 = (bf16[2,320,4480]{2,1,0:T(8,128)(2,1)}, bf16[2,320,4480]{2,1,0:T(8,128)(2,1)}, u32[]{:S(2)}, u32[]{:S(2)}) collective-permute-start(bf16[2,320,4480]{2,1,0:T(8,128)(2,1)} %get-tuple-element.90), channel_id=1, source_target_pairs={{0,2},{2,0},{1,3},{3,1},{4,6},{6,4},{5,7},{7,5}} | collective-permute-start | bytes 17203208 | tf_op jit(solution)/shard_map/ppermute | solution.py:592
  759.9 284.2 %collective-permute-start.3 = (bf16[1120,1280]{1,0:T(8,128)(2,1)}, bf16[1120,1280]{1,0:T(8,128)(2,1)}, u32[]{:S(2)}, u32[]{:S(2)}) collective-permute-start(bf16[1120,1280]{1,0:T(8,128)(2,1)} %get-tuple-element.93), channel_id=1, source_target_pairs={{0,2},{2,0},{1,3},{3,1},{4,6},{6,4},{5,7},{7,5}} | collective-permute-start | bytes 8601608 | tf_op jit(solution)/shard_map/ppermute | solution.py:592
  761.9 360.5 %collective-permute-start.15 = (f32[320,5376]{1,0:T(8,128)}, f32[320,5376]{1,0:T(8,128)}, u32[]{:S(2)}, u32[]{:S(2)}) collective-permute-start(f32[320,5376]{1,0:T(8,128)} %collective-permute-done.14.refs_0_), channel_id=1, source_target_pairs={{0,4},{4,0},{1,5},{5,1},{2,6},{6,2},{3,7},{7,3}} | collective-permute-start | bytes 20643848 | tf_op jit(solution)/shard_map/ppermute | solution.py:615
  860.1 262.3 %collective-permute-start.22 = (f32[320,3584]{1,0:T(8,128)}, f32[320,3584]{1,0:T(8,128)}, u32[]{:S(2)}, u32[]{:S(2)}) collective-permute-start(f32[320,3584]{1,0:T(8,128)} %collective-permute-done.21.refs_2_), channel_id=1, source_target_pairs={{0,4},{4,0},{1,5},{5,1},{2,6},{6,2},{3,7},{7,3}} | collective-permute-start | bytes 13762568 | tf_op jit(solution)/shard_map/ppermute | solution.py:615
  1091.0 115.8 %collective-permute-start.30 = (bf16[896,1280]{1,0:T(8,128)(2,1)}, bf16[896,1280]{1,0:T(8,128)(2,1)}, u32[]{:S(2)}, u32[]{:S(2)}) collective-permute-start(bf16[896,1280]{1,0:T(8,128)(2,1)} %get-tuple-element.133), channel_id=1, source_target_pairs={{0,1},{1,0},{2,3},{3,2},{4,5},{5,4},{6,7},{7,6}} | collective-permute-start | bytes 6881288 | tf_op jit(solution)/shard_map/ppermute | solution.py:596
  1091.0 49.2 %collective-permute-start.32 = (bf16[112,1280]{1,0:T(8,128)(2,1)}, bf16[112,1280]{1,0:T(8,128)(2,1)}, u32[]{:S(2)}, u32[]{:S(2)}) collective-permute-start(bf16[112,1280]{1,0:T(8,128)(2,1)} %get-tuple-element.135), channel_id=1, source_target_pairs={{0,1},{1,0},{2,3},{3,2},{4,5},{5,4},{6,7},{7,6}} | collective-permute-start | bytes 860168 | tf_op jit(solution)/shard_map/ppermute | solution.py:596
  1137.9 116.4 %collective-permute-start.23 = (bf16[320,4480]{1,0:T(8,128)(2,1)}, bf16[320,4480]{1,0:T(8,128)(2,1)}, u32[]{:S(2)}, u32[]{:S(2)}) collective-permute-start(bf16[320,4480]{1,0:T(8,128)(2,1)} %get-tuple-element.123), channel_id=1, source_target_pairs={{0,1},{1,0},{2,3},{3,2},{4,5},{5,4},{6,7},{7,6}} | collective-permute-start | bytes 8601608 | tf_op jit(solution)/shard_map/ppermute | solution.py:596
  1140.2 114.5 %collective-permute-start.20 = (bf16[320,4480]{1,0:T(8,128)(2,1)}, bf16[320,4480]{1,0:T(8,128)(2,1)}, u32[]{:S(2)}, u32[]{:S(2)}) collective-permute-start(bf16[320,4480]{1,0:T(8,128)(2,1)} %get-tuple-element.120), channel_id=1, source_target_pairs={{0,1},{1,0},{2,3},{3,2},{4,5},{5,4},{6,7},{7,6}} | collective-permute-start | bytes 8601608 | tf_op jit(solution)/shard_map/ppermute | solution.py:596
  1143.8 64.7 %collective-permute-start.24 = (bf16[896,1280]{1,0:T(8,128)(2,1)}, bf16[896,1280]{1,0:T(8,128)(2,1)}, u32[]{:S(2)}, u32[]{:S(2)}) collective-permute-start(bf16[896,1280]{1,0:T(8,128)(2,1)} %get-tuple-element.133), channel_id=1, source_target_pairs={{0,2},{2,0},{1,3},{3,1},{4,6},{6,4},{5,7},{7,5}} | collective-permute-start | bytes 6881288 | tf_op jit(solution)/shard_map/ppermute | solution.py:592
  1148.1 54.6 %collective-permute-start.26 = (bf16[112,1280]{1,0:T(8,128)(2,1)}, bf16[112,1280]{1,0:T(8,128)(2,1)S(1)}, u32[]{:S(2)}, u32[]{:S(2)}) collective-permute-start(bf16[112,1280]{1,0:T(8,128)(2,1)} %get-tuple-element.134), channel_id=1, source_target_pairs={{0,2},{2,0},{1,3},{3,1},{4,6},{6,4},{5,7},{7,5}} | collective-permute-start | bytes 860168 | tf_op jit(solution)/shard_map/ppermute | solution.py:592
  1206.6 48.4 %collective-permute-start.19 = (bf16[320,4480]{1,0:T(8,128)(2,1)}, bf16[320,4480]{1,0:T(8,128)(2,1)}, u32[]{:S(2)}, u32[]{:S(2)}) collective-permute-start(bf16[320,4480]{1,0:T(8,128)(2,1)} %get-tuple-element.116), channel_id=1, source_target_pairs={{0,1},{1,0},{2,3},{3,2},{4,5},{5,4},{6,7},{7,6}} | collective-permute-start | bytes 8601608 | tf_op jit(solution)/shard_map/ppermute | solution.py:596
  1206.7 65.3 %collective-permute-start.17 = (bf16[320,4480]{1,0:T(8,128)(2,1)}, bf16[320,4480]{1,0:T(8,128)(2,1)}, u32[]{:S(2)}, u32[]{:S(2)}) collective-permute-start(bf16[320,4480]{1,0:T(8,128)(2,1)} %get-tuple-element.116), channel_id=1, source_target_pairs={{0,2},{2,0},{1,3},{3,1},{4,6},{6,4},{5,7},{7,5}} | collective-permute-start | bytes 8601608 | tf_op jit(solution)/shard_map/ppermute | solution.py:592
  1208.5 65.9 %collective-permute-start.25 = (bf16[896,1280]{1,0:T(8,128)(2,1)}, bf16[896,1280]{1,0:T(8,128)(2,1)}, u32[]{:S(2)}, u32[]{:S(2)}) collective-permute-start(bf16[896,1280]{1,0:T(8,128)(2,1)} %collective-permute-done.24.refs_0_), channel_id=1, source_target_pairs={{0,1},{1,0},{2,3},{3,2},{4,5},{5,4},{6,7},{7,6}} | collective-permute-start | bytes 6881288 | tf_op jit(solution)/shard_map/ppermute | solution.py:596
  1254.3 57.4 %collective-permute-start.16 = (bf16[320,4480]{1,0:T(8,128)(2,1)}, bf16[320,4480]{1,0:T(8,128)(2,1)}, u32[]{:S(2)}, u32[]{:S(2)}) collective-permute-start(bf16[320,4480]{1,0:T(8,128)(2,1)} %get-tuple-element.114), channel_id=1, source_target_pairs={{0,1},{1,0},{2,3},{3,2},{4,5},{5,4},{6,7},{7,6}} | collective-permute-start | bytes 8601608 | tf_op jit(solution)/shard_map/ppermute | solution.py:596
  1254.7 78.8 %collective-permute-start.10 = (bf16[320,4480]{1,0:T(8,128)(2,1)}, bf16[320,4480]{1,0:T(8,128)(2,1)}, u32[]{:S(2)}, u32[]{:S(2)}) collective-permute-start(bf16[320,4480]{1,0:T(8,128)(2,1)} %get-tuple-element.107), channel_id=1, source_target_pairs={{0,2},{2,0},{1,3},{3,1},{4,6},{6,4},{5,7},{7,5}} | collective-permute-start | bytes 8601608 | tf_op jit(solution)/shard_map/ppermute | solution.py:592
  1255.0 85.5 %collective-permute-start.13 = (bf16[320,4480]{1,0:T(8,128)(2,1)}, bf16[320,4480]{1,0:T(8,128)(2,1)}, u32[]{:S(2)}, u32[]{:S(2)}) collective-permute-start(bf16[320,4480]{1,0:T(8,128)(2,1)} %get-tuple-element.111), channel_id=1, source_target_pairs={{0,1},{1,0},{2,3},{3,2},{4,5},{5,4},{6,7},{7,6}} | collective-permute-start | bytes 8601608 | tf_op jit(solution)/shard_map/ppermute | solution.py:596
  1272.1 70.2 %collective-permute-start.12 = (bf16[320,4480]{1,0:T(8,128)(2,1)}, bf16[320,4480]{1,0:T(8,128)(2,1)}, u32[]{:S(2)}, u32[]{:S(2)}) collective-permute-start(bf16[320,4480]{1,0:T(8,128)(2,1)} %get-tuple-element.107), channel_id=1, source_target_pairs={{0,1},{1,0},{2,3},{3,2},{4,5},{5,4},{6,7},{7,6}} | collective-permute-start | bytes 8601608 | tf_op jit(solution)/shard_map/ppermute | solution.py:596
  1274.4 96.0 %collective-permute-start.18 = (bf16[320,4480]{1,0:T(8,128)(2,1)}, bf16[320,4480]{1,0:T(8,128)(2,1)}, u32[]{:S(2)}, u32[]{:S(2)}) collective-permute-start(bf16[320,4480]{1,0:T(8,128)(2,1)} %collective-permute-done.17.refs_0_), channel_id=1, source_target_pairs={{0,1},{1,0},{2,3},{3,2},{4,5},{5,4},{6,7},{7,6}} | collective-permute-start | bytes 8601608 | tf_op jit(solution)/shard_map/ppermute | solution.py:596
  1311.7 58.7 %collective-permute-start.35 = (bf16[672,1280]{1,0:T(8,128)(2,1)}, bf16[672,1280]{1,0:T(8,128)(2,1)}, u32[]{:S(2)}, u32[]{:S(2)}) collective-permute-start(bf16[672,1280]{1,0:T(8,128)(2,1)} %get-tuple-element.141), channel_id=1, source_target_pairs={{0,2},{2,0},{1,3},{3,1},{4,6},{6,4},{5,7},{7,5}} | collective-permute-start | bytes 5160968 | tf_op jit(solution)/shard_map/ppermute | solution.py:592
  1333.5 92.9 %collective-permute-start.11 = (bf16[320,4480]{1,0:T(8,128)(2,1)}, bf16[320,4480]{1,0:T(8,128)(2,1)}, u32[]{:S(2)}, u32[]{:S(2)}) collective-permute-start(bf16[320,4480]{1,0:T(8,128)(2,1)} %collective-permute-done.10.refs_0_), channel_id=1, source_target_pairs={{0,1},{1,0},{2,3},{3,2},{4,5},{5,4},{6,7},{7,6}} | collective-permute-start | bytes 8601608 | tf_op jit(solution)/shard_map/ppermute | solution.py:596
  1340.5 53.9 %collective-permute-start.33 = (bf16[448,1280]{1,0:T(8,128)(2,1)}, bf16[448,1280]{1,0:T(8,128)(2,1)}, u32[]{:S(2)}, u32[]{:S(2)}) collective-permute-start(bf16[448,1280]{1,0:T(8,128)(2,1)} %get-tuple-element.140), channel_id=1, source_target_pairs={{0,2},{2,0},{1,3},{3,1},{4,6},{6,4},{5,7},{7,5}} | collective-permute-start | bytes 3440648 | tf_op jit(solution)/shard_map/ppermute | solution.py:592
  1342.3 87.8 %collective-permute-start.38 = (bf16[672,1280]{1,0:T(8,128)(2,1)}, bf16[672,1280]{1,0:T(8,128)(2,1)}, u32[]{:S(2)}, u32[]{:S(2)}) collective-permute-start(bf16[672,1280]{1,0:T(8,128)(2,1)} %get-tuple-element.141), channel_id=1, source_target_pairs={{0,1},{1,0},{2,3},{3,2},{4,5},{5,4},{6,7},{7,6}} | collective-permute-start | bytes 5160968 | tf_op jit(solution)/shard_map/ppermute | solution.py:596
  1370.4 70.8 %collective-permute-start.36 = (bf16[672,1280]{1,0:T(8,128)(2,1)}, bf16[672,1280]{1,0:T(8,128)(2,1)}, u32[]{:S(2)}, u32[]{:S(2)}) collective-permute-start(bf16[672,1280]{1,0:T(8,128)(2,1)} %collective-permute-done.35.refs_0_), channel_id=1, source_target_pairs={{0,1},{1,0},{2,3},{3,2},{4,5},{5,4},{6,7},{7,6}} | collective-permute-start | bytes 5160968 | tf_op jit(solution)/shard_map/ppermute | solution.py:596
  1370.4 63.9 %collective-permute-start.37 = (bf16[448,1280]{1,0:T(8,128)(2,1)}, bf16[448,1280]{1,0:T(8,128)(2,1)}, u32[]{:S(2)}, u32[]{:S(2)}) collective-permute-start(bf16[448,1280]{1,0:T(8,128)(2,1)} %get-tuple-element.140), channel_id=1, source_target_pairs={{0,1},{1,0},{2,3},{3,2},{4,5},{5,4},{6,7},{7,6}} | collective-permute-start | bytes 3440648 | tf_op jit(solution)/shard_map/ppermute | solution.py:596
  1394.3 53.7 %collective-permute-start.34 = (bf16[448,1280]{1,0:T(8,128)(2,1)}, bf16[448,1280]{1,0:T(8,128)(2,1)}, u32[]{:S(2)}, u32[]{:S(2)}) collective-permute-start(bf16[448,1280]{1,0:T(8,128)(2,1)} %collective-permute-done.33.refs_0_), channel_id=1, source_target_pairs={{0,1},{1,0},{2,3},{3,2},{4,5},{5,4},{6,7},{7,6}} | collective-permute-start | bytes 3440648 | tf_op jit(solution)/shard_map/ppermute | solution.py:596
  (12 other events, 157.7 us)

commit v5 on v4

--- a/solution.py
+++ b/solution.py
@@ -1,4 +1,5 @@
 import functools
+import math
 
 import jax
 import jax.numpy as jnp
@@ -69,16 +70,20 @@
     loop(a.shape[0] // CHUNK, CHUNK, rows)
 
 
+def unless_first(total):
+    return jnp.where(pl.program_id(1) == 0, 0.0, total)
+
+
 def only(a, n, axis):
     return jnp.where(lax.broadcasted_iota(jnp.int32, a.shape, axis) < n, a, jnp.zeros_like(a))
 
 
-PIECES, EARLY = 5, 6
+PIECES, OF_UP, EARLY = 5, 4, 6
 
 
 def copied(at, step, moments, early, late, held, in_sems, out_sems):
     cols = held.shape[2]
-    n = 2 * PIECES
+    n = PIECES + OF_UP
 
     def columns(block):
         return pl.ds(pl.multiple_of(block * cols, 128), cols)
@@ -93,7 +98,7 @@
     for which in range(2):
         for rep in range(2):
 
-            @pl.when((step >= which * PIECES) & (step < (which + 1) * PIECES) & (at[2] == rep))
+            @pl.when((step >= which * PIECES) & (step < min((which + 1) * PIECES, n)) & (at[2] == rep))
             def _(source=moments[2 * which + rep], block=step - which * PIECES):
                 pltpu.make_async_copy(source.at[1, :, columns(block)], held.at[step % 2], in_sems.at[step % 2]).start()
 
@@ -115,18 +120,18 @@
     @pl.when(j == 0)
     def _():
         norm(x, a, a_out)
-        total[...] = jnp.zeros_like(total)
 
     for c in chunks(UNITS):
-        gate, up = dot(a[...], wg[:, c], NN), dot(a[...], wu[:, c], NN)
-        sig = sigmoid(gate)
-        silu = gate * sig
-        units[:, c] = only((silu * up).astype(BF), left - c.start, 1)
-        hid[c, :] = units[:, c].T
-        s_out[:, c] = silu
-        q_out[:, c] = up * (sig + silu * (1 - sig))
+        for r in chunks(a.shape[0]):
+            gate, up = dot(a[r, :], wg[:, c], NN), dot(a[r, :], wu[:, c], NN)
+            sig = sigmoid(gate)
+            silu = gate * sig
+            units[r, c] = only((silu * up).astype(BF), left - c.start, 1)
+            hid[c, r] = units[r, c].T
+            s_out[r, c] = silu
+            q_out[r, c] = up * (sig + silu * (1 - sig))
     for c in chunks(total.shape[1]):
-        total[:, c] += dot(units[...], only(wd[:, c], left, 0), NN)
+        total[:, c] = unless_first(total[:, c]) + dot(units[...], only(wd[:, c], left, 0), NN)
 
     @pl.when(j == pl.num_programs(1) - 1)
     def _():
@@ -140,7 +145,8 @@
     m = moments[0]
     t, d = x.shape
     f = w_gate.shape[2]
-    wide = pl.BlockSpec((TOKENS, UNITS), lambda i, j, at: (i, j))
+    n = pl.cdiv(f, UNITS)
+    wide = pl.BlockSpec((None, TOKENS, UNITS), lambda i, j, at: (j, i, 0))
     weight = pl.BlockSpec((None, d, UNITS), lambda i, j, at: (0, 0, j))
     state = pl.BlockSpec((TOKENS, d), lambda i, j, at: (i, 0))
     return call(
@@ -157,8 +163,8 @@
             state,
         ]
         + [pl.BlockSpec(memory_space=pl.ANY)] * 2,
-        [out((d, t)), out((f, t)), out((t, f), F32), out((t, f), F32), out((t, d))]
-        + [out((m.shape[1], n * f // PIECES), F32) for n in (EARLY, 2 * PIECES - EARLY)],
+        [out((d, t)), out((f, t)), *[out((n, t, UNITS), F32)] * 2, out((t, d))]
+        + [out((m.shape[1], n * f // PIECES), F32) for n in (EARLY, PIECES + OF_UP - EARLY)],
         (x, w_gate, w_up, w_down, *moments),
         6 * t * d * f,
         190e6,
@@ -174,8 +180,8 @@
 
 
 def second_units(a, dy, wg, wu, wd, hid, dgu, left):
-    for c in chunks(UNITS):
-        for r in chunks(a.shape[0], a.shape[0] // (1 if c.start == 0 else 4)):
+    for c in chunks(hid.shape[0]):
+        for r in chunks(a.shape[0]):
             gate, up = dot(a[r, :], wg[:, c], NN), dot(a[r, :], wu[:, c], NN)
             back = dot(dy[r, :], wd[c, :], NT).astype(BF).astype(F32)
             sig = sigmoid(gate)
@@ -192,7 +198,7 @@
     def _():
         norm(h, a, a_out)
 
-    second_units(a, dy, wg, wu, wd, hid, dgu, f - j * UNITS)
+    second_units(a, dy, wg, wu, wd, hid, dgu, f - j * hid.shape[0])
 
 
 def second_back_kernel(at, h, dy, wg, wu, wd, a_out, dgu, hid, d_out, a, of_gate, of_up, *, f):
@@ -202,13 +208,11 @@
     @pl.when(j == 0)
     def _():
         norm(h, a, a_out)
-        of_gate[...] = jnp.zeros_like(of_gate)
-        of_up[...] = jnp.zeros_like(of_up)
 
     second_units(a, dy, wg, wu, wd, hid, dgu, left)
     for c in chunks(of_gate.shape[1]):
-        of_gate[:, c] += dot(dgu[0], only(wg[c, :], left, 1), NT)
-        of_up[:, c] += dot(dgu[1], only(wu[c, :], left, 1), NT)
+        of_gate[:, c] = unless_first(of_gate[:, c]) + dot(dgu[0], only(wg[c, :], left, 1), NT)
+        of_up[:, c] = unless_first(of_up[:, c]) + dot(dgu[1], only(wu[c, :], left, 1), NT)
 
     @pl.when(j == pl.num_programs(1) - 1)
     def _():
@@ -226,15 +230,15 @@
     t, d = h.shape
     f = w_gate.shape[2]
     far = before is not None
-    bt = TOKENS
-    weight = pl.BlockSpec((None, d, UNITS), lambda i, j, at: (1, 0, j))
+    bt, bf = TOKENS, UNITS
+    weight = pl.BlockSpec((None, d, bf), lambda i, j, at: (1, 0, j))
     state = pl.BlockSpec((bt, d), lambda i, j, at: (i, 0))
     which = (lambda at: 1 - at[0]) if far else (lambda at: at[0])
-    in_specs = [state, state, weight, weight, pl.BlockSpec((None, UNITS, d), lambda i, j, at: (1, j, 0))]
+    in_specs = [state, state, weight, weight, pl.BlockSpec((None, bf, d), lambda i, j, at: (1, j, 0))]
     out_specs = [
         pl.BlockSpec((None, d, bt), lambda i, j, at: (which(at), 0, i)),
-        pl.BlockSpec((None, 2, bt, UNITS), lambda i, j, at: (which(at), 0, i, j)),
-        pl.BlockSpec((UNITS, bt), lambda i, j, at: (j, i)),
+        pl.BlockSpec((None, 2, bt, bf), lambda i, j, at: (which(at), 0, i, j)),
+        pl.BlockSpec((bf, bt), lambda i, j, at: (j, i)),
     ]
     shapes = [out((2, d, t)), out((2, 2, t, f)), out((f, t))]
     scratch = [pltpu.VMEM((bt, d), BF)]
@@ -252,7 +256,7 @@
         functools.partial(second_kernel if far else second_back_kernel, f=f),
         grid_spec=pltpu.PrefetchScalarGridSpec(
             num_scalar_prefetch=1,
-            grid=(t // bt, pl.cdiv(f, UNITS)),
+            grid=(t // bt, pl.cdiv(f, bf)),
             in_specs=in_specs,
             out_specs=out_specs,
             scratch_shapes=scratch,
@@ -273,10 +277,10 @@
 
 
 def hidden_back_kernel(at, w, d, s, q, one, two, dgu, theirs):
-    for c in chunks(UNITS):
-        back = dot(d[...], w[c, :], NT).astype(BF).astype(F32)
-        dgu[1, :, c] = (back * s[:, c]).astype(BF)
-        dgu[0, :, c] = (back * q[:, c]).astype(BF)
+    for r in chunks(d.shape[0]):
+        back = dot(d[r, :], w[...], NT).astype(BF).astype(F32)
+        dgu[1, r, :] = (back * s[r, :]).astype(BF)
+        dgu[0, r, :] = (back * q[r, :]).astype(BF)
     left = jnp.concatenate([one[...], two[...]], 0)
     for which in range(2):
         theirs[which] = dot(left, dgu[which], NN).reshape(theirs.shape[1:]).astype(BF)
@@ -284,22 +288,22 @@
 
 def hidden_back(at, w_down, d_h, s, q, a):
     t, d = d_h.shape
-    f = s.shape[1]
-    rows = a.shape[1]
-    wide = pl.BlockSpec((t, UNITS), lambda j, at: (0, j))
+    f = w_down.shape[1]
+    rows, bf = a.shape[1], UNITS
+    wide = pl.BlockSpec((None, t, bf), lambda j, at: (j, 0, 0))
     return call(
         hidden_back_kernel,
         at,
-        (pl.cdiv(f, UNITS),),
+        (pl.cdiv(f, bf),),
         [
-            pl.BlockSpec((None, UNITS, d), lambda j, at: (0, j, 0)),
+            pl.BlockSpec((None, bf, d), lambda j, at: (0, j, 0)),
             once((t, d), lambda j, at: (0, 0)),
             wide,
             wide,
             once((None, rows, t), lambda j, at: (on(False, False)(at), 0, 0)),
             once((None, rows, t), lambda j, at: (on(True, False)(at), 0, 0)),
         ],
-        [pl.BlockSpec((2, t, UNITS), lambda j, at: (0, 0, j)), pl.BlockSpec((2, 2, rows, UNITS), lambda j, at: (0, 0, 0, j))],
+        [pl.BlockSpec((2, t, bf), lambda j, at: (0, 0, j)), pl.BlockSpec((2, 2, rows, bf), lambda j, at: (0, 0, 0, j))],
         [out((2, t, f)), out((2, 2, rows, f))],
         (w_down, d_h, s, q, a, a),
         4 * t * d * f,
@@ -317,7 +321,7 @@
 def grad_wide(at, left, right, one, two, got):
     rows, t = left.shape[1:]
     f = right.shape[2]
-    bn = 768
+    bn = 1536
     return call(
         wide_kernel,
         at,
@@ -332,9 +336,17 @@
     )
 
 
-def whole_kernel(at, left0, left1, right0, right1, send, keep, total):
-    total[...] = (dot(left0[...], right0[...], NN) + dot(left1[...], right1[...], NN)).reshape(total.shape)
-    send[...], keep[...] = total[1 - at[1]].astype(BF), total[at[1]]
+def whole_kernel(at, left0, left1, right0, right1, send, keep, total, *, last):
+    needed = (pl.program_id(0) < 3) | (pl.program_id(1) < last)
+
+    @pl.when(needed)
+    def _():
+        total[...] = (dot(left0[...], right0[...], NN) + dot(left1[...], right1[...], NN)).reshape(total.shape)
+        send[...], keep[...] = total[1 - at[1]].astype(BF), total[at[1]]
+
+    @pl.when(~needed)
+    def _():
+        send[...], keep[...] = jnp.zeros_like(send), jnp.zeros_like(keep)
 
 
 def grad_whole(at, left, right):
@@ -347,7 +359,7 @@
         return jnp.where(w < 2, at[0], 1 - at[0])
 
     return call(
-        whole_kernel,
+        functools.partial(whole_kernel, last=pl.cdiv(f * OF_UP // PIECES, bn)),
         at,
         (4, pl.cdiv(f, bn)),
         [pl.BlockSpec((None, 2 * rows, t), lambda w, j, at, x=x: (x, half(w, at), 0)) for x in range(2)]
@@ -467,20 +479,24 @@
 
 
 def gradient(factor, keep, far, r):
-    return (keep[r, :] + far[r, :].astype(F32)).astype(BF).astype(F32) * factor[0]
-
-
-def adam_kernel(at, factor, keep, far, w, m, v, *rest):
-    w_out, m_out, v_out, w_new = rest[-4:]
+    return (keep[r] + far[r].astype(F32)).astype(BF).astype(F32) * factor[0]
+
+
+def adam_kernel(at, factor, keep, far, w, m, v, *rest, tails):
+    w_out, m_out, v_out, w_new, *tail = rest[-4 - tails :]
 
     def rows(r):
-        w_out[r, :], m_out[r, :], v_out[r, :] = updated(gradient(factor, keep, far, r), w[r, :], m[r, :], v[r, :])
-        w_new[r, :] = w_out[r, :]
-
-    loop(w.shape[0] // 16, 16, rows)
-
-
-def adam(at, factor, layer, which, part, keep, far, w, m, v, before):
+        w_out[r], m_out[r], v_out[r] = updated(gradient(factor, keep, far, r), w[r], m[r], v[r])
+        w_new[r] = w_out[r]
+
+    cols = w.shape[1] // PIECES
+    size = math.gcd(w.shape[0], 32)
+    loop(w.shape[0] // size, size, lambda r: loop(PIECES, cols, lambda c: rows((r, c))))
+    for o in tail:
+        o[...] = w_out[:, w.shape[1] - o.shape[1] :]
+
+
+def adam(at, factor, layer, which, part, keep, far, w, m, v, before, tail=0):
     rows, cols = keep.shape[1:]
     low, high, n = part
     br = rows // n
@@ -488,12 +504,12 @@
     grad = pl.BlockSpec((None, br, cols), lambda i, at: (which, low + i, 0))
     there = pl.BlockSpec((None, br, cols), lambda i, at: (layer, (2 * at[0] + at[1]) * n + low + i, 0))
     return call(
-        adam_kernel,
+        functools.partial(adam_kernel, tails=int(tail > 0)),
         at,
         (high - low,),
         [pl.BlockSpec(memory_space=pltpu.SMEM), grad, grad, there, own, own] + [pl.BlockSpec(memory_space=pl.ANY)] * len(before),
-        [pl.BlockSpec((br, cols), lambda i, at: (i, 0)), own, own, there],
-        [out((br * (high - low), cols)), out(m.shape, F32), out(v.shape, F32), out(w.shape)],
+        [pl.BlockSpec((br, cols), lambda i, at: (i, 0)), own, own, there] + [pl.BlockSpec((br, tail), lambda i, at: (i, 0))] * (tail > 0),
+        [out((br * (high - low), cols)), out(m.shape, F32), out(v.shape, F32), out(w.shape)] + [out((br * (high - low), tail))] * (tail > 0),
         [factor, keep, far, w, m, v, *before],
         1e9,
         6e6 * (high - low),
@@ -508,7 +524,7 @@
     def update(crossed, handed):
         def rows(r):
             m, v = jnp.where(first, crossed[r, :], handed[r, :]), jnp.where(first, handed[r, :], crossed[r, :])
-            w_out[r, :], _, _ = updated(gradient(factor, keep, far, r), w[r, :], m, v)
+            w_out[r, :], _, _ = updated(gradient(factor, keep, far, (r, slice(None))), w[r, :], m, v)
             w_new[r, :] = w_out[r, :]
 
         loop(w.shape[0] // 32, 32, rows)
@@ -521,7 +537,7 @@
         pl.when(~early)(lambda: update(*moments[2:]))
 
 
-def adam_far(at, factor, layer, which, start, keep, far, w, moments, before):
+def adam_far(at, factor, layer, which, start, count, keep, far, w, moments, before):
     rows, cols = keep.shape[1:]
     n = 2
     br, bc = rows // n, cols // PIECES
@@ -530,15 +546,15 @@
     there = pl.BlockSpec((None, br, bc), lambda i, j, at: (layer, (2 * (1 - at[0]) + at[1]) * n + i, j))
     early = pl.BlockSpec((br, bc), lambda i, j, at: (i, jnp.minimum(j + start, EARLY - 1)))
     late = pl.BlockSpec((br, bc), lambda i, j, at: (i, jnp.maximum(j + start - EARLY, 0)))
-    specs = ([early] * 2 if start < EARLY else []) + ([late] * 2 if start + PIECES > EARLY else [])
+    specs = ([early] * 2 if start < EARLY else []) + ([late] * 2 if start + count > EARLY else [])
     moments = moments[: len(specs)]
     return call(
         functools.partial(adam_far_kernel, start=start),
         at,
-        (n, PIECES),
+        (n, count),
         [pl.BlockSpec(memory_space=pltpu.SMEM), grad, grad, there, *specs, pl.BlockSpec(memory_space=pl.ANY)],
         [flat, there],
-        [out((rows, cols)), out(w.shape)],
+        [out((rows, bc * count)), out(w.shape)],
         [factor, keep, far, w, *moments, before],
         1e9,
         30e6,
@@ -551,27 +567,31 @@
         pl.when(pl.program_id(0) == n)(functools.partial(lambda n: refs[-1].__setitem__(..., refs[n][...]), n))
 
 
-def place(at, layer, part, blocks, wheres, before):
+def place(at, layer, part, blocks, wheres, before, piece=None):
     low, high, n = part
     k = high - low
-    cols = blocks[0].shape[1]
-    br = blocks[0].shape[0] // k
+    rows, cols = blocks[0].shape
+    br, bc = rows // k, cols if piece is None else before.shape[2] // PIECES
+    m = cols // bc
 
     def spec(n):
-        return pl.BlockSpec((br, cols), lambda i, j, at: (jnp.where(i < n, 0, jnp.where(i > n, k - 1, j)), 0))
-
-    def where(i, j, at):
+        def index(i, j, l, at):
+            return jnp.where(i < n, 0, jnp.where(i > n, k - 1, j)), jnp.where(i < n, 0, jnp.where(i > n, m - 1, l))
+
+        return pl.BlockSpec((br, bc), index)
+
+    def where(i, j, l, at):
         b = wheres[0](at)
         for k, w in enumerate(wheres[1:], 1):
             b = jnp.where(i == k, w(at), b)
-        return layer, b * n + low + j, 0
+        return layer, b * n + low + j, l + (piece or 0)
 
     return call(
         functools.partial(place_kernel, count=len(blocks)),
         at,
-        (len(blocks), k),
+        (len(blocks), k, m),
         [spec(n) for n in range(len(blocks))] + [pl.BlockSpec(memory_space=pl.ANY)],
-        pl.BlockSpec((None, br, cols), where),
+        pl.BlockSpec((None, br, bc), where),
         out(before.shape),
         [*blocks, before],
         1e9,
@@ -626,7 +646,7 @@
     send, keep_wide1 = grad_wide(at, blocks(a1), dgu1, on(False, True), on(True, True), got_wide)
     far_wide1 = across(send)
     got_down = after(got_down, keep_wide1)
-    send, keep_down1 = grad_tall(at, pairs, on(False, True), on(True, True), got_down, half=7)
+    send, keep_down1 = grad_tall(at, pairs, on(False, True), on(True, True), got_down)
     far_down1 = across(send)
 
     h1_far = after(h1_far, keep_down1)
@@ -634,7 +654,7 @@
     send, keep_wide2 = grad_whole(at, a2, dgu2)
     far_wide2 = sibling(send)
     pairs = [(blocks(hid2), dy), (blocks(after(hid2f, keep_wide2)), dy_far)]
-    send, keep_down2 = grad_tall(at, pairs, on(True, False), on(True, True), half=7)
+    send, keep_down2 = grad_tall(at, pairs, on(True, False), on(True, True))
     far_down2 = sibling(send)
     keep_down1, far_down1, keep_down2, far_down2 = (a[None] for a in (keep_down1, far_down1, keep_down2, far_down2))
     squares = sum_of_squares((keep_wide1, far_wide1, 2), (keep_down1, far_down1, 1), (keep_wide2, far_wide2, 2))
@@ -655,20 +675,21 @@
     }
     new = dict.fromkeys(weights, ())
 
-    def update(which, part):
+    def update(which, part, tail=0):
         name = which[:-1]
-        own, *new[name] = adam(at, factor, *grads[which][:2], part, *grads[which][2:], *weights[name], new[name])
-        return own
-
-    def put(which, part, *blocks):
+        first, *rest = adam(at, factor, *grads[which][:2], part, *grads[which][2:], *weights[name], new[name], tail)
+        new[name] = rest[:3]
+        return first, *rest[3:]
+
+    def put(which, part, *blocks, piece=None):
         name = which[:-1]
         *moments, w = new[name]
         where, arrays = zip(*blocks, strict=True)
-        new[name] = [*moments, place(at, grads[which][0], part, arrays, where, w)]
+        new[name] = [*moments, place(at, grads[which][0], part, arrays, where, w, piece)]
 
     def send(n):
         which, part = PARTS[n]
-        own = update(which, part)
+        (own,) = update(which, part)
         return across(own), sibling(own)
 
     def settle(sent):
@@ -678,20 +699,26 @@
             put(*PARTS[n], (on(False, True), away))
             put(*PARTS[n], (on(False, False), sibling(away)))
 
-    def both_blocks(name, which):
-        part = (0, 2, 2)
-        own = update(name + "1", part)
+    whole = (0, 2, 2)
+
+    def update_far(name, which, count):
         *moments, w = new[name]
         arrays = keep_wide2, far_wide2, weights[name][0], far_moments
-        away, w = adam_far(at, factor, 1, which, (which - 2) * PIECES, *arrays, w)
+        away, w = adam_far(at, factor, 1, which, (which - 2) * PIECES, count, *arrays, w)
         new[name] = [*moments, w]
-        beside, last = sibling(own), sibling(away)
-        put(name + "1", part, (on(True, False), beside), (on(False, False), last))
+        return sibling(away)
 
     sent = {n: send(n) for n in range(len(PARTS) - 2)}
-    both_blocks("gate", 2)
-    both_blocks("up", 3)
+    (own,) = update("gate1", whole)
+    last = update_far("gate", 2, PIECES)
+    put("gate1", whole, (on(True, False), sibling(own)), (on(False, False), last))
+    own, tail = update("up1", whole, f // PIECES * (PIECES - OF_UP))
+    tail = across(tail)
+    put("up1", whole, (on(True, False), sibling(own)))
+    last = update_far("up", 3, OF_UP)
+    put("up1", whole, (on(False, False), last), piece=0)
     settle(sent)
+    put("up1", whole, (on(False, True), tail), (on(False, False), sibling(tail)), piece=OF_UP)
     settle({n: send(n) for n in range(len(sent), len(PARTS))})
     return tuple(new[name][i] for i in (2, 0, 1) for name in weights)
 
@@ -699,7 +726,8 @@
 PARTS = [
     ("down1", (0, 1, 10)),
     ("down1", (1, 2, 10)),
-    ("down1", (1, 5, 5)),
+    ("down1", (1, 2, 5)),
+    ("down1", (2, 5, 5)),
     ("gate0", (0, 2, 2)),
     ("up0", (0, 2, 2)),
     ("down0", (0, 3, 5)),

time: 1460 us -> 1420 us (0.973)
  waiting for transfers between devices: 567 us -> 527 us
    ppermute x14 -> x16, waiting for transfers between devices: 559 us -> 500 us  [across(): return lax.ppermute(a, 'dp', ACROSS)]
    ppermute x2, waiting for transfers between devices: 0.01 us -> 20.6 us  [brought(): return (crossed, lax.ppermute(crossed, 'rep', [(0, 1), (1, 0)]))]
    pallas_call x41 -> x47, Pallas kernels: 594 us -> 596 us  [call(): pl.pallas_call(kernel, grid_spec=pltpu.PrefetchScalarGridSpec(num_scalar_...]
  transfers between devices with their start and end apart: 39 -> 44, of which waited for: 15 -> 16; matrix products, arithmetic and copies ran while one was open for 0% -> 0% of each run, Pallas kernels for 37% -> 39%
where the time goes in v5:
time: 1420 us; the launch traced here: 1410 us
  Pallas kernels  850 us (60%)
  waiting for transfers between devices  527 us (37%)
  starting transfers between devices  26.6 us (2%)
    pallas_call x47, Pallas kernels, call(): pl.pallas_call(kernel, grid_spec=pltpu.PrefetchScalarGridSpec(num_scalar_...  596 us
    ppermute x16, waiting for transfers between devices, across(): return lax.ppermute(a, 'dp', ACROSS)  500 us
    pallas_call x2, Pallas kernels, second(): pl.pallas_call(functools.partial(second_kernel if far else second_back_ke...  235 us
  transfers between devices with their start and end apart: 44, of which 16 were waited for; matrix products, arithmetic and copies ran while one was open for 0% of the time, Pallas kernels for 39%

profile of v5, /device:TPU:0, one launch (start us, length us, event | category | flops | bytes accessed | tf_op | source)
XLA Modules:
  0.0 1407.5 jit_solution(10830955105465094968)
XLA Ops:
  1.3 93.0 %shard_map.178 = (bf16[1280,2048]{1,0:T(8,128)(2,1)}, bf16[4480,2048]{1,0:T(8,128)(2,1)}, f32[9,2048,512]{2,1,0:T(8,128)}, f32[9,2048,512]{2,1,0:T(8,128)}, bf16...) custom-call(s32[3]{0:T(128)} %pad_add_fusion.at, bf16[2048,1280]{1,0:T(8,128)(2,1)} %bitcast.22, ...), custom_call_target="tpu_custom_call" | custom-call | flops 70464307200 | bytes 190000000 | tf_op jit(solution)/shard_map/pallas_call | solution.py:39
  94.3 144.2 %second_back.1 = (bf16[2,1280,2048]{2,1,0:T(8,128)(2,1)}, bf16[2,2,2048,4480]{3,2,1,0:T(8,128)(2,1)}, bf16[4480,2048]{1,0:T(8,128)(2,1)}, bf16[2048,1280]{1,0:T(8,128)(2,1)}) custom-call(s32[3]{0:T(128)} %pad_add_fusion.at, bf16[2048,1280]{1,0:T(8,128)(2,1)} %get-tuple-element.85.h, bf16[2048,1280]{1,0:T(8,128)(2,1)} %bitcast.23, bf16[2,1280,4480]{2,1,0:T(8,128)(2,1)} %w.16, ...), custom_call_target="tpu_custom_call" | custom-call | flops 117440512000 | bytes 130000000 | tf_op jit(solution)/shard_map/second_back/pallas_call | solution.py:255
  238.5 60.5 %shard_map.179 = (bf16[2,2048,4480]{2,1,0:T(8,128)(2,1)}, bf16[2,2,320,4480]{3,2,1,0:T(8,128)(2,1)}) custom-call(s32[3]{0:T(128)} %pad_add_fusion.at, bf16[2,4480,1280]{2,1,0:T(8,128)(2,1)} %w.25, bf16[2048,1280]{1,0:T(8,128)(2,1)} %get-tuple-element.92.d.refs_1_, f32[9,2048,512]{2,1,0:T(8,128)} %get-tuple-element.87.s, ...), custom_call_target="tpu_custom_call" | custom-call | flops 46976204800 | bytes 160000000 | tf_op jit(solution)/shard_map/pallas_call | solution.py:39
  299.8 18.3 %shard_map.180 = bf16[2,1120,1280]{2,1,0:T(8,128)(2,1)} custom-call(s32[3]{0:T(128)} %pad_add_fusion.at, bf16[4,1120,2048]{2,1,0:T(8,128)(2,1)} %bitcast.27, bf16[2048,1280]{1,0:T(8,128)(2,1)} %get-tuple-element.92.d.refs_1_), custom_call_target="tpu_custom_call" | custom-call | flops 11744051200 | bytes 60000000 | tf_op jit(solution)/shard_map/pallas_call | solution.py:39
  323.1 32.1 %shard_map.181 = (bf16[2,320,4480]{2,1,0:T(8,128)(2,1)}, f32[2,320,4480]{2,1,0:T(8,128)}) custom-call(s32[3]{0:T(128)} %pad_add_fusion.at, bf16[4,320,2048]{2,1,0:T(8,128)(2,1)} %bitcast.32, bf16[4,320,2048]{2,1,0:T(8,128)(2,1)} %bitcast.33, bf16[2,2048,4480]{2,1,0:T(8,128)(2,1)} %get-tuple-element.89.right, bf16[2,2,320,4480]{3,2,1,0:T(8,128)(2,1)} %collective-permute-done.got), custom_call_target="tpu_custom_call" | custom-call | flops 23488102400 | bytes 60000000 | tf_op jit(solution)/shard_map/pallas_call | solution.py:39
  355.2 19.9 %shard_map.182 = (bf16[1120,1280]{1,0:T(8,128)(2,1)}, f32[1120,1280]{1,0:T(8,128)}) custom-call(s32[3]{0:T(128)} %pad_add_fusion.at, bf16[4,1120,2048]{2,1,0:T(8,128)(2,1)} %bitcast.28, bf16[2048,1280]{1,0:T(8,128)(2,1)} %get-tuple-element.92.d.refs_1_, bf16[2,1120,1280]{2,1,0:T(8,128)(2,1)} %collective-permute-done.2.refs_2_), custom_call_target="tpu_custom_call" | custom-call | flops 11744051200 | bytes 60000000 | tf_op jit(solution)/shard_map/pallas_call | solution.py:39
  375.1 60.1 %collective-permute-done.4.h = bf16[2048,1280]{1,0:T(8,128)(2,1)} collective-permute-done((bf16[2048,1280]{1,0:T(8,128)(2,1)}, bf16[2048,1280]{1,0:T(8,128)(2,1)}, u32[]{:S(2)}, u32[]{:S(2)}) %collective-permute-start.4) | collective-permute-done | bytes 5242912 | tf_op jit(solution)/shard_map/ppermute | solution.py:612
  435.3 112.4 %collective-permute-done.5.dy.refs_3_ = bf16[2048,1280]{1,0:T(8,128)(2,1)} collective-permute-done((bf16[2048,1280]{1,0:T(8,128)(2,1)}, bf16[2048,1280]{1,0:T(8,128)(2,1)}, u32[]{:S(2)}, u32[]{:S(2)}) %collective-permute-start.5) | collective-permute-done | bytes 5242912 | tf_op jit(solution)/shard_map/ppermute | solution.py:612
  547.6 90.4 %second.1 = (bf16[2,1280,2048]{2,1,0:T(8,128)(2,1)}, bf16[2,2,2048,4480]{3,2,1,0:T(8,128)(2,1)}, bf16[4480,2048]{1,0:T(8,128)(2,1)}) custom-call(s32[3]{0:T(128)} %pad_add_fusion.at, bf16[2048,1280]{1,0:T(8,128)(2,1)} %collective-permute-done.4.h, ...), custom_call_target="tpu_custom_call", output_to_operand_aliasing={{0}: (6, {}), {1}: (7, {})} | custom-call | flops 70464307200 | bytes 130000000 | tf_op jit(solution)/shard_map/second/pallas_call | solution.py:255
  638.1 109.3 %shard_map.183 = (bf16[4,320,4480]{2,1,0:T(8,128)(2,1)}, f32[4,320,4480]{2,1,0:T(8,128)}) custom-call(s32[3]{0:T(128)} %pad_add_fusion.at, bf16[2,1280,2048]{2,1,0:T(8,128)(2,1)} %get-tuple-element.102.left0.left1, bf16[2,1280,2048]{2,1,0:T(8,128)(2,1)} %get-tuple-element.102.left0.left1, bf16[2,2,2048,4480]{3,2,1,0:T(8,128)(2,1)} %get-tuple-element.103.right0.right1, ...), custom_call_target="tpu_custom_call" | custom-call | flops 93952409600 | bytes 120000000 | tf_op jit(solution)/shard_map/pallas_call | solution.py:39
  753.1 33.6 %shard_map.184 = (bf16[1120,1280]{1,0:T(8,128)(2,1)}, f32[1120,1280]{1,0:T(8,128)}) custom-call(s32[3]{0:T(128)} %pad_add_fusion.at, bf16[4,1120,2048]{2,1,0:T(8,128)(2,1)} %bitcast.26, bf16[2048,1280]{1,0:T(8,128)(2,1)} %bitcast.25, bf16[4,1120,2048]{2,1,0:T(8,128)(2,1)} %bitcast.29, bf16[2048,1280]{1,0:T(8,128)(2,1)} %collective-permute-done.5.dy.refs_3_), custom_call_target="tpu_custom_call" | custom-call | flops 23488102400 | bytes 60000000 | tf_op jit(solution)/shard_map/pallas_call | solution.py:39
  786.7 38.5 %collective-permute-done.22.refs_2_ = f32[320,2688]{1,0:T(8,128)} collective-permute-done((f32[320,2688]{1,0:T(8,128)}, f32[320,2688]{1,0:T(8,128)}, u32[]{:S(2)}, u32[]{:S(2)}) %collective-permute-start.22) | collective-permute-done | bytes 3440672 | tf_op jit(solution)/shard_map/ppermute | solution.py:612
  825.1 184.1 %collective-permute-done.3 = bf16[1120,1280]{1,0:T(8,128)(2,1)} collective-permute-done((bf16[1120,1280]{1,0:T(8,128)(2,1)}, bf16[1120,1280]{1,0:T(8,128)(2,1)}, u32[]{:S(2)}, u32[]{:S(2)}) %collective-permute-start.3) | collective-permute-done | bytes 2867232 | tf_op jit(solution)/shard_map/ppermute | solution.py:612
  1010.9 14.9 %squares.2 = f32[8,128]{1,0:T(8,128)} custom-call(f32[2,320,4480]{2,1,0:T(8,128)} %get-tuple-element.94.refs_0_.keep, bf16[2,320,4480]{2,1,0:T(8,128)(2,1)} %collective-permute-done.1.refs_1_.far, f32[1,1120,1280]{2,1,0:T(8,128)} %bitcast.19, bf16[1,1120,1280]{2,1,0:T(8,128)(2,1)} %bitcast.8.refs_3_.far, f32[4,320,4480]{2,1,0:T(8,128)} %get-tuple-element.104.refs_4_.keep, ...), custom_call_target="tpu_custom_call" | custom-call | flops 1000000000 | bytes 24000000 | tf_op jit(solution)/shard_map/squares/pallas_call | solution.py:462
  1051.6 11.8 shard_map.204
  1065.3 20.6 %collective-permute-done.23.refs_3_ = f32[320,2688]{1,0:T(8,128)} collective-permute-done((f32[320,2688]{1,0:T(8,128)}, f32[320,2688]{1,0:T(8,128)}, u32[]{:S(2)}, u32[]{:S(2)}) %collective-permute-start.23) | collective-permute-done | bytes 3440672 | tf_op jit(solution)/shard_map/ppermute | solution.py:635
  1087.3 14.3 %shard_map.192 = (bf16[320,4480]{1,0:T(8,128)(2,1)}, f32[2,320,4480]{2,1,0:T(8,128)}, f32[2,320,4480]{2,1,0:T(8,128)}, bf16[2,1280,4480]{2,1,0:T(8,128)(2,1)}) custom-call(s32[3]{0:T(128)} %pad_add_fusion.at, f32[1]{0:T(128)} %bitcast.13.factor, f32[2,320,4480]{2,1,0:T(8,128)} %get-tuple-element.94.refs_0_.keep, ...), custom_call_target="tpu_custom_call" | custom-call | flops 1000000000 | bytes 12000000 | tf_op jit(solution)/shard_map/pallas_call | solution.py:39
  1101.6 14.6 %shard_map.193 = (bf16[320,4480]{1,0:T(8,128)(2,1)}, f32[2,320,4480]{2,1,0:T(8,128)}, f32[2,320,4480]{2,1,0:T(8,128)}, bf16[2,1280,4480]{2,1,0:T(8,128)(2,1)}, bf16[320,896]{1,0:T(8,128)(2,1)}) custom-call(s32[3]{0:T(128)} %pad_add_fusion.at, f32[1]{0:T(128)} %bitcast.13.factor, ...), custom_call_target="tpu_custom_call", output_to_operand_aliasing={{1}: (7, {}), {2}: (8, {}), {3}: (9, {})} | custom-call | flops 1000000000 | bytes 12000000 | tf_op jit(solution)/shard_map/pallas_call | solution.py:39
  1117.3 8.4 collective-permute-done.30.refs_0_
  1129.2 12.1 collective-permute-done.28.refs_0_
  1141.9 14.2 %collective-permute-done.17.refs_0_ = bf16[320,896]{1,0:T(8,128)(2,1)} collective-permute-done((bf16[320,896]{1,0:T(8,128)(2,1)}, bf16[320,896]{1,0:T(8,128)(2,1)}, u32[]{:S(2)}, u32[]{:S(2)}) %collective-permute-start.17) | collective-permute-done | bytes 573472 | tf_op jit(solution)/shard_map/ppermute | solution.py:612
  1159.5 14.3 %shard_map.185 = (bf16[320,4480]{1,0:T(8,128)(2,1)}, f32[2,320,4480]{2,1,0:T(8,128)}, f32[2,320,4480]{2,1,0:T(8,128)}, bf16[2,1280,4480]{2,1,0:T(8,128)(2,1)}) custom-call(s32[3]{0:T(128)} %pad_add_fusion.at, f32[1]{0:T(128)} %bitcast.13.factor, f32[2,320,4480]{2,1,0:T(8,128)} %get-tuple-element.94.refs_0_.keep, ...), custom_call_target="tpu_custom_call" | custom-call | flops 1000000000 | bytes 12000000 | tf_op jit(solution)/shard_map/pallas_call | solution.py:39
  1173.8 14.3 %shard_map.186 = (bf16[320,4480]{1,0:T(8,128)(2,1)}, f32[2,320,4480]{2,1,0:T(8,128)}, f32[2,320,4480]{2,1,0:T(8,128)}, bf16[2,1280,4480]{2,1,0:T(8,128)(2,1)}) custom-call(s32[3]{0:T(128)} %pad_add_fusion.at, f32[1]{0:T(128)} %bitcast.13.factor, ...), custom_call_target="tpu_custom_call", output_to_operand_aliasing={{1}: (7, {}), {2}: (8, {}), {3}: (9, {})} | custom-call | flops 1000000000 | bytes 12000000 | tf_op jit(solution)/shard_map/pallas_call | solution.py:39
  1188.2 14.8 %shard_map.187 = (bf16[320,4480]{1,0:T(8,128)(2,1)}, bf16[2,1280,4480]{2,1,0:T(8,128)(2,1)}) custom-call(s32[3]{0:T(128)} %pad_add_fusion.at, f32[1]{0:T(128)} %bitcast.13.factor, f32[4,320,4480]{2,1,0:T(8,128)} %get-tuple-element.104.refs_4_.keep, bf16[4,320,4480]{2,1,0:T(8,128)(2,1)} %collective-permute-done.6.refs_5_.far, ...), custom_call_target="tpu_custom_call", output_to_operand_aliasing={{1}: (7, {})} | custom-call | flops 1000000000 | bytes 30000000 | tf_op jit(solution)/shard_map/pallas_call | solution.py:39
  1239.2 11.9 shard_map.217
  1251.1 7.2 shard_map.218
  1264.3 13.0 shard_map.195
  1277.3 8.4 collective-permute-done.10.refs_0_
  1286.3 24.1 %collective-permute-done.38.refs_0_ = bf16[448,1280]{1,0:T(8,128)(2,1)} collective-permute-done((bf16[448,1280]{1,0:T(8,128)(2,1)}, bf16[448,1280]{1,0:T(8,128)(2,1)}, u32[]{:S(2)}, u32[]{:S(2)}) %collective-permute-start.38) | collective-permute-done | bytes 1146912 | tf_op jit(solution)/shard_map/ppermute | solution.py:612
  1310.3 36.0 %collective-permute-done.40.refs_0_ = bf16[672,1280]{1,0:T(8,128)(2,1)} collective-permute-done((bf16[672,1280]{1,0:T(8,128)(2,1)}, bf16[672,1280]{1,0:T(8,128)(2,1)}, u32[]{:S(2)}, u32[]{:S(2)}) %collective-permute-start.40) | collective-permute-done | bytes 1720352 | tf_op jit(solution)/shard_map/ppermute | solution.py:612
  1346.4 6.8 shard_map.188.refs_1_
  1361.0 6.4 shard_map.196.refs_1_
  (121 shorter events, 141.3 us)
Async XLA Ops:
  318.0 37.2 %collective-permute-start.2 = (bf16[2,1120,1280]{2,1,0:T(8,128)(2,1)}, bf16[2,1120,1280]{2,1,0:T(8,128)(2,1)}, u32[]{:S(2)}, u32[]{:S(2)}) collective-permute-start(bf16[2,1120,1280]{2,1,0:T(8,128)(2,1)} %shard_map.180), channel_id=1, source_target_pairs={{0,1},{1,0},{2,3},{3,2},{4,5},{5,4},{6,7},{7,6}} | collective-permute-start | bytes 17203208 | tf_op jit(solution)/shard_map/ppermute | solution.py:616
  318.0 117.2 %collective-permute-start.4 = (bf16[2048,1280]{1,0:T(8,128)(2,1)}, bf16[2048,1280]{1,0:T(8,128)(2,1)}, u32[]{:S(2)}, u32[]{:S(2)}) collective-permute-start(bf16[2048,1280]{1,0:T(8,128)(2,1)} %get-tuple-element.85.h), channel_id=1, source_target_pairs={{0,2},{2,0},{1,3},{3,1},{4,6},{6,4},{5,7},{7,5}} | collective-permute-start | bytes 15728648 | tf_op jit(solution)/shard_map/ppermute | solution.py:612
  321.1 226.6 %collective-permute-start.5 = (bf16[2048,1280]{1,0:T(8,128)(2,1)}, bf16[2048,1280]{1,0:T(8,128)(2,1)}, u32[]{:S(2)}, u32[]{:S(2)}) collective-permute-start(bf16[2048,1280]{1,0:T(8,128)(2,1)} %bitcast.24), channel_id=1, source_target_pairs={{0,2},{2,0},{1,3},{3,1},{4,6},{6,4},{5,7},{7,5}} | collective-permute-start | bytes 15728648 | tf_op jit(solution)/shard_map/ppermute | solution.py:612
  321.1 428.5 %collective-permute-start.14 = (f32[320,5376]{1,0:T(8,128)}, f32[320,5376]{1,0:T(8,128)}, u32[]{:S(2)}, u32[]{:S(2)}) collective-permute-start(f32[320,5376]{1,0:T(8,128)} %get-tuple-element.117), channel_id=1, source_target_pairs={{0,2},{2,0},{1,3},{3,1},{4,6},{6,4},{5,7},{7,5}} | collective-permute-start | bytes 20643848 | tf_op jit(solution)/shard_map/ppermute | solution.py:612
  747.3 263.5 %collective-permute-start.6 = (bf16[4,320,4480]{2,1,0:T(8,128)(2,1)}, bf16[4,320,4480]{2,1,0:T(8,128)(2,1)}, u32[]{:S(2)}, u32[]{:S(2)}) collective-permute-start(bf16[4,320,4480]{2,1,0:T(8,128)(2,1)} %get-tuple-element.105), channel_id=1, source_target_pairs={{0,1},{1,0},{2,3},{3,2},{4,5},{5,4},{6,7},{7,6}} | collective-permute-start | bytes 34406408 | tf_op jit(solution)/shard_map/ppermute | solution.py:616
  747.4 77.8 %collective-permute-start.22 = (f32[320,2688]{1,0:T(8,128)}, f32[320,2688]{1,0:T(8,128)}, u32[]{:S(2)}, u32[]{:S(2)}) collective-permute-start(f32[320,2688]{1,0:T(8,128)} %get-tuple-element.126), channel_id=1, source_target_pairs={{0,2},{2,0},{1,3},{3,1},{4,6},{6,4},{5,7},{7,5}} | collective-permute-start | bytes 10321928 | tf_op jit(solution)/shard_map/ppermute | solution.py:612
  749.6 352.0 %collective-permute-start.15 = (f32[320,5376]{1,0:T(8,128)}, f32[320,5376]{1,0:T(8,128)}, u32[]{:S(2)}, u32[]{:S(2)}) collective-permute-start(f32[320,5376]{1,0:T(8,128)} %collective-permute-done.14.refs_0_), channel_id=1, source_target_pairs={{0,4},{4,0},{1,5},{5,1},{2,6},{6,2},{3,7},{7,3}} | collective-permute-start | bytes 20643848 | tf_op jit(solution)/shard_map/ppermute | solution.py:635
  751.1 259.8 %collective-permute-start.1 = (bf16[2,320,4480]{2,1,0:T(8,128)(2,1)}, bf16[2,320,4480]{2,1,0:T(8,128)(2,1)}, u32[]{:S(2)}, u32[]{:S(2)}) collective-permute-start(bf16[2,320,4480]{2,1,0:T(8,128)(2,1)} %get-tuple-element.95), channel_id=1, source_target_pairs={{0,2},{2,0},{1,3},{3,1},{4,6},{6,4},{5,7},{7,5}} | collective-permute-start | bytes 17203208 | tf_op jit(solution)/shard_map/ppermute | solution.py:612
  751.4 257.8 %collective-permute-start.3 = (bf16[1120,1280]{1,0:T(8,128)(2,1)}, bf16[1120,1280]{1,0:T(8,128)(2,1)}, u32[]{:S(2)}, u32[]{:S(2)}) collective-permute-start(bf16[1120,1280]{1,0:T(8,128)(2,1)} %get-tuple-element.98), channel_id=1, source_target_pairs={{0,2},{2,0},{1,3},{3,1},{4,6},{6,4},{5,7},{7,5}} | collective-permute-start | bytes 8601608 | tf_op jit(solution)/shard_map/ppermute | solution.py:612
  825.1 200.6 %collective-permute-start.7 = (bf16[1120,1280]{1,0:T(8,128)(2,1)}, bf16[1120,1280]{1,0:T(8,128)(2,1)}, u32[]{:S(2)}, u32[]{:S(2)}) collective-permute-start(bf16[1120,1280]{1,0:T(8,128)(2,1)} %get-tuple-element.110), channel_id=1, source_target_pairs={{0,1},{1,0},{2,3},{3,2},{4,5},{5,4},{6,7},{7,6}} | collective-permute-start | bytes 8601608 | tf_op jit(solution)/shard_map/ppermute | solution.py:616
  1009.3 76.5 %collective-permute-start.23 = (f32[320,2688]{1,0:T(8,128)}, f32[320,2688]{1,0:T(8,128)}, u32[]{:S(2)}, u32[]{:S(2)}) collective-permute-start(f32[320,2688]{1,0:T(8,128)} %collective-permute-done.22.refs_2_), channel_id=1, source_target_pairs={{0,4},{4,0},{1,5},{5,1},{2,6},{6,2},{3,7},{7,3}} | collective-permute-start | bytes 10321928 | tf_op jit(solution)/shard_map/ppermute | solution.py:635
  1041.4 74.8 %collective-permute-start.37 = (bf16[112,1280]{1,0:T(8,128)(2,1)}, bf16[112,1280]{1,0:T(8,128)(2,1)}, u32[]{:S(2)}, u32[]{:S(2)}) collective-permute-start(bf16[112,1280]{1,0:T(8,128)(2,1)} %get-tuple-element.145), channel_id=1, source_target_pairs={{0,1},{1,0},{2,3},{3,2},{4,5},{5,4},{6,7},{7,6}} | collective-permute-start | bytes 860168 | tf_op jit(solution)/shard_map/ppermute | solution.py:616
  1063.4 78.5 %collective-permute-start.26 = (bf16[672,1280]{1,0:T(8,128)(2,1)}, bf16[672,1280]{1,0:T(8,128)(2,1)}, u32[]{:S(2)}, u32[]{:S(2)}) collective-permute-start(bf16[672,1280]{1,0:T(8,128)(2,1)} %get-tuple-element.142), channel_id=1, source_target_pairs={{0,2},{2,0},{1,3},{3,1},{4,6},{6,4},{5,7},{7,5}} | collective-permute-start | bytes 5160968 | tf_op jit(solution)/shard_map/ppermute | solution.py:612
  1065.0 51.7 %collective-permute-start.36 = (bf16[112,1280]{1,0:T(8,128)(2,1)}, bf16[112,1280]{1,0:T(8,128)(2,1)}, u32[]{:S(2)}, u32[]{:S(2)}) collective-permute-start(bf16[112,1280]{1,0:T(8,128)(2,1)} %get-tuple-element.144), channel_id=1, source_target_pairs={{0,1},{1,0},{2,3},{3,2},{4,5},{5,4},{6,7},{7,6}} | collective-permute-start | bytes 860168 | tf_op jit(solution)/shard_map/ppermute | solution.py:616
  1085.8 31.5 %collective-permute-start.32 = (bf16[112,1280]{1,0:T(8,128)(2,1)}, bf16[112,1280]{1,0:T(8,128)(2,1)}, u32[]{:S(2)}, u32[]{:S(2)}) collective-permute-start(bf16[112,1280]{1,0:T(8,128)(2,1)} %get-tuple-element.145), channel_id=1, source_target_pairs={{0,2},{2,0},{1,3},{3,1},{4,6},{6,4},{5,7},{7,5}} | collective-permute-start | bytes 860168 | tf_op jit(solution)/shard_map/ppermute | solution.py:612
  1116.2 86.8 %collective-permute-start.24 = (bf16[320,4480]{1,0:T(8,128)(2,1)}, bf16[320,4480]{1,0:T(8,128)(2,1)}, u32[]{:S(2)}, u32[]{:S(2)}) collective-permute-start(bf16[320,4480]{1,0:T(8,128)(2,1)} %get-tuple-element.127), channel_id=1, source_target_pairs={{0,1},{1,0},{2,3},{3,2},{4,5},{5,4},{6,7},{7,6}} | collective-permute-start | bytes 8601608 | tf_op jit(solution)/shard_map/ppermute | solution.py:616
  1117.3 86.2 %collective-permute-start.21 = (bf16[320,4480]{1,0:T(8,128)(2,1)}, bf16[320,4480]{1,0:T(8,128)(2,1)}, u32[]{:S(2)}, u32[]{:S(2)}) collective-permute-start(bf16[320,4480]{1,0:T(8,128)(2,1)} %get-tuple-element.125), channel_id=1, source_target_pairs={{0,1},{1,0},{2,3},{3,2},{4,5},{5,4},{6,7},{7,6}} | collective-permute-start | bytes 8601608 | tf_op jit(solution)/shard_map/ppermute | solution.py:616
  1129.1 73.9 %collective-permute-start.34 = (bf16[672,1280]{1,0:T(8,128)(2,1)}, bf16[672,1280]{1,0:T(8,128)(2,1)}, u32[]{:S(2)}, u32[]{:S(2)}) collective-permute-start(bf16[672,1280]{1,0:T(8,128)(2,1)} %get-tuple-element.142), channel_id=1, source_target_pairs={{0,1},{1,0},{2,3},{3,2},{4,5},{5,4},{6,7},{7,6}} | collective-permute-start | bytes 5160968 | tf_op jit(solution)/shard_map/ppermute | solution.py:616
  1141.9 61.6 %collective-permute-start.27 = (bf16[672,1280]{1,0:T(8,128)(2,1)}, bf16[672,1280]{1,0:T(8,128)(2,1)}, u32[]{:S(2)}, u32[]{:S(2)}) collective-permute-start(bf16[672,1280]{1,0:T(8,128)(2,1)} %collective-permute-done.26.refs_0_), channel_id=1, source_target_pairs={{0,1},{1,0},{2,3},{3,2},{4,5},{5,4},{6,7},{7,6}} | collective-permute-start | bytes 5160968 | tf_op jit(solution)/shard_map/ppermute | solution.py:616
  1159.0 99.4 %collective-permute-start.19 = (bf16[320,4480]{1,0:T(8,128)(2,1)}, bf16[320,4480]{1,0:T(8,128)(2,1)}, u32[]{:S(2)}, u32[]{:S(2)}) collective-permute-start(bf16[320,4480]{1,0:T(8,128)(2,1)} %get-tuple-element.125), channel_id=1, source_target_pairs={{0,2},{2,0},{1,3},{3,1},{4,6},{6,4},{5,7},{7,5}} | collective-permute-start | bytes 8601608 | tf_op jit(solution)/shard_map/ppermute | solution.py:612
  1203.0 55.6 %collective-permute-start.16 = (bf16[320,4480]{1,0:T(8,128)(2,1)}, bf16[320,4480]{1,0:T(8,128)(2,1)}, u32[]{:S(2)}, u32[]{:S(2)}) collective-permute-start(bf16[320,4480]{1,0:T(8,128)(2,1)} %get-tuple-element.119), channel_id=1, source_target_pairs={{0,1},{1,0},{2,3},{3,2},{4,5},{5,4},{6,7},{7,6}} | collective-permute-start | bytes 8601608 | tf_op jit(solution)/shard_map/ppermute | solution.py:616
  1203.0 56.1 %collective-permute-start.13 = (bf16[320,4480]{1,0:T(8,128)(2,1)}, bf16[320,4480]{1,0:T(8,128)(2,1)}, u32[]{:S(2)}, u32[]{:S(2)}) collective-permute-start(bf16[320,4480]{1,0:T(8,128)(2,1)} %get-tuple-element.116), channel_id=1, source_target_pairs={{0,1},{1,0},{2,3},{3,2},{4,5},{5,4},{6,7},{7,6}} | collective-permute-start | bytes 8601608 | tf_op jit(solution)/shard_map/ppermute | solution.py:616
  1203.5 73.8 %collective-permute-start.12 = (bf16[320,4480]{1,0:T(8,128)(2,1)}, bf16[320,4480]{1,0:T(8,128)(2,1)}, u32[]{:S(2)}, u32[]{:S(2)}) collective-permute-start(bf16[320,4480]{1,0:T(8,128)(2,1)} %get-tuple-element.112), channel_id=1, source_target_pairs={{0,1},{1,0},{2,3},{3,2},{4,5},{5,4},{6,7},{7,6}} | collective-permute-start | bytes 8601608 | tf_op jit(solution)/shard_map/ppermute | solution.py:616
  1203.5 82.2 %collective-permute-start.10 = (bf16[320,4480]{1,0:T(8,128)(2,1)}, bf16[320,4480]{1,0:T(8,128)(2,1)}, u32[]{:S(2)}, u32[]{:S(2)}) collective-permute-start(bf16[320,4480]{1,0:T(8,128)(2,1)} %get-tuple-element.112), channel_id=1, source_target_pairs={{0,2},{2,0},{1,3},{3,1},{4,6},{6,4},{5,7},{7,5}} | collective-permute-start | bytes 8601608 | tf_op jit(solution)/shard_map/ppermute | solution.py:612
  1258.6 51.8 %collective-permute-start.38 = (bf16[448,1280]{1,0:T(8,128)(2,1)}, bf16[448,1280]{1,0:T(8,128)(2,1)}, u32[]{:S(2)}, u32[]{:S(2)}) collective-permute-start(bf16[448,1280]{1,0:T(8,128)(2,1)} %get-tuple-element.150), channel_id=1, source_target_pairs={{0,2},{2,0},{1,3},{3,1},{4,6},{6,4},{5,7},{7,5}} | collective-permute-start | bytes 3440648 | tf_op jit(solution)/shard_map/ppermute | solution.py:612
  1259.1 87.2 %collective-permute-start.40 = (bf16[672,1280]{1,0:T(8,128)(2,1)}, bf16[672,1280]{1,0:T(8,128)(2,1)}, u32[]{:S(2)}, u32[]{:S(2)}) collective-permute-start(bf16[672,1280]{1,0:T(8,128)(2,1)} %get-tuple-element.151), channel_id=1, source_target_pairs={{0,2},{2,0},{1,3},{3,1},{4,6},{6,4},{5,7},{7,5}} | collective-permute-start | bytes 5160968 | tf_op jit(solution)/shard_map/ppermute | solution.py:612
  1277.3 75.9 %collective-permute-start.25 = (bf16[320,3584]{1,0:T(8,128)(2,1)}, bf16[320,3584]{1,0:T(8,128)(2,1)}, u32[]{:S(2)}, u32[]{:S(2)}) collective-permute-start(bf16[320,3584]{1,0:T(8,128)(2,1)} %get-tuple-element.129), channel_id=1, source_target_pairs={{0,1},{1,0},{2,3},{3,2},{4,5},{5,4},{6,7},{7,6}} | collective-permute-start | bytes 6881288 | tf_op jit(solution)/shard_map/ppermute | solution.py:616
  1285.7 100.2 %collective-permute-start.20 = (bf16[320,4480]{1,0:T(8,128)(2,1)}, bf16[320,4480]{1,0:T(8,128)(2,1)}, u32[]{:S(2)}, u32[]{:S(2)}) collective-permute-start(bf16[320,4480]{1,0:T(8,128)(2,1)} %collective-permute-done.19.refs_0_), channel_id=1, source_target_pairs={{0,1},{1,0},{2,3},{3,2},{4,5},{5,4},{6,7},{7,6}} | collective-permute-start | bytes 8601608 | tf_op jit(solution)/shard_map/ppermute | solution.py:616
  1285.7 108.2 %collective-permute-start.11 = (bf16[320,4480]{1,0:T(8,128)(2,1)}, bf16[320,4480]{1,0:T(8,128)(2,1)}, u32[]{:S(2)}, u32[]{:S(2)}) collective-permute-start(bf16[320,4480]{1,0:T(8,128)(2,1)} %collective-permute-done.10.refs_0_), channel_id=1, source_target_pairs={{0,1},{1,0},{2,3},{3,2},{4,5},{5,4},{6,7},{7,6}} | collective-permute-start | bytes 8601608 | tf_op jit(solution)/shard_map/ppermute | solution.py:616
  1310.3 50.7 %collective-permute-start.43 = (bf16[672,1280]{1,0:T(8,128)(2,1)}, bf16[672,1280]{1,0:T(8,128)(2,1)}, u32[]{:S(2)}, u32[]{:S(2)}) collective-permute-start(bf16[672,1280]{1,0:T(8,128)(2,1)} %get-tuple-element.151), channel_id=1, source_target_pairs={{0,1},{1,0},{2,3},{3,2},{4,5},{5,4},{6,7},{7,6}} | collective-permute-start | bytes 5160968 | tf_op jit(solution)/shard_map/ppermute | solution.py:616
  1346.4 51.3 %collective-permute-start.41 = (bf16[672,1280]{1,0:T(8,128)(2,1)}, bf16[672,1280]{1,0:T(8,128)(2,1)}, u32[]{:S(2)}, u32[]{:S(2)}) collective-permute-start(bf16[672,1280]{1,0:T(8,128)(2,1)} %collective-permute-done.40.refs_0_), channel_id=1, source_target_pairs={{0,1},{1,0},{2,3},{3,2},{4,5},{5,4},{6,7},{7,6}} | collective-permute-start | bytes 5160968 | tf_op jit(solution)/shard_map/ppermute | solution.py:616
  1353.1 51.4 %collective-permute-start.39 = (bf16[448,1280]{1,0:T(8,128)(2,1)}, bf16[448,1280]{1,0:T(8,128)(2,1)}, u32[]{:S(2)}, u32[]{:S(2)}) collective-permute-start(bf16[448,1280]{1,0:T(8,128)(2,1)} %collective-permute-done.38.refs_0_), channel_id=1, source_target_pairs={{0,1},{1,0},{2,3},{3,2},{4,5},{5,4},{6,7},{7,6}} | collective-permute-start | bytes 3440648 | tf_op jit(solution)/shard_map/ppermute | solution.py:616
  (17 other events, 229.1 us)

commit v6 on v5

--- a/solution.py
+++ b/solution.py
@@ -78,7 +78,7 @@
     return jnp.where(lax.broadcasted_iota(jnp.int32, a.shape, axis) < n, a, jnp.zeros_like(a))
 
 
-PIECES, OF_UP, EARLY = 5, 4, 6
+PIECES, OF_UP, EARLY = 5, 2, 6
 
 
 def copied(at, step, moments, early, late, held, in_sems, out_sems):
@@ -336,8 +336,8 @@
     )
 
 
-def whole_kernel(at, left0, left1, right0, right1, send, keep, total, *, last):
-    needed = (pl.program_id(0) < 3) | (pl.program_id(1) < last)
+def whole_kernel(at, which, left0, left1, right0, right1, send, keep, total):
+    needed = (pl.program_id(0) == 0) | (pl.program_id(1) < which[1])
 
     @pl.when(needed)
     def _():
@@ -349,28 +349,27 @@
         send[...], keep[...] = jnp.zeros_like(send), jnp.zeros_like(keep)
 
 
-def grad_whole(at, left, right):
+def grad_whole(at, left, right, x, pieces):
     d, t = left.shape[1:]
     f = right.shape[3]
     rows, bn = d // 4, 768
-    same = pl.BlockSpec((None, rows, bn), lambda w, j, at: (w, 0, j))
-
-    def half(w, at):
-        return jnp.where(w < 2, at[0], 1 - at[0])
-
-    return call(
-        functools.partial(whole_kernel, last=pl.cdiv(f * OF_UP // PIECES, bn)),
-        at,
-        (4, pl.cdiv(f, bn)),
-        [pl.BlockSpec((None, 2 * rows, t), lambda w, j, at, x=x: (x, half(w, at), 0)) for x in range(2)]
-        + [pl.BlockSpec((None, None, t, bn), lambda w, j, at, x=x: (x, w % 2, 0, j)) for x in range(2)],
-        [same, same],
-        [out((4, rows, f)), out((4, rows, f), F32)],
-        (left, left, right, right),
-        8 * d * t * f,
-        120e6,
-        scratch=[pltpu.VMEM((2, rows, bn), F32)],
-    )
+    same = pl.BlockSpec((None, rows, bn), lambda w, j, at, which: (w, 0, j))
+    which = jnp.stack([x, jnp.full((), pl.cdiv(f * pieces // PIECES, bn), x.dtype)])
+    return pl.pallas_call(
+        whole_kernel,
+        grid_spec=pltpu.PrefetchScalarGridSpec(
+            num_scalar_prefetch=2,
+            grid=(2, pl.cdiv(f, bn)),
+            in_specs=[pl.BlockSpec((None, 2 * rows, t), lambda w, j, at, which, x=x: (x, which[0], 0)) for x in range(2)]
+            + [pl.BlockSpec((None, None, t, bn), lambda w, j, at, which, x=x: (x, w, 0, j)) for x in range(2)],
+            out_specs=[same, same],
+            scratch_shapes=[pltpu.VMEM((2, rows, bn), F32)],
+        ),
+        out_shape=[out((2, rows, f)), out((2, rows, f), F32)],
+        compiler_params=params(),
+        cost_estimate=cost(4 * d * t * f, 80e6),
+        name="grad_whole",
+    )(at, which, left, left, right, right)
 
 
 def tall_kernel(at, *refs, terms, add, keeps):
@@ -489,9 +488,9 @@
         w_out[r], m_out[r], v_out[r] = updated(gradient(factor, keep, far, r), w[r], m[r], v[r])
         w_new[r] = w_out[r]
 
-    cols = w.shape[1] // PIECES
+    cols = w.shape[1] // (PIECES if w.shape[1] > 2048 else 1)
     size = math.gcd(w.shape[0], 32)
-    loop(w.shape[0] // size, size, lambda r: loop(PIECES, cols, lambda c: rows((r, c))))
+    loop(w.shape[0] // size, size, lambda r: loop(w.shape[1] // cols, cols, lambda c: rows((r, c))))
     for o in tail:
         o[...] = w_out[:, w.shape[1] - o.shape[1] :]
 
@@ -651,7 +650,7 @@
 
     h1_far = after(h1_far, keep_down1)
     a2, dgu2, hid2f = second(at, h1_far, dy_far, w_gate, w_up, w_down, [a2, dgu2])
-    send, keep_wide2 = grad_whole(at, a2, dgu2)
+    send, keep_wide2 = grad_whole(at, a2, dgu2, at[0], PIECES)
     far_wide2 = sibling(send)
     pairs = [(blocks(hid2), dy), (blocks(after(hid2f, keep_wide2)), dy_far)]
     send, keep_down2 = grad_tall(at, pairs, on(True, False), on(True, True))
@@ -703,19 +702,21 @@
 
     def update_far(name, which, count):
         *moments, w = new[name]
-        arrays = keep_wide2, far_wide2, weights[name][0], far_moments
-        away, w = adam_far(at, factor, 1, which, (which - 2) * PIECES, count, *arrays, w)
+        arrays = keep_other, far_other, weights[name][0], far_moments
+        away, w = adam_far(at, factor, 1, which, which * PIECES, count, *arrays, w)
         new[name] = [*moments, w]
         return sibling(away)
 
     sent = {n: send(n) for n in range(len(PARTS) - 2)}
+    send_other, keep_other = grad_whole(at, a2, dgu2, 1 - at[0], OF_UP)
+    far_other = sibling(send_other)
     (own,) = update("gate1", whole)
-    last = update_far("gate", 2, PIECES)
+    last = update_far("gate", 0, PIECES)
     put("gate1", whole, (on(True, False), sibling(own)), (on(False, False), last))
     own, tail = update("up1", whole, f // PIECES * (PIECES - OF_UP))
     tail = across(tail)
     put("up1", whole, (on(True, False), sibling(own)))
-    last = update_far("up", 3, OF_UP)
+    last = update_far("up", 1, OF_UP)
     put("up1", whole, (on(False, False), last), piece=0)
     settle(sent)
     put("up1", whole, (on(False, True), tail), (on(False, False), sibling(tail)), piece=OF_UP)

time: 1420 us -> 1370 us (0.965)
  waiting for transfers between devices: 527 us -> 478 us
    pallas_call x47 -> x46, Pallas kernels: 596 us -> 482 us  [call(): pl.pallas_call(kernel, grid_spec=pltpu.PrefetchScalarGridSpec(num_scalar_...]
    pallas_call x0 -> x2, Pallas kernels: none -> 111 us  [grad_whole(): pl.pallas_call(whole_kernel, grid_spec=pltpu.PrefetchScalarGridSpec(num_s...]
    ppermute x16, waiting for transfers between devices: 500 us -> 477 us  [across(): return lax.ppermute(a, 'dp', ACROSS)]
    ppermute x2, waiting for transfers between devices: 20.6 us -> 0.01 us  [brought(): return (crossed, lax.ppermute(crossed, 'rep', [(0, 1), (1, 0)]))]
  transfers between devices with their start and end apart: 44 -> 45, of which waited for: 16 -> 10; matrix products, arithmetic and copies ran while one was open for 0% -> 0% of each run, Pallas kernels for 39% -> 40%
where the time goes in v6:
time: 1370 us; the launch traced here: 1360 us
  Pallas kernels  847 us (62%)
  waiting for transfers between devices  478 us (35%)
  starting transfers between devices  29.9 us (2%)
    pallas_call x46, Pallas kernels, call(): pl.pallas_call(kernel, grid_spec=pltpu.PrefetchScalarGridSpec(num_scalar_...  482 us
    ppermute x16, waiting for transfers between devices, across(): return lax.ppermute(a, 'dp', ACROSS)  477 us
    pallas_call x2, Pallas kernels, second(): pl.pallas_call(functools.partial(second_kernel if far else second_back_ke...  235 us
    pallas_call x2, Pallas kernels, grad_whole(): pl.pallas_call(whole_kernel, grid_spec=pltpu.PrefetchScalarGridSpec(num_s...  111 us
  transfers between devices with their start and end apart: 45, of which 10 were waited for; matrix products, arithmetic and copies ran while one was open for 0% of the time, Pallas kernels for 40%

profile of v6, /device:TPU:0, one launch (start us, length us, event | category | flops | bytes accessed | tf_op | source)
XLA Modules:
  0.0 1359.4 jit_solution(15517278271209574333)
XLA Ops:
  1.3 92.4 %shard_map.178 = (bf16[1280,2048]{1,0:T(8,128)(2,1)}, bf16[4480,2048]{1,0:T(8,128)(2,1)}, f32[9,2048,512]{2,1,0:T(8,128)}, f32[9,2048,512]{2,1,0:T(8,128)}, bf16...) custom-call(s32[3]{0:T(128)} %pad_add_fusion.at, bf16[2048,1280]{1,0:T(8,128)(2,1)} %bitcast.23, ...), custom_call_target="tpu_custom_call" | custom-call | flops 70464307200 | bytes 190000000 | tf_op jit(solution)/shard_map/pallas_call | solution.py:39
  93.7 144.2 %second_back.1 = (bf16[2,1280,2048]{2,1,0:T(8,128)(2,1)}, bf16[2,2,2048,4480]{3,2,1,0:T(8,128)(2,1)}, bf16[4480,2048]{1,0:T(8,128)(2,1)}, bf16[2048,1280]{1,0:T(8,128)(2,1)}) custom-call(s32[3]{0:T(128)} %pad_add_fusion.at, bf16[2048,1280]{1,0:T(8,128)(2,1)} %get-tuple-element.87.h, bf16[2048,1280]{1,0:T(8,128)(2,1)} %bitcast.24, bf16[2,1280,4480]{2,1,0:T(8,128)(2,1)} %w.16, ...), custom_call_target="tpu_custom_call" | custom-call | flops 117440512000 | bytes 130000000 | tf_op jit(solution)/shard_map/second_back/pallas_call | solution.py:255
  237.9 60.5 %shard_map.179 = (bf16[2,2048,4480]{2,1,0:T(8,128)(2,1)}, bf16[2,2,320,4480]{3,2,1,0:T(8,128)(2,1)}) custom-call(s32[3]{0:T(128)} %pad_add_fusion.at, bf16[2,4480,1280]{2,1,0:T(8,128)(2,1)} %w.25, bf16[2048,1280]{1,0:T(8,128)(2,1)} %get-tuple-element.94.d.refs_1_, f32[9,2048,512]{2,1,0:T(8,128)} %get-tuple-element.89.s, ...), custom_call_target="tpu_custom_call" | custom-call | flops 46976204800 | bytes 160000000 | tf_op jit(solution)/shard_map/pallas_call | solution.py:39
  301.7 18.3 %shard_map.180 = bf16[2,1120,1280]{2,1,0:T(8,128)(2,1)} custom-call(s32[3]{0:T(128)} %pad_add_fusion.at, bf16[4,1120,2048]{2,1,0:T(8,128)(2,1)} %bitcast.28, bf16[2048,1280]{1,0:T(8,128)(2,1)} %get-tuple-element.94.d.refs_1_), custom_call_target="tpu_custom_call" | custom-call | flops 11744051200 | bytes 60000000 | tf_op jit(solution)/shard_map/pallas_call | solution.py:39
  323.5 127.5 %collective-permute-done.15.refs_0_ = f32[320,5376]{1,0:T(8,128)} collective-permute-done((f32[320,5376]{1,0:T(8,128)}, f32[320,5376]{1,0:T(8,128)}, u32[]{:S(2)}, u32[]{:S(2)}) %collective-permute-start.15) | collective-permute-done | bytes 6881312 | tf_op jit(solution)/shard_map/ppermute | solution.py:611
  454.6 32.1 %shard_map.181 = (bf16[2,320,4480]{2,1,0:T(8,128)(2,1)}, f32[2,320,4480]{2,1,0:T(8,128)}) custom-call(s32[3]{0:T(128)} %pad_add_fusion.at, bf16[4,320,2048]{2,1,0:T(8,128)(2,1)} %bitcast.33, bf16[4,320,2048]{2,1,0:T(8,128)(2,1)} %bitcast.34, bf16[2,2048,4480]{2,1,0:T(8,128)(2,1)} %get-tuple-element.91.right, bf16[2,2,320,4480]{3,2,1,0:T(8,128)(2,1)} %collective-permute-done.got), custom_call_target="tpu_custom_call" | custom-call | flops 23488102400 | bytes 60000000 | tf_op jit(solution)/shard_map/pallas_call | solution.py:39
  487.3 19.9 %shard_map.182 = (bf16[1120,1280]{1,0:T(8,128)(2,1)}, f32[1120,1280]{1,0:T(8,128)}) custom-call(s32[3]{0:T(128)} %pad_add_fusion.at, bf16[4,1120,2048]{2,1,0:T(8,128)(2,1)} %bitcast.29, bf16[2048,1280]{1,0:T(8,128)(2,1)} %get-tuple-element.94.d.refs_1_, bf16[2,1120,1280]{2,1,0:T(8,128)(2,1)} %collective-permute-done.2.refs_2_), custom_call_target="tpu_custom_call" | custom-call | flops 11744051200 | bytes 60000000 | tf_op jit(solution)/shard_map/pallas_call | solution.py:39
  507.2 56.2 %collective-permute-done.4.h = bf16[2048,1280]{1,0:T(8,128)(2,1)} collective-permute-done((bf16[2048,1280]{1,0:T(8,128)(2,1)}, bf16[2048,1280]{1,0:T(8,128)(2,1)}, u32[]{:S(2)}, u32[]{:S(2)}) %collective-permute-start.4) | collective-permute-done | bytes 5242912 | tf_op jit(solution)/shard_map/ppermute | solution.py:611
  565.4 110.3 %collective-permute-done.5.dy.refs_3_ = bf16[2048,1280]{1,0:T(8,128)(2,1)} collective-permute-done((bf16[2048,1280]{1,0:T(8,128)(2,1)}, bf16[2048,1280]{1,0:T(8,128)(2,1)}, u32[]{:S(2)}, u32[]{:S(2)}) %collective-permute-start.5) | collective-permute-done | bytes 5242912 | tf_op jit(solution)/shard_map/ppermute | solution.py:611
  675.7 90.5 %second.1 = (bf16[2,1280,2048]{2,1,0:T(8,128)(2,1)}, bf16[2,2,2048,4480]{3,2,1,0:T(8,128)(2,1)}, bf16[4480,2048]{1,0:T(8,128)(2,1)}) custom-call(s32[3]{0:T(128)} %pad_add_fusion.at, bf16[2048,1280]{1,0:T(8,128)(2,1)} %collective-permute-done.4.h, ...), custom_call_target="tpu_custom_call", output_to_operand_aliasing={{0}: (6, {}), {1}: (7, {})} | custom-call | flops 70464307200 | bytes 130000000 | tf_op jit(solution)/shard_map/second/pallas_call | solution.py:255
  766.2 59.0 %grad_whole.2 = (bf16[2,320,4480]{2,1,0:T(8,128)(2,1)}, f32[2,320,4480]{2,1,0:T(8,128)}) custom-call(s32[3]{0:T(128)} %pad_add_fusion.at, s32[2]{0:T(128)} %pad_add_fusion.1.which, bf16[2,1280,2048]{2,1,0:T(8,128)(2,1)} %get-tuple-element.104.left0.left1, bf16[2,1280,2048]{2,1,0:T(8,128)(2,1)} %get-tuple-element.104.left0.left1, ...), custom_call_target="tpu_custom_call" | custom-call | flops 46976204800 | bytes 80000000 | tf_op jit(solution)/shard_map/grad_whole/pallas_call | solution.py:358
  825.2 52.0 %grad_whole.3 = (bf16[2,320,4480]{2,1,0:T(8,128)(2,1)}, f32[2,320,4480]{2,1,0:T(8,128)}) custom-call(s32[3]{0:T(128)} %pad_add_fusion.at, s32[2]{0:T(128)} %pad_add_fusion.2.which, bf16[2,1280,2048]{2,1,0:T(8,128)(2,1)} %get-tuple-element.104.left0.left1, bf16[2,1280,2048]{2,1,0:T(8,128)(2,1)} %get-tuple-element.104.left0.left1, ...), custom_call_target="tpu_custom_call" | custom-call | flops 46976204800 | bytes 80000000 | tf_op jit(solution)/shard_map/grad_whole/pallas_call | solution.py:358
  877.7 33.7 %shard_map.183 = (bf16[1120,1280]{1,0:T(8,128)(2,1)}, f32[1120,1280]{1,0:T(8,128)}) custom-call(s32[3]{0:T(128)} %pad_add_fusion.at, bf16[4,1120,2048]{2,1,0:T(8,128)(2,1)} %bitcast.27, bf16[2048,1280]{1,0:T(8,128)(2,1)} %bitcast.26, bf16[4,1120,2048]{2,1,0:T(8,128)(2,1)} %bitcast.30, bf16[2048,1280]{1,0:T(8,128)(2,1)} %collective-permute-done.5.dy.refs_3_), custom_call_target="tpu_custom_call" | custom-call | flops 23488102400 | bytes 60000000 | tf_op jit(solution)/shard_map/pallas_call | solution.py:39
  913.5 14.8 %squares.2 = f32[8,128]{1,0:T(8,128)} custom-call(f32[2,320,4480]{2,1,0:T(8,128)} %get-tuple-element.96.refs_0_.keep, bf16[2,320,4480]{2,1,0:T(8,128)(2,1)} %collective-permute-done.1.refs_1_.far, f32[1,1120,1280]{2,1,0:T(8,128)} %bitcast.20, bf16[1,1120,1280]{2,1,0:T(8,128)(2,1)} %bitcast.8.refs_3_.far, f32[2,320,4480]{2,1,0:T(8,128)} %get-tuple-element.106.refs_4_.keep, ...), custom_call_target="tpu_custom_call" | custom-call | flops 1000000000 | bytes 24000000 | tf_op jit(solution)/shard_map/squares/pallas_call | solution.py:461
  928.4 4.6 squares.3
  939.7 14.3 %shard_map.191 = (bf16[320,4480]{1,0:T(8,128)(2,1)}, f32[2,320,4480]{2,1,0:T(8,128)}, f32[2,320,4480]{2,1,0:T(8,128)}, bf16[2,1280,4480]{2,1,0:T(8,128)(2,1)}) custom-call(s32[3]{0:T(128)} %pad_add_fusion.at, f32[1]{0:T(128)} %bitcast.13.factor, f32[2,320,4480]{2,1,0:T(8,128)} %get-tuple-element.96.refs_0_.keep, ...), custom_call_target="tpu_custom_call" | custom-call | flops 1000000000 | bytes 12000000 | tf_op jit(solution)/shard_map/pallas_call | solution.py:39
  954.0 14.6 %shard_map.192 = (bf16[320,4480]{1,0:T(8,128)(2,1)}, f32[2,320,4480]{2,1,0:T(8,128)}, f32[2,320,4480]{2,1,0:T(8,128)}, bf16[2,1280,4480]{2,1,0:T(8,128)(2,1)}, bf16[320,2688]{1,0:T(8,128)(2,1)}) custom-call(s32[3]{0:T(128)} %pad_add_fusion.at, f32[1]{0:T(128)} %bitcast.13.factor, ...), custom_call_target="tpu_custom_call", output_to_operand_aliasing={{1}: (7, {}), {2}: (8, {}), {3}: (9, {})} | custom-call | flops 1000000000 | bytes 12000000 | tf_op jit(solution)/shard_map/pallas_call | solution.py:39
  978.4 5.7 shard_map.202
  986.1 29.4 %collective-permute-done.31.refs_0_ = bf16[112,1280]{1,0:T(8,128)(2,1)} collective-permute-done((bf16[112,1280]{1,0:T(8,128)(2,1)}, bf16[112,1280]{1,0:T(8,128)(2,1)}, u32[]{:S(2)}, u32[]{:S(2)}) %collective-permute-start.31) | collective-permute-done | bytes 286752 | tf_op jit(solution)/shard_map/ppermute | solution.py:611
  1015.6 16.9 %collective-permute-done.33.refs_0_ = bf16[112,1280]{1,0:T(8,128)(2,1)} collective-permute-done((bf16[112,1280]{1,0:T(8,128)(2,1)}, bf16[112,1280]{1,0:T(8,128)(2,1)}, u32[]{:S(2)}, u32[]{:S(2)}) %collective-permute-start.33) | collective-permute-done | bytes 286752 | tf_op jit(solution)/shard_map/ppermute | solution.py:611
  1033.5 14.3 %shard_map.184 = (bf16[320,4480]{1,0:T(8,128)(2,1)}, f32[2,320,4480]{2,1,0:T(8,128)}, f32[2,320,4480]{2,1,0:T(8,128)}, bf16[2,1280,4480]{2,1,0:T(8,128)(2,1)}) custom-call(s32[3]{0:T(128)} %pad_add_fusion.at, f32[1]{0:T(128)} %bitcast.13.factor, f32[2,320,4480]{2,1,0:T(8,128)} %get-tuple-element.96.refs_0_.keep, ...), custom_call_target="tpu_custom_call" | custom-call | flops 1000000000 | bytes 12000000 | tf_op jit(solution)/shard_map/pallas_call | solution.py:39
  1049.9 11.7 shard_map.203
  1062.2 14.3 %shard_map.185 = (bf16[320,4480]{1,0:T(8,128)(2,1)}, f32[2,320,4480]{2,1,0:T(8,128)}, f32[2,320,4480]{2,1,0:T(8,128)}, bf16[2,1280,4480]{2,1,0:T(8,128)(2,1)}) custom-call(s32[3]{0:T(128)} %pad_add_fusion.at, f32[1]{0:T(128)} %bitcast.13.factor, ...), custom_call_target="tpu_custom_call", output_to_operand_aliasing={{1}: (7, {}), {2}: (8, {}), {3}: (9, {})} | custom-call | flops 1000000000 | bytes 12000000 | tf_op jit(solution)/shard_map/pallas_call | solution.py:39
  1076.5 72.6 %collective-permute-done.27.refs_0_ = bf16[672,1280]{1,0:T(8,128)(2,1)} collective-permute-done((bf16[672,1280]{1,0:T(8,128)(2,1)}, bf16[672,1280]{1,0:T(8,128)(2,1)}, u32[]{:S(2)}, u32[]{:S(2)}) %collective-permute-start.27) | collective-permute-done | bytes 1720352 | tf_op jit(solution)/shard_map/ppermute | solution.py:611
  1149.1 14.8 %shard_map.186 = (bf16[320,4480]{1,0:T(8,128)(2,1)}, bf16[2,1280,4480]{2,1,0:T(8,128)(2,1)}) custom-call(s32[3]{0:T(128)} %pad_add_fusion.at, f32[1]{0:T(128)} %bitcast.13.factor, f32[2,320,4480]{2,1,0:T(8,128)} %get-tuple-element.119.keep, bf16[2,320,4480]{2,1,0:T(8,128)(2,1)} %collective-permute-done.14.far, ...), custom_call_target="tpu_custom_call", output_to_operand_aliasing={{1}: (7, {})} | custom-call | flops 1000000000 | bytes 30000000 | tf_op jit(solution)/shard_map/pallas_call | solution.py:39
  1200.2 7.6 shard_map.194
  1212.1 11.8 shard_map.216
  1223.8 7.2 shard_map.217
  1233.6 25.9 %collective-permute-done.39.refs_0_ = bf16[448,1280]{1,0:T(8,128)(2,1)} collective-permute-done((bf16[448,1280]{1,0:T(8,128)(2,1)}, bf16[448,1280]{1,0:T(8,128)(2,1)}, u32[]{:S(2)}, u32[]{:S(2)}) %collective-permute-start.39) | collective-permute-done | bytes 1146912 | tf_op jit(solution)/shard_map/ppermute | solution.py:611
  1260.0 35.9 %collective-permute-done.41.refs_0_ = bf16[672,1280]{1,0:T(8,128)(2,1)} collective-permute-done((bf16[672,1280]{1,0:T(8,128)(2,1)}, bf16[672,1280]{1,0:T(8,128)(2,1)}, u32[]{:S(2)}, u32[]{:S(2)}) %collective-permute-start.41) | collective-permute-done | bytes 1720352 | tf_op jit(solution)/shard_map/ppermute | solution.py:611
  1295.9 6.8 shard_map.187.refs_1_
  1340.5 8.9 shard_map.199
  (116 shorter events, 128.8 us)
Async XLA Ops:
  298.4 154.7 %collective-permute-start = (bf16[2,2,320,4480]{3,2,1,0:T(8,128)(2,1)}, bf16[2,2,320,4480]{3,2,1,0:T(8,128)(2,1)}, u32[]{:S(2)}, u32[]{:S(2)}) collective-permute-start(bf16[2,2,320,4480]{3,2,1,0:T(8,128)(2,1)} %get-tuple-element.92), channel_id=1, source_target_pairs={{0,1},{1,0},{2,3},{3,2},{4,5},{5,4},{6,7},{7,6}} | collective-permute-start | bytes 34406408 | tf_op jit(solution)/shard_map/ppermute | solution.py:615
  299.2 151.8 %collective-permute-start.15 = (f32[320,5376]{1,0:T(8,128)}, f32[320,5376]{1,0:T(8,128)}, u32[]{:S(2)}, u32[]{:S(2)}) collective-permute-start(f32[320,5376]{1,0:T(8,128)} %get-tuple-element.121), channel_id=1, source_target_pairs={{0,2},{2,0},{1,3},{3,1},{4,6},{6,4},{5,7},{7,5}} | collective-permute-start | bytes 20643848 | tf_op jit(solution)/shard_map/ppermute | solution.py:611
  320.0 166.7 %collective-permute-start.2 = (bf16[2,1120,1280]{2,1,0:T(8,128)(2,1)}, bf16[2,1120,1280]{2,1,0:T(8,128)(2,1)}, u32[]{:S(2)}, u32[]{:S(2)}) collective-permute-start(bf16[2,1120,1280]{2,1,0:T(8,128)(2,1)} %shard_map.180), channel_id=1, source_target_pairs={{0,1},{1,0},{2,3},{3,2},{4,5},{5,4},{6,7},{7,6}} | collective-permute-start | bytes 17203208 | tf_op jit(solution)/shard_map/ppermute | solution.py:615
  320.2 243.2 %collective-permute-start.4 = (bf16[2048,1280]{1,0:T(8,128)(2,1)}, bf16[2048,1280]{1,0:T(8,128)(2,1)}, u32[]{:S(2)}, u32[]{:S(2)}) collective-permute-start(bf16[2048,1280]{1,0:T(8,128)(2,1)} %get-tuple-element.87.h), channel_id=1, source_target_pairs={{0,2},{2,0},{1,3},{3,1},{4,6},{6,4},{5,7},{7,5}} | collective-permute-start | bytes 15728648 | tf_op jit(solution)/shard_map/ppermute | solution.py:611
  320.5 355.3 %collective-permute-start.5 = (bf16[2048,1280]{1,0:T(8,128)(2,1)}, bf16[2048,1280]{1,0:T(8,128)(2,1)}, u32[]{:S(2)}, u32[]{:S(2)}) collective-permute-start(bf16[2048,1280]{1,0:T(8,128)(2,1)} %bitcast.25), channel_id=1, source_target_pairs={{0,2},{2,0},{1,3},{3,1},{4,6},{6,4},{5,7},{7,5}} | collective-permute-start | bytes 15728648 | tf_op jit(solution)/shard_map/ppermute | solution.py:611
  451.0 426.2 %collective-permute-start.23 = (f32[320,896]{1,0:T(8,128)}, f32[320,896]{1,0:T(8,128)}, u32[]{:S(2)}, u32[]{:S(2)}) collective-permute-start(f32[320,896]{1,0:T(8,128)} %get-tuple-element.130), channel_id=1, source_target_pairs={{0,2},{2,0},{1,3},{3,1},{4,6},{6,4},{5,7},{7,5}} | collective-permute-start | bytes 3440648 | tf_op jit(solution)/shard_map/ppermute | solution.py:611
  453.0 532.6 %collective-permute-start.16 = (f32[320,5376]{1,0:T(8,128)}, f32[320,5376]{1,0:T(8,128)}, u32[]{:S(2)}, u32[]{:S(2)}) collective-permute-start(f32[320,5376]{1,0:T(8,128)} %collective-permute-done.15.refs_0_), channel_id=1, source_target_pairs={{0,4},{4,0},{1,5},{5,1},{2,6},{6,2},{3,7},{7,3}} | collective-permute-start | bytes 20643848 | tf_op jit(solution)/shard_map/ppermute | solution.py:634
  486.7 424.7 %collective-permute-start.1 = (bf16[2,320,4480]{2,1,0:T(8,128)(2,1)}, bf16[2,320,4480]{2,1,0:T(8,128)(2,1)}, u32[]{:S(2)}, u32[]{:S(2)}) collective-permute-start(bf16[2,320,4480]{2,1,0:T(8,128)(2,1)} %get-tuple-element.97), channel_id=1, source_target_pairs={{0,2},{2,0},{1,3},{3,1},{4,6},{6,4},{5,7},{7,5}} | collective-permute-start | bytes 17203208 | tf_op jit(solution)/shard_map/ppermute | solution.py:611
  563.4 348.0 %collective-permute-start.3 = (bf16[1120,1280]{1,0:T(8,128)(2,1)}, bf16[1120,1280]{1,0:T(8,128)(2,1)}, u32[]{:S(2)}, u32[]{:S(2)}) collective-permute-start(bf16[1120,1280]{1,0:T(8,128)(2,1)} %get-tuple-element.100), channel_id=1, source_target_pairs={{0,2},{2,0},{1,3},{3,1},{4,6},{6,4},{5,7},{7,5}} | collective-permute-start | bytes 8601608 | tf_op jit(solution)/shard_map/ppermute | solution.py:611
  825.2 88.3 %collective-permute-start.6 = (bf16[2,320,4480]{2,1,0:T(8,128)(2,1)}, bf16[2,320,4480]{2,1,0:T(8,128)(2,1)}, u32[]{:S(2)}, u32[]{:S(2)}) collective-permute-start(bf16[2,320,4480]{2,1,0:T(8,128)(2,1)} %get-tuple-element.107), channel_id=1, source_target_pairs={{0,1},{1,0},{2,3},{3,2},{4,5},{5,4},{6,7},{7,6}} | collective-permute-start | bytes 17203208 | tf_op jit(solution)/shard_map/ppermute | solution.py:615
  877.2 108.9 %collective-permute-start.14 = (bf16[2,320,4480]{2,1,0:T(8,128)(2,1)}, bf16[2,320,4480]{2,1,0:T(8,128)(2,1)}, u32[]{:S(2)}, u32[]{:S(2)}) collective-permute-start(bf16[2,320,4480]{2,1,0:T(8,128)(2,1)} %get-tuple-element.120), channel_id=1, source_target_pairs={{0,1},{1,0},{2,3},{3,2},{4,5},{5,4},{6,7},{7,6}} | collective-permute-start | bytes 17203208 | tf_op jit(solution)/shard_map/ppermute | solution.py:615
  911.4 72.7 %collective-permute-start.24 = (f32[320,896]{1,0:T(8,128)}, f32[320,896]{1,0:T(8,128)}, u32[]{:S(2)}, u32[]{:S(2)}) collective-permute-start(f32[320,896]{1,0:T(8,128)} %collective-permute-done.23.refs_2_), channel_id=1, source_target_pairs={{0,4},{4,0},{1,5},{5,1},{2,6},{6,2},{3,7},{7,3}} | collective-permute-start | bytes 3440648 | tf_op jit(solution)/shard_map/ppermute | solution.py:634
  968.7 93.5 %collective-permute-start.18 = (bf16[320,2688]{1,0:T(8,128)(2,1)}, bf16[320,2688]{1,0:T(8,128)(2,1)}, u32[]{:S(2)}, u32[]{:S(2)}) collective-permute-start(bf16[320,2688]{1,0:T(8,128)(2,1)} %get-tuple-element.128), channel_id=1, source_target_pairs={{0,2},{2,0},{1,3},{3,1},{4,6},{6,4},{5,7},{7,5}} | collective-permute-start | bytes 5160968 | tf_op jit(solution)/shard_map/ppermute | solution.py:611
  984.1 48.9 %collective-permute-start.29 = (bf16[224,1280]{1,0:T(8,128)(2,1)}, bf16[224,1280]{1,0:T(8,128)(2,1)}, u32[]{:S(2)}, u32[]{:S(2)}) collective-permute-start(bf16[224,1280]{1,0:T(8,128)(2,1)} %get-tuple-element.147), channel_id=1, source_target_pairs={{0,2},{2,0},{1,3},{3,1},{4,6},{6,4},{5,7},{7,5}} | collective-permute-start | bytes 1720328 | tf_op jit(solution)/shard_map/ppermute | solution.py:611
  985.6 46.9 %collective-permute-start.33 = (bf16[112,1280]{1,0:T(8,128)(2,1)}, bf16[112,1280]{1,0:T(8,128)(2,1)}, u32[]{:S(2)}, u32[]{:S(2)}) collective-permute-start(bf16[112,1280]{1,0:T(8,128)(2,1)} %get-tuple-element.149), channel_id=1, source_target_pairs={{0,2},{2,0},{1,3},{3,1},{4,6},{6,4},{5,7},{7,5}} | collective-permute-start | bytes 860168 | tf_op jit(solution)/shard_map/ppermute | solution.py:611
  986.1 46.3 %collective-permute-start.37 = (bf16[112,1280]{1,0:T(8,128)(2,1)}, bf16[112,1280]{1,0:T(8,128)(2,1)}, u32[]{:S(2)}, u32[]{:S(2)}) collective-permute-start(bf16[112,1280]{1,0:T(8,128)(2,1)} %get-tuple-element.148), channel_id=1, source_target_pairs={{0,1},{1,0},{2,3},{3,2},{4,5},{5,4},{6,7},{7,6}} | collective-permute-start | bytes 860168 | tf_op jit(solution)/shard_map/ppermute | solution.py:615
  1047.8 116.6 %collective-permute-start.10 = (bf16[320,4480]{1,0:T(8,128)(2,1)}, bf16[320,4480]{1,0:T(8,128)(2,1)}, u32[]{:S(2)}, u32[]{:S(2)}) collective-permute-start(bf16[320,4480]{1,0:T(8,128)(2,1)} %get-tuple-element.114), channel_id=1, source_target_pairs={{0,2},{2,0},{1,3},{3,1},{4,6},{6,4},{5,7},{7,5}} | collective-permute-start | bytes 8601608 | tf_op jit(solution)/shard_map/ppermute | solution.py:611
  1049.4 116.6 %collective-permute-start.12 = (bf16[320,4480]{1,0:T(8,128)(2,1)}, bf16[320,4480]{1,0:T(8,128)(2,1)}, u32[]{:S(2)}, u32[]{:S(2)}) collective-permute-start(bf16[320,4480]{1,0:T(8,128)(2,1)} %get-tuple-element.114), channel_id=1, source_target_pairs={{0,1},{1,0},{2,3},{3,2},{4,5},{5,4},{6,7},{7,6}} | collective-permute-start | bytes 8601608 | tf_op jit(solution)/shard_map/ppermute | solution.py:615
  1049.4 116.6 %collective-permute-start.25 = (bf16[320,4480]{1,0:T(8,128)(2,1)}, bf16[320,4480]{1,0:T(8,128)(2,1)}, u32[]{:S(2)}, u32[]{:S(2)}) collective-permute-start(bf16[320,4480]{1,0:T(8,128)(2,1)} %get-tuple-element.131), channel_id=1, source_target_pairs={{0,1},{1,0},{2,3},{3,2},{4,5},{5,4},{6,7},{7,6}} | collective-permute-start | bytes 8601608 | tf_op jit(solution)/shard_map/ppermute | solution.py:615
  1061.6 87.5 %collective-permute-start.27 = (bf16[672,1280]{1,0:T(8,128)(2,1)}, bf16[672,1280]{1,0:T(8,128)(2,1)}, u32[]{:S(2)}, u32[]{:S(2)}) collective-permute-start(bf16[672,1280]{1,0:T(8,128)(2,1)} %get-tuple-element.146), channel_id=1, source_target_pairs={{0,2},{2,0},{1,3},{3,1},{4,6},{6,4},{5,7},{7,5}} | collective-permute-start | bytes 5160968 | tf_op jit(solution)/shard_map/ppermute | solution.py:611
  1062.2 101.8 %collective-permute-start.35 = (bf16[672,1280]{1,0:T(8,128)(2,1)}, bf16[672,1280]{1,0:T(8,128)(2,1)}, u32[]{:S(2)}, u32[]{:S(2)}) collective-permute-start(bf16[672,1280]{1,0:T(8,128)(2,1)} %get-tuple-element.146), channel_id=1, source_target_pairs={{0,1},{1,0},{2,3},{3,2},{4,5},{5,4},{6,7},{7,6}} | collective-permute-start | bytes 5160968 | tf_op jit(solution)/shard_map/ppermute | solution.py:615
  1149.1 82.0 %collective-permute-start.13 = (bf16[320,4480]{1,0:T(8,128)(2,1)}, bf16[320,4480]{1,0:T(8,128)(2,1)}, u32[]{:S(2)}, u32[]{:S(2)}) collective-permute-start(bf16[320,4480]{1,0:T(8,128)(2,1)} %get-tuple-element.118), channel_id=1, source_target_pairs={{0,1},{1,0},{2,3},{3,2},{4,5},{5,4},{6,7},{7,6}} | collective-permute-start | bytes 8601608 | tf_op jit(solution)/shard_map/ppermute | solution.py:615
  1163.9 67.7 %collective-permute-start.17 = (bf16[320,4480]{1,0:T(8,128)(2,1)}, bf16[320,4480]{1,0:T(8,128)(2,1)}, u32[]{:S(2)}, u32[]{:S(2)}) collective-permute-start(bf16[320,4480]{1,0:T(8,128)(2,1)} %get-tuple-element.123), channel_id=1, source_target_pairs={{0,1},{1,0},{2,3},{3,2},{4,5},{5,4},{6,7},{7,6}} | collective-permute-start | bytes 8601608 | tf_op jit(solution)/shard_map/ppermute | solution.py:615
  1164.4 68.7 %collective-permute-start.20 = (bf16[320,4480]{1,0:T(8,128)(2,1)}, bf16[320,4480]{1,0:T(8,128)(2,1)}, u32[]{:S(2)}, u32[]{:S(2)}) collective-permute-start(bf16[320,4480]{1,0:T(8,128)(2,1)} %get-tuple-element.129), channel_id=1, source_target_pairs={{0,2},{2,0},{1,3},{3,1},{4,6},{6,4},{5,7},{7,5}} | collective-permute-start | bytes 8601608 | tf_op jit(solution)/shard_map/ppermute | solution.py:611
  1165.9 67.2 %collective-permute-start.22 = (bf16[320,4480]{1,0:T(8,128)(2,1)}, bf16[320,4480]{1,0:T(8,128)(2,1)}, u32[]{:S(2)}, u32[]{:S(2)}) collective-permute-start(bf16[320,4480]{1,0:T(8,128)(2,1)} %get-tuple-element.129), channel_id=1, source_target_pairs={{0,1},{1,0},{2,3},{3,2},{4,5},{5,4},{6,7},{7,6}} | collective-permute-start | bytes 8601608 | tf_op jit(solution)/shard_map/ppermute | solution.py:615
  1231.6 64.3 %collective-permute-start.41 = (bf16[672,1280]{1,0:T(8,128)(2,1)}, bf16[672,1280]{1,0:T(8,128)(2,1)}, u32[]{:S(2)}, u32[]{:S(2)}) collective-permute-start(bf16[672,1280]{1,0:T(8,128)(2,1)} %get-tuple-element.155), channel_id=1, source_target_pairs={{0,2},{2,0},{1,3},{3,1},{4,6},{6,4},{5,7},{7,5}} | collective-permute-start | bytes 5160968 | tf_op jit(solution)/shard_map/ppermute | solution.py:611
  1233.1 100.0 %collective-permute-start.11 = (bf16[320,4480]{1,0:T(8,128)(2,1)}, bf16[320,4480]{1,0:T(8,128)(2,1)}, u32[]{:S(2)}, u32[]{:S(2)}) collective-permute-start(bf16[320,4480]{1,0:T(8,128)(2,1)} %collective-permute-done.10.refs_0_), channel_id=1, source_target_pairs={{0,1},{1,0},{2,3},{3,2},{4,5},{5,4},{6,7},{7,6}} | collective-permute-start | bytes 8601608 | tf_op jit(solution)/shard_map/ppermute | solution.py:615
  1233.1 103.7 %collective-permute-start.21 = (bf16[320,4480]{1,0:T(8,128)(2,1)}, bf16[320,4480]{1,0:T(8,128)(2,1)}, u32[]{:S(2)}, u32[]{:S(2)}) collective-permute-start(bf16[320,4480]{1,0:T(8,128)(2,1)} %collective-permute-done.20.refs_0_), channel_id=1, source_target_pairs={{0,1},{1,0},{2,3},{3,2},{4,5},{5,4},{6,7},{7,6}} | collective-permute-start | bytes 8601608 | tf_op jit(solution)/shard_map/ppermute | solution.py:615
  1259.5 43.1 %collective-permute-start.44 = (bf16[672,1280]{1,0:T(8,128)(2,1)}, bf16[672,1280]{1,0:T(8,128)(2,1)}, u32[]{:S(2)}, u32[]{:S(2)}) collective-permute-start(bf16[672,1280]{1,0:T(8,128)(2,1)} %get-tuple-element.155), channel_id=1, source_target_pairs={{0,1},{1,0},{2,3},{3,2},{4,5},{5,4},{6,7},{7,6}} | collective-permute-start | bytes 5160968 | tf_op jit(solution)/shard_map/ppermute | solution.py:615
  1259.5 81.0 %collective-permute-start.19 = (bf16[320,2688]{1,0:T(8,128)(2,1)}, bf16[320,2688]{1,0:T(8,128)(2,1)}, u32[]{:S(2)}, u32[]{:S(2)}) collective-permute-start(bf16[320,2688]{1,0:T(8,128)(2,1)} %collective-permute-done.18.refs_0_), channel_id=1, source_target_pairs={{0,1},{1,0},{2,3},{3,2},{4,5},{5,4},{6,7},{7,6}} | collective-permute-start | bytes 5160968 | tf_op jit(solution)/shard_map/ppermute | solution.py:615
  1295.9 53.5 %collective-permute-start.42 = (bf16[672,1280]{1,0:T(8,128)(2,1)}, bf16[672,1280]{1,0:T(8,128)(2,1)}, u32[]{:S(2)}, u32[]{:S(2)}) collective-permute-start(bf16[672,1280]{1,0:T(8,128)(2,1)} %collective-permute-done.41.refs_0_), channel_id=1, source_target_pairs={{0,1},{1,0},{2,3},{3,2},{4,5},{5,4},{6,7},{7,6}} | collective-permute-start | bytes 5160968 | tf_op jit(solution)/shard_map/ppermute | solution.py:615
  1302.7 53.7 %collective-permute-start.40 = (bf16[448,1280]{1,0:T(8,128)(2,1)}, bf16[448,1280]{1,0:T(8,128)(2,1)}, u32[]{:S(2)}, u32[]{:S(2)}) collective-permute-start(bf16[448,1280]{1,0:T(8,128)(2,1)} %collective-permute-done.39.refs_0_), channel_id=1, source_target_pairs={{0,1},{1,0},{2,3},{3,2},{4,5},{5,4},{6,7},{7,6}} | collective-permute-start | bytes 3440648 | tf_op jit(solution)/shard_map/ppermute | solution.py:615
  (13 other events, 276.1 us)
